TPU v7x, 16 devices: a whole 2x2x2 slice. The times are simulated.
16 devices in a mesh: tp: 2 (over z), dp: 8 (over y, x, core).
Axes of the slice: x: 2, y: 2, z: 2, core: 2. Of those that a mesh axis runs over, the one named last changes fastest.
Arguments:
- tokens: int32 [128, 512], P('dp')
- cotangent: bfloat16 [128, 512, 768], P('dp')
- emb_table: bfloat16 [30592, 768], P('tp')
- w_qkv: bfloat16 [768, 2304], P(None, 'tp')
- b_qkv: bfloat16 [12, 192], P('tp')
- w_out: bfloat16 [768, 768], P('tp')
- b_out: bfloat16 [768], replicated
- ln1_gain: bfloat16 [768], replicated
- ln1_bias: bfloat16 [768], replicated
- w_gate: bfloat16 [768, 3072], P(None, 'tp')
- b_gate: bfloat16 [3072], P('tp')
- w_lin: bfloat16 [768, 3072], P(None, 'tp')
- b_lin: bfloat16 [3072], P('tp')
- w_down: bfloat16 [3072, 768], P('tp')
- b_down: bfloat16 [768], replicated
- ln2_gain: bfloat16 [768], replicated
Outputs:
- output 1: float32 [30592, 768], P('tp')
- output 2: float32 [768, 2304], P(None, 'tp')
- output 3: float32 [12, 192], P('tp')
- output 4: float32 [768, 768], P('tp')
- output 5: float32 [768], replicated
- output 6: float32 [768], replicated
- output 7: float32 [768], replicated
- output 8: float32 [768, 3072], P(None, 'tp')
- output 9: float32 [3072], P('tp')
- output 10: float32 [768, 3072], P(None, 'tp')
- output 11: float32 [3072], P('tp')
- output 12: float32 [3072, 768], P('tp')
- output 13: float32 [768], replicated
- output 14: float32 [768], replicated
All inputs are finite; a program needn't handle non-finite values.
Results may differ from a plain program's by a relative error of at most 0.0151514.
Values sent between devices are 32-bit elements.
A program may use at most 1 GiB of HBM per device.

v0:
```python
import jax
import jax.numpy as jnp
from jax import lax
from jax.sharding import PartitionSpec as P

ALPHA = 140.0 ** 0.5
EPS = 1e-5
SHRINK = 0.1
ROPE_BASE = 10000.0
WEIGHT_SPECS = (P(None, 'tp'), P('tp', None), P('tp', None), P(), P(), P(), P(None, 'tp'), P('tp'), P(None, 'tp'), P('tp'), P('tp', None), P(), P())


def norm_scaled(values, gain):
    mean_val = jnp.mean(values, axis=-1, keepdims=True)
    centered = values - mean_val
    variance = jnp.mean(centered * centered, axis=-1, keepdims=True)
    return centered * lax.rsqrt(variance + EPS) * gain


def geglu(gate_pre, lin_pre):
    return jax.nn.gelu(gate_pre, approximate=False) * lin_pre


def rope_tables(seq_len, head_dim):
    half_dim = head_dim // 2
    inv_freq = ROPE_BASE ** (-2.0 * jnp.arange(half_dim, dtype=jnp.float32) / head_dim)
    angles = jnp.arange(seq_len, dtype=jnp.float32)[:, None] * inv_freq[None, :]
    return jnp.cos(angles)[:, None, :], jnp.sin(angles)[:, None, :]


def apply_rope(values, cos_tab, sin_tab):
    half_dim = values.shape[-1] // 2
    first_half = values[..., :half_dim]
    second_half = values[..., half_dim:]
    return jnp.concatenate([first_half * cos_tab - second_half * sin_tab, second_half * cos_tab + first_half * sin_tab], axis=-1)


def local_layer(embedded, cotangent, weights):
    (w_qkv, b_qkv, w_out, b_out, ln1_gain, ln1_bias, w_gate, b_gate, w_lin, b_lin, w_down, b_down, ln2_gain) = weights
    batch_loc, seq_len = embedded.shape[0], embedded.shape[1]
    heads_loc = b_qkv.shape[0]
    head_dim = b_qkv.shape[1] // 3
    emb_bf = embedded.astype(jnp.bfloat16)
    qkv_pre = jnp.einsum('bsd,de->bse', emb_bf, w_qkv, preferred_element_type=jnp.float32) + b_qkv.reshape(-1).astype(jnp.float32)
    qkv_all = qkv_pre.astype(jnp.bfloat16).reshape(batch_loc, seq_len, heads_loc, 3, head_dim)
    cos_tab, sin_tab = rope_tables(seq_len, head_dim)
    queries = apply_rope(qkv_all[:, :, :, 0].astype(jnp.float32), cos_tab, sin_tab).astype(jnp.bfloat16)
    keys_rot = apply_rope(qkv_all[:, :, :, 1].astype(jnp.float32), cos_tab, sin_tab).astype(jnp.bfloat16)
    values = qkv_all[:, :, :, 2]
    attn_scale = head_dim ** -0.5
    causal = jnp.arange(seq_len)[:, None] >= jnp.arange(seq_len)[None, :]
    scores = jnp.einsum('bqhd,bkhd->bhqk', queries, keys_rot, preferred_element_type=jnp.float32) * attn_scale
    attn_probs = jax.nn.softmax(jnp.where(causal, scores, -1e30), axis=-1).astype(jnp.bfloat16)
    context = jnp.einsum('bhqk,bkhd->bqhd', attn_probs, values, preferred_element_type=jnp.float32).astype(jnp.bfloat16).reshape(batch_loc, seq_len, heads_loc * head_dim)
    attn_part = jnp.einsum('bse,ed->bsd', context, w_out, preferred_element_type=jnp.float32)
    attn_out = lax.psum(attn_part, 'tp') + b_out.astype(jnp.float32)
    normed_one, norm_one_pull = jax.vjp(norm_scaled, ALPHA * embedded + attn_out, ln1_gain.astype(jnp.float32))
    hidden = (normed_one + ln1_bias.astype(jnp.float32)).astype(jnp.bfloat16)
    gate_pre = jnp.einsum('bsd,df->bsf', hidden, w_gate, preferred_element_type=jnp.float32) + b_gate.astype(jnp.float32)
    lin_pre = jnp.einsum('bsd,df->bsf', hidden, w_lin, preferred_element_type=jnp.float32) + b_lin.astype(jnp.float32)
    inner_val, act_pull = jax.vjp(geglu, gate_pre, lin_pre)
    inner_act = inner_val.astype(jnp.bfloat16)
    ffn_part = jnp.einsum('bsf,fd->bsd', inner_act, w_down, preferred_element_type=jnp.float32)
    ffn_out = lax.psum(ffn_part, 'tp') + b_down.astype(jnp.float32)
    norm_two_pull = jax.vjp(norm_scaled, ALPHA * hidden.astype(jnp.float32) + ffn_out, ln2_gain.astype(jnp.float32))[1]

    d_resid_two, d_ln2_gain = norm_two_pull(cotangent.astype(jnp.float32))
    d_b_down = jnp.sum(d_resid_two, axis=(0, 1))
    d_ffn_bf = d_resid_two.astype(jnp.bfloat16)
    d_w_down = jnp.einsum('bsf,bsd->fd', inner_act, d_ffn_bf, preferred_element_type=jnp.float32)
    d_inner = jnp.einsum('bsd,fd->bsf', d_ffn_bf, w_down, preferred_element_type=jnp.float32).astype(jnp.bfloat16)
    d_gate_pre, d_lin_pre = act_pull(d_inner.astype(jnp.float32))
    d_b_gate = jnp.sum(d_gate_pre, axis=(0, 1))
    d_b_lin = jnp.sum(d_lin_pre, axis=(0, 1))
    d_gate_bf = d_gate_pre.astype(jnp.bfloat16)
    d_lin_bf = d_lin_pre.astype(jnp.bfloat16)
    d_w_gate = jnp.einsum('bsd,bsf->df', hidden, d_gate_bf, preferred_element_type=jnp.float32)
    d_w_lin = jnp.einsum('bsd,bsf->df', hidden, d_lin_bf, preferred_element_type=jnp.float32)
    d_hidden_part = jnp.einsum('bsf,df->bsd', d_gate_bf, w_gate, preferred_element_type=jnp.float32) + jnp.einsum('bsf,df->bsd', d_lin_bf, w_lin, preferred_element_type=jnp.float32)
    d_hidden = ALPHA * d_resid_two + lax.psum(d_hidden_part, 'tp')
    d_ln1_bias = jnp.sum(d_hidden, axis=(0, 1))
    d_resid_one, d_ln1_gain = norm_one_pull(d_hidden)
    d_b_out = jnp.sum(d_resid_one, axis=(0, 1))
    d_attn_bf = d_resid_one.astype(jnp.bfloat16)
    d_w_out = jnp.einsum('bse,bsd->ed', context, d_attn_bf, preferred_element_type=jnp.float32)
    d_context = jnp.einsum('bsd,ed->bse', d_attn_bf, w_out, preferred_element_type=jnp.float32).astype(jnp.bfloat16).reshape(batch_loc, seq_len, heads_loc, head_dim)
    d_probs = jnp.einsum('bqhd,bkhd->bhqk', d_context, values, preferred_element_type=jnp.float32)
    d_values = jnp.einsum('bhqk,bqhd->bkhd', attn_probs, d_context, preferred_element_type=jnp.float32)
    probs_f32 = attn_probs.astype(jnp.float32)
    d_scores = (probs_f32 * (d_probs - jnp.sum(d_probs * probs_f32, axis=-1, keepdims=True)) * attn_scale).astype(jnp.bfloat16)
    d_queries = apply_rope(jnp.einsum('bhqk,bkhd->bqhd', d_scores, keys_rot, preferred_element_type=jnp.float32), cos_tab, -sin_tab)
    d_keys = apply_rope(jnp.einsum('bhqk,bqhd->bkhd', d_scores, queries, preferred_element_type=jnp.float32), cos_tab, -sin_tab)
    d_qkv = jnp.stack([d_queries, d_keys, d_values], axis=3).reshape(batch_loc, seq_len, -1)
    d_b_qkv = jnp.sum(d_qkv, axis=(0, 1)).reshape(heads_loc, 3 * head_dim)
    d_qkv_bf = d_qkv.astype(jnp.bfloat16)
    d_w_qkv = jnp.einsum('bsd,bse->de', emb_bf, d_qkv_bf, preferred_element_type=jnp.float32)
    d_emb_part = jnp.einsum('bse,de->bsd', d_qkv_bf, w_qkv, preferred_element_type=jnp.float32)
    d_embedded = ALPHA * d_resid_one + lax.psum(d_emb_part, 'tp')
    grads = (d_w_qkv, d_b_qkv, d_w_out, d_b_out, d_ln1_gain, d_ln1_bias, d_w_gate, d_b_gate, d_w_lin, d_b_lin, d_w_down, d_b_down, d_ln2_gain)
    return d_embedded, grads


def solution(mesh):
    in_specs = (P('dp', None), P('dp', None, None), P('tp', None)) + WEIGHT_SPECS
    out_specs = (P('tp', None),) + WEIGHT_SPECS

    def device_step(tokens, cotangent, emb_table, *weights):
        vocab_loc = emb_table.shape[0]
        local_ids = tokens - lax.axis_index('tp') * vocab_loc
        in_shard = (local_ids >= 0) & (local_ids < vocab_loc)
        safe_ids = jnp.where(in_shard, local_ids, 0)
        own_rows = jnp.where(in_shard[:, :, None], jnp.take(emb_table, safe_ids, axis=0), 0.0)
        embedded = lax.psum(own_rows.astype(jnp.float32), 'tp')
        d_embedded, grads = local_layer(embedded, cotangent, weights)
        d_rows = jnp.where(in_shard[:, :, None], SHRINK * d_embedded, 0.0)
        d_table = jax.ops.segment_sum(d_rows.reshape(-1, d_rows.shape[-1]), safe_ids.reshape(-1), num_segments=vocab_loc)
        return lax.psum((d_table,) + grads, 'dp')

    return jax.shard_map(device_step, mesh=mesh, in_specs=in_specs, out_specs=out_specs, check_vma=False)
```

profile of v0, /device:TPU:0, one launch (start us, length us, event | category | flops | bytes accessed | tf_op | source)
XLA Modules:
  0.0 4830.2 jit_solution(4765117584802307832)
XLA Ops:
  9.6 47.8 gather_fusion
  71.7 555.4 %all-reduce.9.cloned.1.call-done = f32[16,512,768]{2,1,0:T(8,128)} async-done(((f32[16,512,768]{2,1,0:T(8,128)}), f32[16,512,768]{2,1,0:T(8,128)}) %all-reduce.9.cloned.1.call-update) | async-done | bytes 25165840 | tf_op jit(solution)/shard_map/psum | solution.py:113
  627.2 24.0 add_convert_fusion
  651.2 24.7 copy.74
  696.8 45.2 fusion.100
  742.0 48.3 %divide_convert_fusion = bf16[16,6,512,512]{2,3,1,0:T(8,128)(2,1)} fusion(f32[16,6,512,512]{2,3,1,0:T(8,128)} %get-tuple-element.75, f32[16,6,512]{2,1,0:T(8,128)S(1)} %get-tuple-element.74), kind=kLoop, calls=%fused_computation.8 | loop fusion | flops 50331648 | bytes 151191552 | tf_op jit(solution)/shard_map/convert_element_type | solution.py:53
  828.0 555.2 %all-reduce.11.cloned.1.call-done = f32[16,512,768]{2,1,0:T(8,128)} async-done(((f32[16,512,768]{2,1,0:T(8,128)}), f32[16,512,768]{2,1,0:T(8,128)}) %all-reduce.11.cloned.1.call-update) | async-done | bytes 25165840 | tf_op jit(solution)/shard_map/psum | solution.py:56
  1383.2 25.7 fusion.99
  1431.4 47.1 fusion.26
  1478.6 138.1 %multiply_convert_fusion = (bf16[16,512,1536]{2,1,0:T(8,128)(2,1)}, f32[16,512,1536]{2,1,0:T(8,128)}, f32[16,512,1536]{2,1,0:T(8,128)}, f32[16,512,1536]{2,1,0:T(8,128)}) fusion(f32[1536]{0:T(1024)S(1)} %convert_element_type.130, f32[16,512,1536]{2,1,0:T(8,128)} %get-tuple-element.76, f32[1536]{0:T(1024)S(1)} %convert_element_type.129, ...), kind=kOutput, calls=%fused_computation.23 | convolution fusion | flops 20245905408 | bytes 244592640 | tf_op jit(solution)/shard_map/bsd,df->bsf/dot_general | solution.py:60
  1616.7 26.0 fusion.57
  1643.3 554.7 %all-reduce.13.cloned.1.call-done = f32[16,512,768]{2,1,0:T(8,128)} async-done(((f32[16,512,768]{2,1,0:T(8,128)}), f32[16,512,768]{2,1,0:T(8,128)}) %all-reduce.13.cloned.1.call-update) | async-done | bytes 25165840 | tf_op jit(solution)/shard_map/psum | solution.py:64
  2252.4 89.7 %fusion.94 = (f32[1536]{0:T(1024)}, bf16[16,512,1536]{2,1,0:T(8,128)(2,1)}, f32[1536]{0:T(1024)}, bf16[16,512,1536]{2,1,0:T(8,128)(2,1)}) fusion(f32[16,512,1536]{2,1,0:T(8,128)} %get-tuple-element.46, f32[16,512,1536]{2,1,0:T(8,128)} %get-tuple-element.77, f32[1536]{0:T(1024)S(1)} %convert_element_type.130, f32[16,512,1536]{2,1,0:T(8,128)} %get-tuple-element.76, ...), kind=kOutput, calls=%fused_computation.165 | convolution fusion | flops 19616755712 | bytes 279240704 | tf_op jit(solution)/shard_map/bsd,fd->bsf/dot_general | solution.py:71
  2342.1 26.8 fusion.31
  2368.8 43.1 convolution_add_fusion
  2412.0 555.3 %all-reduce.15.cloned.1.call-done = f32[16,512,768]{2,1,0:T(8,128)} async-done(((f32[16,512,768]{2,1,0:T(8,128)}), f32[16,512,768]{2,1,0:T(8,128)}) %all-reduce.15.cloned.1.call-update) | async-done | bytes 25165840 | tf_op jit(solution)/shard_map/psum | solution.py:80
  2967.3 33.7 multiply_reduce_fusion
  3001.1 26.0 fusion.95
  3039.8 26.0 convolution_bitcast_fusion
  3065.9 38.7 fusion.40
  3104.5 97.5 %fusion.45 = f32[16,512,6,64]{1,3,2,0:T(8,128)} fusion(bf16[16,6,512,512]{2,3,1,0:T(8,128)(2,1)} %divide_convert_fusion, f32[16,6,512,512]{2,3,1,0:T(8,128)} %fusion.40, bf16[16,512,6,32]{1,3,2,0:T(8,128)(2,1)} %get-tuple-element.65, bf16[16,512,6,32]{1,3,2,0:T(8,128)(2,1)} %get-tuple-element.66), kind=kOutput, calls=%fused_computation.106 | convolution fusion | flops 3410018816 | bytes 169869312 | tf_op jit(solution)/shard_map/bhqk,bkhd->bqhd/dot_general | solution.py:91
  3202.1 96.8 %fusion.46 = f32[16,512,6,64]{1,3,2,0:T(8,128)} fusion(bf16[16,6,512,512]{2,3,1,0:T(8,128)(2,1)} %divide_convert_fusion, f32[16,6,512,512]{2,3,1,0:T(8,128)} %fusion.40, bf16[16,512,6,32]{1,3,2,0:T(8,128)(2,1)} %get-tuple-element.60, bf16[16,512,6,32]{1,3,2,0:T(8,128)(2,1)} %get-tuple-element.59), kind=kOutput, calls=%fused_computation.107 | convolution fusion | flops 3410018816 | bytes 169869312 | tf_op jit(solution)/shard_map/bhqk,bqhd->bkhd/dot_general | solution.py:92
  3354.7 25.5 fusion.66
  3380.9 26.6 fusion.47
  3407.5 28.0 fusion.50
  3435.5 34.1 convolution_bitcast_fusion.1
  3509.2 426.4 %all-reduce.17.cloned.1.call-done = f32[16,512,768]{2,1,0:T(8,128)} async-done(((f32[16,512,768]{2,1,0:T(8,128)}), f32[16,512,768]{2,1,0:T(8,128)}) %all-reduce.17.cloned.1.call-update) | async-done | bytes 25165840 | tf_op jit(solution)/shard_map/psum | solution.py:98
  3935.5 24.9 add_reduce_fusion
  3960.4 72.7 %scatter_custom_fusion = f32[15296,768]{1,0:T(8,128)} fusion(s32[8192]{0:T(1024)S(1)} %bitcast.123, f32[8192,768]{1,0:T(8,128)} %bitcast.117, f32[]{:T(128)} %constant.48.clone.1), kind=kCustom, calls=%fused_computation.67 | custom fusion | flops 6291456 | bytes 46989824 | tf_op jit(solution)/shard_map/scatter-add | solution.py:116
  4045.9 26.1 all-reduce
  4072.0 701.1 %all-reduce.19.cloned.1.call-done = (f32[15296,768]{1,0:T(8,128)}, f32[768,1152]{1,0:T(8,128)}, f32[384,768]{1,0:T(8,128)}, f32[768,1536]{1,0:T(8,128)}, f32[768,1536]{1,0:T(8,128)}, /*index=5*/f32[1536,768]{1,0:T(8,128)}) async-done(((f32[15296,768]{1,0:T(8,128)}, f32[768,1152]{1,0:T(8,128)}, f32[384,768]{1,0:T(8,128)}, f32[768,1536]{1,0:T(8,128)}, f32[768,1536]{1,0:T(8,128)}, ...) | async-done | bytes 65863696 | tf_op jit(solution)/shard_map/psum | solution.py:117
  4773.1 32.7 copy.118
  (155 shorter events, 291.3 us)
Async XLA Ops:
  7.2 1471.4 %copy-start = (bf16[768,1536]{1,0:T(8,128)(2,1)S(1)}, bf16[768,1536]{1,0:T(8,128)(2,1)}, u32[]{:S(2)}) copy-start(bf16[768,1536]{1,0:T(8,128)(2,1)} %param.27) | copy-start | bytes 7077892
  7.2 620.0 %all-reduce.9.cloned.1.call-start = ((), (), s32[]{:S(2)}) async-start(), calls=%async_computation | async-start | bytes 50331648 | tf_op jit(solution)/shard_map/psum | solution.py:113
  8.2 49.2 %copy-start.24 = (pred[16,512]{1,0:T(8,128)(4,1)}, pred[16,512]{1,0:T(8,128)(4,1)S(1)}, u32[]{:S(2)}) copy-start(pred[16,512]{1,0:T(8,128)(4,1)S(1)} %get-tuple-element.67) | copy-start | bytes 24580
  70.3 1312.8 %all-reduce.11.cloned.1.call-start = ((), (), s32[]{:S(2)}) async-start(), calls=%async_computation.1 | async-start | bytes 50331648 | tf_op jit(solution)/shard_map/psum | solution.py:56
  71.7 615.3 %copy-start.9 = (f32[512,32]{0,1:T(8,128)}, f32[512,32]{0,1:T(8,128)S(1)}, u32[]{:S(2)}) copy-start(f32[512,32]{0,1:T(8,128)S(1)} %get-tuple-element.73) | copy-start | bytes 196612
  790.3 23.1 copy-start.11
  813.4 14.6 copy-start.36
  827.8 1370.2 %all-reduce.13.cloned.1.call-start = ((), (), s32[]{:S(2)}) async-start(), calls=%async_computation.2 | async-start | bytes 50331648 | tf_op jit(solution)/shard_map/psum | solution.py:64
  827.9 593.9 %copy-start.21 = (f32[768]{0:T(1024)}, f32[768]{0:T(1024)S(1)}, u32[]{:S(2)}) copy-start(f32[768]{0:T(1024)S(1)} %convert_element_type.125) | copy-start | bytes 9220
  828.0 593.9 %copy-start.26 = (f32[768]{0:T(1024)}, f32[768]{0:T(1024)S(1)}, u32[]{:S(2)}) copy-start(f32[768]{0:T(1024)S(1)} %convert_element_type.126) | copy-start | bytes 9220
  1408.9 15.5 copy-start.1
  1478.6 138.1 %copy-start.42 = (bf16[1536,768]{1,0:T(8,128)(2,1)S(1)}, bf16[1536,768]{1,0:T(8,128)(2,1)}, u32[]{:S(2)}) copy-start(bf16[1536,768]{1,0:T(8,128)(2,1)} %param.29) | copy-start | bytes 7077892
  1642.6 555.4 %copy-start.4 = (f32[16,512]{1,0:T(8,128)S(1)}, f32[16,512]{1,0:T(8,128)}, u32[]{:S(2)}) copy-start(f32[16,512]{1,0:T(8,128)} %copy-done.3) | copy-start | bytes 98308
  1642.6 555.4 %copy-start.7 = (f32[16,512]{1,0:T(8,128)S(1)}, f32[16,512]{1,0:T(8,128)}, u32[]{:S(2)}) copy-start(f32[16,512]{1,0:T(8,128)} %copy-done.6) | copy-start | bytes 98308
  1642.6 555.4 %copy-start.22 = (f32[768]{0:T(1024)S(1)}, f32[768]{0:T(1024)}, u32[]{:S(2)}) copy-start(f32[768]{0:T(1024)} %copy-done.21) | copy-start | bytes 9220
  1642.7 555.4 %copy-start.27 = (f32[768]{0:T(1024)S(1)}, f32[768]{0:T(1024)}, u32[]{:S(2)}) copy-start(f32[768]{0:T(1024)} %copy-done.26) | copy-start | bytes 9220
  1642.7 1324.6 %all-reduce.15.cloned.1.call-start = ((), (), s32[]{:S(2)}) async-start(), calls=%async_computation.3 | async-start | bytes 50331648 | tf_op jit(solution)/shard_map/psum | solution.py:80
  2252.3 715.0 %copy-start.16 = (f32[16,512]{1,0:T(8,128)}, f32[16,512]{1,0:T(8,128)S(1)}, u32[]{:S(2)}) copy-start(f32[16,512]{1,0:T(8,128)S(1)} %negate_multiply_fusion.2) | copy-start | bytes 98308
  2411.9 555.4 %copy-start.5 = (f32[16,512]{1,0:T(8,128)S(1)}, f32[16,512]{1,0:T(8,128)}, u32[]{:S(2)}) copy-start(f32[16,512]{1,0:T(8,128)} %copy-done.3) | copy-start | bytes 98308
  2411.9 555.4 %copy-start.8 = (f32[16,512]{1,0:T(8,128)S(1)}, f32[16,512]{1,0:T(8,128)}, u32[]{:S(2)}) copy-start(f32[16,512]{1,0:T(8,128)} %copy-done.6) | copy-start | bytes 98308
  2411.9 555.4 %copy-start.23 = (f32[768]{0:T(1024)S(1)}, f32[768]{0:T(1024)}, u32[]{:S(2)}) copy-start(f32[768]{0:T(1024)} %copy-done.21) | copy-start | bytes 9220
  2412.0 589.1 %copy-start.14 = (f32[16,512]{1,0:T(8,128)S(1)}, f32[16,512]{1,0:T(8,128)}, u32[]{:S(2)}) copy-start(f32[16,512]{1,0:T(8,128)} %copy-done.13) | copy-start | bytes 98308
  2412.0 1523.6 %all-reduce.17.cloned.1.call-start = ((), (), s32[]{:S(2)}) async-start(), calls=%async_computation.4 | async-start | bytes 50331648 | tf_op jit(solution)/shard_map/psum | solution.py:98
  3001.1 26.0 copy-start.12
  3202.1 96.8 %copy-start.10 = (f32[512,32]{0,1:T(8,128)S(1)}, f32[512,32]{0,1:T(8,128)}, u32[]{:S(2)}) copy-start(f32[512,32]{0,1:T(8,128)} %copy-done.9) | copy-start | bytes 196612
  3202.1 96.8 %copy-start.15 = (f32[512,32]{0,1:T(8,128)S(1)}, f32[512,32]{0,1:T(8,128)}, u32[]{:S(2)}) copy-start(f32[512,32]{0,1:T(8,128)} %get-tuple-element.71) | copy-start | bytes 196612
  3380.2 1392.9 %all-reduce.19.cloned.1.call-start = ((), (), s32[]{:S(2)}) async-start(), calls=%async_computation.5 | async-start | bytes 131727360 | tf_op jit(solution)/shard_map/psum | solution.py:117
  3380.9 26.6 copy-start.17
  3435.5 34.1 copy-start.19
  3485.7 449.8 %copy-start.25 = (pred[16,512]{1,0:T(8,128)(4,1)S(1)}, pred[16,512]{1,0:T(8,128)(4,1)}, u32[]{:S(2)}) copy-start(pred[16,512]{1,0:T(8,128)(4,1)} %copy-done.24) | copy-start | bytes 24580
  4773.1 36.9 copy-start.2
  4805.8 14.9 slice-start
  (20 other events, 193.7 us)
Sparse Core Ops, SparseCore 0:
  70.5 556.6 all-reduce.8
  828.0 555.1 all-reduce.10
  1642.8 555.2 all-reduce.12
  2412.1 555.1 all-reduce.14
  3380.3 555.1 all-reduce.16
  4033.2 739.8 all-reduce.18
where the time goes:
time: 4840 us; the launch traced here: 4830 us
  waiting for transfers between devices  3350 us (69%)
  matrix products  903 us (19%)
  other arithmetic  404 us (8%)
  local copies, waits for them, and re-layouts  134 us (3%)
    psum x1, waiting for transfers between devices, device_step(): return lax.psum((d_table,) + grads, 'dp')  701 us
    psum x1, waiting for transfers between devices, device_step(): embedded = lax.psum(own_rows.astype(jnp.float32), 'tp')  555 us
    psum x1, waiting for transfers between devices, local_layer(): d_hidden = ALPHA * d_resid_two + lax.psum(d_hidden_part, 'tp')  555 us
    psum x1, waiting for transfers between devices, local_layer(): attn_out = lax.psum(attn_part, 'tp') + b_out.astype(jnp.float32)  555 us
    psum x1, waiting for transfers between devices, local_layer(): ffn_out = lax.psum(ffn_part, 'tp') + b_down.astype(jnp.float32)  555 us
    psum x1, waiting for transfers between devices, local_layer(): d_embedded = ALPHA * d_resid_one + lax.psum(d_emb_part, 'tp')  426 us
    dot_general x1, matrix products, local_layer(): jnp.einsum('bsd,df->bsf', hidden, w_lin, preferred_element_type=jnp.float32)  138 us
    dot_general x1, matrix products, local_layer(): jnp.einsum('bhqk,bkhd->bqhd', d_scores, keys_rot, preferred_element_type=...  97.5 us
  transfers between devices with their start and end apart: 6, of which 6 were waited for; matrix products, arithmetic and copies ran while one was open for 3% of the time, Pallas kernels for 0%

commit v1 on v0

v1 whole, which is shorter than its diff:
```python
import functools

import jax
import jax.numpy as jnp
from jax import lax
from jax.experimental import pallas as pl
from jax.experimental.pallas import tpu as pltpu
from jax.sharding import PartitionSpec as P

ALPHA = 140.0 ** 0.5
EPS = 1e-5
SHRINK = 0.1
ROPE_BASE = 10000.0
WEIGHT_SPECS = (P(None, 'tp'), P('tp', None), P('tp', None), P(), P(), P(), P(None, 'tp'), P('tp'), P(None, 'tp'), P('tp'), P('tp', None), P(), P())

F32 = jnp.float32
BF16 = jnp.bfloat16
LANES = 128
HALF_Q = 256
CHUNK = 512
VMEM_LIMIT = 66 * 1024 * 1024 - 512 * 1024
LOG2E = 1.4426950408889634
MASKED = -8e30
NT = (((1,), (1,)), ((), ()))
NN = (((1,), (0,)), ((), ()))
SWAP = ((0, 1), (1, 0))


def dot_nn(left, right):
    return lax.dot_general(left, right, NN, preferred_element_type=F32)


def dot_nt(left, right):
    return lax.dot_general(left, right, NT, preferred_element_type=F32)


def row_sums(values):
    return jnp.sum(values.reshape(values.shape[0] // 8, 8, values.shape[1]), axis=0)


def rope(values, cos_tab, sin_tab, first_half):
    partner = jnp.where(first_half, pltpu.roll(values, 96, 1), pltpu.roll(values, 32, 1))
    return values * cos_tab + partner * sin_tab


def lane_masks():
    lane = lax.broadcasted_iota(jnp.int32, (1, LANES), 1)
    low = lane < 64
    return low, low.astype(F32).astype(BF16), (1.0 - low.astype(F32)).astype(BF16), (lane % 64) < 32


def attn_forward_kernel(head_dim, alias_count, *refs):
    (emb_ref, wqkv_ref, bqkv_ref, wo_ref, bo_ref, gain_ref, bias_ref, cos_ref, sin_ref) = refs[:9]
    (qkv_ref, prob_ref, ctx_ref, hat_ref, rstd_ref, hid_ref) = refs[9 + alias_count:]
    seq_len, width = emb_ref.shape[1], emb_ref.shape[2]
    low, mask_low, mask_high, first_half = lane_masks()
    score_scale = head_dim ** -0.5 * LOG2E
    causal = lax.broadcasted_iota(jnp.int32, (HALF_Q, HALF_Q), 0) <= lax.broadcasted_iota(jnp.int32, (HALF_Q, HALF_Q), 1)
    step = 4 * 3 * head_dim

    def quad(index, carry):
        col = pl.multiple_of(index * step, step)
        pre = dot_nn(emb_ref[0], wqkv_ref[:, pl.ds(col, step)]) + bqkv_ref[:, pl.ds(col, step)]
        pre = pre.astype(BF16).astype(F32)
        for half in range(2):
            parts = [pre[:, (half * 3 + part) * LANES:(half * 3 + part + 1) * LANES] for part in range(3)]
            pair = index * 2 + half
            pair_col = pl.multiple_of(pair * LANES, LANES)
            q_pair = jnp.where(low, parts[0], parts[1])
            k_pair = pltpu.roll(jnp.where(low, parts[2], parts[0]), 64, 1)
            v_pair = jnp.where(low, parts[1], parts[2])
            q_rot = rope(q_pair, cos_ref[...], sin_ref[...], first_half).astype(BF16)
            k_rot = rope(k_pair, cos_ref[...], sin_ref[...], first_half).astype(BF16)
            qkv_ref[0, :, pl.ds(pair_col, LANES)] = q_rot
            qkv_ref[0, :, pl.ds(width + pair_col, LANES)] = k_rot
            qkv_ref[0, :, pl.ds(2 * width + pair_col, LANES)] = v_pair.astype(BF16)
            v_trans = v_pair.T.astype(BF16)
            ctx_rows = []
            for head in range(2):
                k_one = k_rot * (mask_low if head == 0 else mask_high)
                v_one = v_trans[head * 64:(head + 1) * 64]
                blocks = []
                for block in range(2):
                    q_block = q_rot[block * HALF_Q:(block + 1) * HALF_Q]
                    diag = jnp.where(causal, dot_nt(k_one[block * HALF_Q:(block + 1) * HALF_Q], q_block), MASKED)
                    pieces = [diag] if block == 0 else [dot_nt(k_one[:HALF_Q], q_block), diag]
                    peak = functools.reduce(jnp.maximum, [jnp.max(piece, axis=0, keepdims=True) for piece in pieces])
                    exps = [jnp.exp2((piece - peak) * score_scale) for piece in pieces]
                    total = functools.reduce(jnp.add, [jnp.sum(piece, axis=0, keepdims=True) for piece in exps])
                    inverse = 1.0 / total
                    ctx = None
                    for num, piece in enumerate(exps):
                        prob = (piece * inverse).astype(BF16)
                        prob_ref[0, pair * 2 + head, (block + num) * HALF_Q:(block + num + 1) * HALF_Q, :] = prob
                        term = dot_nn(v_one[:, num * HALF_Q:(num + 1) * HALF_Q], prob)
                        ctx = term if ctx is None else ctx + term
                    blocks.append(ctx)
                ctx_rows.append(jnp.concatenate(blocks, axis=1))
            ctx_pair = jnp.concatenate(ctx_rows, axis=0)
            ctx_ref[0, :, pl.ds(pair_col, LANES)] = ctx_pair.T.astype(BF16)
        return carry

    lax.fori_loop(0, wqkv_ref.shape[1] // step, quad, 0)
    attn = dot_nn(ctx_ref[0], wo_ref[...]) + bo_ref[...]
    resid = ALPHA * emb_ref[0].astype(F32) + attn
    centered = resid - jnp.mean(resid, axis=-1, keepdims=True)
    variance = jnp.mean(centered * centered, axis=-1, keepdims=True)
    rstd = lax.rsqrt(variance + EPS)
    hat = centered * rstd
    hat_ref[0] = hat
    rstd_ref[0] = jnp.broadcast_to(rstd, (seq_len, LANES))
    hid_ref[0] = (hat * gain_ref[...] + bias_ref[...]).astype(BF16)


def ffn_kernel(hid_ref, cot_ref, hat_ref, rstd_ref, wg_ref, wl_ref, wd_ref, bg_ref, bl_ref, bd_ref, gain1_ref, gain2_ref,
               inner_out, gate_out, lin_out, dffn_ref, dres_ref, narrow_ref, wide_ref,
               act_buf, slope_buf, inner_buf, gate_buf, lin_buf, acc_buf, sems):
    step = pl.program_id(0)
    last = pl.num_programs(0) - 1
    rows, width = hid_ref.shape[1], hid_ref.shape[2]
    chunks = wg_ref.shape[1] // CHUNK

    def copy_out(buf, out, kind, chunk, block):
        cols = pl.ds(pl.multiple_of(chunk * CHUNK, CHUNK), CHUNK)
        return pltpu.make_async_copy(buf.at[:, cols], out.at[pl.ds(block * rows, rows), cols], sems.at[kind, chunk])

    @pl.when(step == 0)
    def _():
        narrow_ref[...] = jnp.zeros_like(narrow_ref)
        wide_ref[...] = jnp.zeros_like(wide_ref)

    acc_buf[...] = jnp.zeros_like(acc_buf)

    def forward(chunk, carry):
        cols = pl.ds(pl.multiple_of(chunk * CHUNK, CHUNK), CHUNK)
        gate_pre = dot_nn(hid_ref[0], wg_ref[:, cols]) + bg_ref[:, cols]
        lin_pre = dot_nn(hid_ref[0], wl_ref[:, cols]) + bl_ref[:, cols]
        cdf = 0.5 + 0.5 * lax.erf(gate_pre * (0.5 ** 0.5))
        act = gate_pre * cdf
        pdf = jnp.exp2(gate_pre * gate_pre * (-0.5 * LOG2E)) * 0.3989422804014327
        act_buf[:, cols] = act
        slope_buf[:, cols] = lin_pre * (cdf + gate_pre * pdf)

        @pl.when(step > 0)
        def _():
            copy_out(inner_buf, inner_out, 0, chunk, step - 1).wait()

        inner = (act * lin_pre).astype(BF16)
        inner_buf[:, cols] = inner
        acc_buf[...] += dot_nn(inner, wd_ref[cols, :])
        copy_out(inner_buf, inner_out, 0, chunk, step).start()
        return carry

    lax.fori_loop(0, chunks, forward, 0)
    resid = ALPHA * hid_ref[0].astype(F32) + (acc_buf[...] + bd_ref[...])
    centered = resid - jnp.mean(resid, axis=-1, keepdims=True)
    variance = jnp.mean(centered * centered, axis=-1, keepdims=True)
    rstd = lax.rsqrt(variance + EPS)
    hat = centered * rstd
    cot = cot_ref[0].astype(F32)
    narrow_ref[0:8] += row_sums(cot * hat)
    d_hat = cot * gain2_ref[...]
    d_resid = rstd * (d_hat - jnp.mean(d_hat, axis=-1, keepdims=True) - hat * jnp.mean(d_hat * hat, axis=-1, keepdims=True))
    narrow_ref[8:16] += row_sums(d_resid)
    dffn_ref[0] = d_resid.astype(BF16)
    acc_buf[...] = ALPHA * d_resid

    def backward(chunk, carry):
        cols = pl.ds(pl.multiple_of(chunk * CHUNK, CHUNK), CHUNK)
        d_inner = dot_nt(dffn_ref[0], wd_ref[cols, :]).astype(BF16).astype(F32)
        d_gate = d_inner * slope_buf[:, cols]
        d_lin = d_inner * act_buf[:, cols]
        wide_ref[0:8, cols] += row_sums(d_gate)
        wide_ref[8:16, cols] += row_sums(d_lin)

        @pl.when(step > 0)
        def _():
            copy_out(gate_buf, gate_out, 1, chunk, step - 1).wait()
            copy_out(lin_buf, lin_out, 2, chunk, step - 1).wait()

        d_gate = d_gate.astype(BF16)
        d_lin = d_lin.astype(BF16)
        gate_buf[:, cols] = d_gate
        lin_buf[:, cols] = d_lin
        acc_buf[...] += dot_nt(d_gate, wg_ref[:, cols]) + dot_nt(d_lin, wl_ref[:, cols])
        copy_out(gate_buf, gate_out, 1, chunk, step).start()
        copy_out(lin_buf, lin_out, 2, chunk, step).start()
        return carry

    lax.fori_loop(0, chunks, backward, 0)
    d_hid = acc_buf[...]
    hat = hat_ref[0]
    narrow_ref[16:24] += row_sums(d_hid)
    narrow_ref[24:32] += row_sums(d_hid * hat)
    d_hat = d_hid * gain1_ref[...]
    d_resid = rstd_ref[0][:, :1] * (d_hat - jnp.mean(d_hat, axis=-1, keepdims=True) - hat * jnp.mean(d_hat * hat, axis=-1, keepdims=True))
    narrow_ref[32:40] += row_sums(d_resid)
    dres_ref[0] = d_resid

    @pl.when(step == last)
    def _():
        def drain(chunk, carry):
            copy_out(inner_buf, inner_out, 0, chunk, step).wait()
            copy_out(gate_buf, gate_out, 1, chunk, step).wait()
            copy_out(lin_buf, lin_out, 2, chunk, step).wait()
            return carry

        lax.fori_loop(0, chunks, drain, 0)


def attn_backward_kernel(head_dim, alias_count, *refs):
    (dres_ref, qkv_ref, prob_ref, wqkv_ref, wo_ref, cos_ref, sin_ref) = refs[:7]
    (demb_ref, dqkv_ref, acc_ref) = refs[7 + alias_count:]
    width = dres_ref.shape[2]
    low, mask_low, mask_high, first_half = lane_masks()
    attn_scale = head_dim ** -0.5
    step = 4 * 3 * head_dim

    @pl.when(pl.program_id(0) == 0)
    def _():
        acc_ref[...] = jnp.zeros_like(acc_ref)

    d_attn = dres_ref[0].astype(BF16)

    def quad(index, carry):
        col = pl.multiple_of(index * step, step)
        ctx_row = pl.multiple_of(index * 4 * head_dim, 4 * head_dim)
        d_ctx_quad = dot_nt(d_attn, wo_ref[pl.ds(ctx_row, 4 * head_dim), :]).astype(BF16)
        pieces = []
        for half in range(2):
            pair = index * 2 + half
            pair_col = pl.multiple_of(pair * LANES, LANES)
            d_ctx = d_ctx_quad[:, half * LANES:(half + 1) * LANES]
            q_rot = qkv_ref[0, :, pl.ds(pair_col, LANES)]
            k_rot = qkv_ref[0, :, pl.ds(width + pair_col, LANES)]
            v_pair = qkv_ref[0, :, pl.ds(2 * width + pair_col, LANES)]
            k_trans = k_rot.astype(F32).T.astype(BF16)
            dq_rows, dk_heads, dv_heads = [], [], []
            for head in range(2):
                v_one = v_pair * (mask_low if head == 0 else mask_high)
                k_one = k_trans[head * 64:(head + 1) * 64]
                d_v, d_k, d_q = [None, None], [None, None], []
                for block in range(2):
                    rows = slice(block * HALF_Q, (block + 1) * HALF_Q)
                    keys = range(block + 1)
                    probs = [prob_ref[0, pair * 2 + head, (block + num) * HALF_Q:(block + num + 1) * HALF_Q, :] for num in keys]
                    d_probs = [dot_nt(v_one[num * HALF_Q:(num + 1) * HALF_Q], d_ctx[rows]) for num in keys]
                    wide = [prob.astype(F32) for prob in probs]
                    inner = functools.reduce(jnp.add, [jnp.sum(d_prob * prob, axis=0, keepdims=True) for d_prob, prob in zip(d_probs, wide)])
                    d_q_block = None
                    for num in keys:
                        d_score = (wide[num] * (d_probs[num] - inner) * attn_scale).astype(BF16)
                        terms = (dot_nn(probs[num], d_ctx[rows]), dot_nn(d_score, q_rot[rows]), dot_nn(k_one[:, num * HALF_Q:(num + 1) * HALF_Q], d_score))
                        d_v[num] = terms[0] if d_v[num] is None else d_v[num] + terms[0]
                        d_k[num] = terms[1] if d_k[num] is None else d_k[num] + terms[1]
                        d_q_block = terms[2] if d_q_block is None else d_q_block + terms[2]
                    d_q.append(d_q_block)
                dq_rows.append(jnp.concatenate(d_q, axis=1))
                dk_heads.append(jnp.concatenate(d_k, axis=0))
                dv_heads.append(jnp.concatenate(d_v, axis=0))
            d_q = rope(jnp.concatenate(dq_rows, axis=0).T, cos_ref[...], -sin_ref[...], first_half)
            d_k = rope(jnp.where(low, dk_heads[0], dk_heads[1]), cos_ref[...], -sin_ref[...], first_half)
            d_v = jnp.where(low, dv_heads[0], dv_heads[1])
            d_k = pltpu.roll(d_k, 64, 1)
            pieces += [jnp.where(low, d_q, d_k), jnp.where(low, d_v, d_q), jnp.where(low, d_k, d_v)]
        for num, piece in enumerate(pieces):
            lanes = pl.ds(col + num * LANES, LANES)
            acc_ref[:, lanes] += row_sums(piece)
            dqkv_ref[0, :, lanes] = piece.astype(BF16)
        return carry

    lax.fori_loop(0, wqkv_ref.shape[1] // step, quad, 0)
    demb_ref[0] = SHRINK * (ALPHA * dres_ref[0] + dot_nt(dqkv_ref[0], wqkv_ref[...]))


def whole(shape):
    return pl.BlockSpec(shape, lambda i: (0,) * len(shape), pipeline_mode=pl.Buffered(1))


def per_seq(shape, base=0):
    return pl.BlockSpec((1,) + tuple(shape), lambda i: (i + base,) + (0,) * len(shape))


def params():
    return pltpu.CompilerParams(dimension_semantics=('arbitrary',), vmem_limit_bytes=VMEM_LIMIT)


def attn_forward(base, total, emb, weights, tables, previous, head_dim):
    count, seq_len, width = emb.shape
    wqkv = weights[0]
    heads = width // head_dim
    shapes = [((seq_len, 3 * width), BF16), ((heads, seq_len * 3 // 2, HALF_Q), BF16), ((seq_len, width), BF16),
              ((seq_len, width), F32), ((seq_len, LANES), F32), ((seq_len, width), BF16)]
    operands = (emb,) + tuple(weights) + tuple(tables)
    specs = [per_seq((seq_len, width))] + [whole(item.shape) for item in operands[1:]]
    extra = tuple(previous) if previous is not None else ()
    specs += [pl.BlockSpec(memory_space=pl.ANY)] * len(extra)
    flops = count * (2 * seq_len * width * (wqkv.shape[1] + width) + 4 * heads * seq_len * seq_len * 64)
    return pl.pallas_call(
        functools.partial(attn_forward_kernel, head_dim, len(extra)),
        grid=(count,),
        in_specs=specs,
        out_specs=[per_seq(shape, base) for shape, _ in shapes],
        out_shape=[jax.ShapeDtypeStruct((total,) + shape, dtype) for shape, dtype in shapes],
        input_output_aliases={len(operands) + num: num for num in range(len(extra))},
        compiler_params=params(),
        cost_estimate=pl.CostEstimate(flops=2 * flops, bytes_accessed=count * 12_000_000, transcendentals=0),
        name='attn_forward',
    )(*operands, *extra)


def ffn(hidden, cotangent, hat, rstd, weights):
    count, seq_len, width = hidden.shape
    wide = weights[0].shape[1]
    rows = count * seq_len
    operands = (hidden, cotangent, hat, rstd) + tuple(weights)
    specs = [per_seq(item.shape[1:]) for item in operands[:4]] + [whole(item.shape) for item in operands[4:]]
    anywhere = pl.BlockSpec(memory_space=pl.ANY)
    big = jax.ShapeDtypeStruct((rows, wide), BF16)
    flops = 12 * rows * width * wide
    return pl.pallas_call(
        ffn_kernel,
        grid=(count,),
        in_specs=specs,
        out_specs=[anywhere] * 3 + [per_seq((seq_len, width))] * 2 + [pl.BlockSpec((40, width), lambda i: (0, 0)), pl.BlockSpec((16, wide), lambda i: (0, 0))],
        out_shape=[big] * 3 + [jax.ShapeDtypeStruct((count, seq_len, width), BF16), jax.ShapeDtypeStruct((count, seq_len, width), F32),
                               jax.ShapeDtypeStruct((40, width), F32), jax.ShapeDtypeStruct((16, wide), F32)],
        scratch_shapes=[pltpu.VMEM((seq_len, wide), F32)] * 2 + [pltpu.VMEM((seq_len, wide), BF16)] * 3
        + [pltpu.VMEM((seq_len, width), F32), pltpu.SemaphoreType.DMA((3, wide // CHUNK))],
        compiler_params=params(),
        cost_estimate=pl.CostEstimate(flops=int(1.5 * flops), bytes_accessed=count * 14_000_000, transcendentals=0),
        name='ffn',
    )(*operands)


def attn_backward(base, count, total, d_resid, qkv, probs, weights, tables, previous, head_dim):
    seq_len, width = d_resid.shape[1:]
    wqkv, wout = weights
    heads = width // head_dim
    operands = (d_resid, qkv, probs, wqkv, wout) + tuple(tables)
    specs = [per_seq(item.shape[1:], base) for item in operands[:3]] + [whole(item.shape) for item in operands[3:]]
    extra = (previous,) if previous is not None else ()
    specs += [pl.BlockSpec(memory_space=pl.ANY)] * len(extra)
    flops = count * (2 * seq_len * width * (wqkv.shape[1] + width) + 8 * heads * seq_len * seq_len * 64)
    return pl.pallas_call(
        functools.partial(attn_backward_kernel, head_dim, len(extra)),
        grid=(count,),
        in_specs=specs,
        out_specs=[per_seq((seq_len, width)), per_seq((seq_len, wqkv.shape[1]), base), pl.BlockSpec((8, wqkv.shape[1]), lambda i: (0, 0))],
        out_shape=[jax.ShapeDtypeStruct((count, seq_len, width), F32), jax.ShapeDtypeStruct((total, seq_len, wqkv.shape[1]), BF16),
                   jax.ShapeDtypeStruct((8, wqkv.shape[1]), F32)],
        input_output_aliases={len(operands): 1} if extra else {},
        compiler_params=params(),
        cost_estimate=pl.CostEstimate(flops=2 * flops, bytes_accessed=count * 12_000_000, transcendentals=0),
        name='attn_backward',
    )(*operands, *extra)


def groups_of(total, size):
    return [(base, min(size, total - base)) for base in range(0, total, size)]


def join_kernel(axis, blocks, own_ref, peer_ref, out_ref):
    if axis == 1:
        split = own_ref.shape[1]
        out_ref[:, :split] = own_ref[...]
        out_ref[:, split:] = peer_ref[...].astype(BF16)
    else:
        @pl.when(pl.program_id(0) < blocks)
        def _():
            out_ref[...] = own_ref[...]

        @pl.when(pl.program_id(0) >= blocks)
        def _():
            out_ref[...] = peer_ref[...].astype(BF16)


def with_peer_half(own, axis, index, parts):
    rows = own.shape[0] // parts
    piece = lax.dynamic_slice_in_dim(own, index * rows, rows, 0).astype(F32)
    piece = lax.ppermute(piece, 'tp', SWAP)
    peer = lax.all_gather(piece, 'dp', axis=0, tiled=True)
    blocks = 4
    shape = (own.shape[0] // blocks, own.shape[1])
    if axis == 1:
        grid, out_block, out_shape = (blocks,), (shape[0], 2 * shape[1]), (own.shape[0], 2 * own.shape[1])
        own_map = peer_map = lambda i: (i, 0)
    else:
        grid, out_block, out_shape = (2 * blocks,), shape, (2 * own.shape[0], own.shape[1])
        own_map, peer_map = (lambda i: (jnp.minimum(i, blocks - 1), 0)), (lambda i: (jnp.maximum(i - blocks, 0), 0))
    return pl.pallas_call(
        functools.partial(join_kernel, axis, blocks),
        grid=grid,
        in_specs=[pl.BlockSpec(shape, own_map), pl.BlockSpec(shape, peer_map)],
        out_specs=pl.BlockSpec(out_block, lambda i: (i, 0)),
        out_shape=jax.ShapeDtypeStruct(out_shape, BF16),
        compiler_params=params(),
        cost_estimate=pl.CostEstimate(flops=own.size * 64, bytes_accessed=own.size * 10, transcendentals=0),
        name='join_weight',
    )(own, peer)


def reduce_weight(grad, parts):
    piece = lax.psum_scatter(grad, 'dp', scatter_dimension=1, tiled=True)
    mine = piece[0] + lax.ppermute(piece[1], 'tp', SWAP)
    return lax.all_gather(mine, 'dp', axis=0, tiled=True)


def solution(mesh):
    in_specs = (P('dp', None), P('dp', None, None), P('tp', None)) + WEIGHT_SPECS
    out_specs = (P('tp', None),) + WEIGHT_SPECS
    parts = mesh.shape['dp']

    def device_step(tokens, cotangent, emb_table, *weights):
        (w_qkv, b_qkv, w_out, b_out, ln1_gain, ln1_bias, w_gate, b_gate, w_lin, b_lin, w_down, b_down, ln2_gain) = weights
        tp_index, dp_index = lax.axis_index('tp'), lax.axis_index('dp')
        vocab_loc, width = emb_table.shape
        head_dim = b_qkv.shape[1] // 3
        seq_len = tokens.shape[1]
        total = tokens.shape[0] // 2

        local_ids = tokens - tp_index * vocab_loc
        in_shard = (local_ids >= 0) & (local_ids < vocab_loc)
        own_ids = lax.dynamic_slice_in_dim(local_ids, tp_index * total, total, 0)
        own_in = lax.dynamic_slice_in_dim(in_shard, tp_index * total, total, 0)
        peer_ids = lax.dynamic_slice_in_dim(local_ids, (1 - tp_index) * total, total, 0)
        peer_in = lax.dynamic_slice_in_dim(in_shard, (1 - tp_index) * total, total, 0)
        own_cot = lax.dynamic_slice_in_dim(cotangent, tp_index * total, total, 0)

        def rows_of(ids, inside):
            rows = jnp.take(emb_table, jnp.where(inside, ids, 0), axis=0)
            return jnp.where(inside[:, :, None], rows, 0.0).astype(F32)

        def small_of(own):
            return jnp.concatenate([own, lax.ppermute(own, 'tp', SWAP)])

        fwd_groups = groups_of(total, 2)
        arrived = []
        for base, count in fwd_groups:
            arrived.append(lax.ppermute(rows_of(peer_ids[base:base + count], peer_in[base:base + count]), 'tp', SWAP))
            if base == 0:
                wqkv_full = with_peer_half(w_qkv, 1, dp_index, parts)
                wout_full = with_peer_half(w_out, 0, dp_index, parts)
                packed = small_of(jnp.concatenate([b_qkv.astype(F32).reshape(-1), b_gate.astype(F32), b_lin.astype(F32)]).reshape(1, -1))
                own_size = b_qkv.size
                wide_loc = b_gate.shape[0]
                bqkv_full = packed[:, :own_size].reshape(1, -1)
                bgate_full = packed[:, own_size:own_size + wide_loc].reshape(1, -1)
                blin_full = packed[:, own_size + wide_loc:].reshape(1, -1)
        wgate_full = with_peer_half(w_gate, 1, dp_index, parts)
        wlin_full = with_peer_half(w_lin, 1, dp_index, parts)
        wdown_full = with_peer_half(w_down, 0, dp_index, parts)

        half_dim = head_dim // 2
        inv_freq = ROPE_BASE ** (-2.0 * jnp.arange(half_dim, dtype=F32) / head_dim)
        angles = jnp.arange(seq_len, dtype=F32)[:, None] * inv_freq[None, :]
        cos_half, sin_half = jnp.cos(angles), jnp.sin(angles)
        tables = (jnp.concatenate([cos_half] * 4, axis=1), jnp.concatenate([-sin_half, sin_half] * 2, axis=1))

        def row_of(vector):
            return vector.astype(F32).reshape(1, -1)

        front = (wqkv_full, bqkv_full, wout_full, row_of(b_out), row_of(ln1_gain), row_of(ln1_bias))
        saved, embs = None, []
        for (base, count), other in zip(fwd_groups, arrived):
            emb = (rows_of(own_ids[base:base + count], own_in[base:base + count]) + other).astype(BF16)
            embs.append(emb)
            saved = attn_forward(base, total, emb, front, tables, saved, head_dim)
        qkv, probs, context, hat, rstd, hidden = saved
        emb_rows = jnp.concatenate(embs, axis=0).reshape(-1, width)

        (inner, d_gate, d_lin, d_ffn, d_resid, narrow, wide) = ffn(
            hidden, own_cot, hat, rstd, (wgate_full, wlin_full, wdown_full, bgate_full, blin_full, row_of(b_down), row_of(ln1_gain), row_of(ln2_gain)))

        def outer(left, right):
            return lax.dot_general(left, right, (((0,), (0,)), ((), ())), preferred_element_type=F32)

        hid_rows, ffn_rows = hidden.reshape(-1, width), d_ffn.reshape(-1, width)
        wide_loc = w_gate.shape[1]
        d_w_down = reduce_weight(outer(inner, ffn_rows).reshape(2, wide_loc, width), parts)
        d_w_gate = reduce_weight(jnp.stack([outer(hid_rows, d_gate[:, :wide_loc]), outer(hid_rows, d_gate[:, wide_loc:])]), parts)
        d_w_lin = reduce_weight(jnp.stack([outer(hid_rows, d_lin[:, :wide_loc]), outer(hid_rows, d_lin[:, wide_loc:])]), parts)

        d_qkv, bias_parts, d_own, d_peer = None, [], [], []
        for base, count in groups_of(total, 2):
            d_emb, d_qkv, bias_part = attn_backward(base, count, total, d_resid, qkv, probs, (wqkv_full, wout_full), tables, d_qkv, head_dim)
            bias_parts.append(bias_part)
            d_own.append(d_emb)
            d_peer.append(lax.ppermute(d_emb, 'tp', SWAP))

        d_rows = jnp.concatenate(d_own + d_peer, axis=0).reshape(-1, width)
        row_ids = jnp.concatenate([jnp.where(own_in, own_ids, vocab_loc), jnp.where(peer_in, peer_ids, vocab_loc)], axis=0).reshape(-1)
        d_table = jnp.zeros((vocab_loc, width), F32).at[row_ids].add(d_rows, mode='drop')
        d_table = lax.psum(d_table, 'dp')

        qkv_rows = d_qkv.reshape(-1, d_qkv.shape[-1])
        qkv_loc = w_qkv.shape[1]
        d_w_qkv = reduce_weight(jnp.stack([outer(emb_rows, qkv_rows[:, :qkv_loc]), outer(emb_rows, qkv_rows[:, qkv_loc:])]), parts)
        d_w_out = reduce_weight(outer(context.reshape(-1, width), d_resid.astype(BF16).reshape(-1, width)).reshape(2, w_out.shape[0], width), parts)

        d_bqkv = jnp.sum(sum(bias_parts), axis=0).reshape(2, -1)
        d_bwide = jnp.sum(wide.reshape(2, 8, -1), axis=1).reshape(2, 2, -1)
        split = jnp.concatenate([d_bqkv, d_bwide[0], d_bwide[1]], axis=1)
        split = jnp.where(tp_index == 0, split, split[::-1])
        flat = jnp.concatenate([split.reshape(-1), jnp.sum(narrow.reshape(5, 8, -1), axis=1).reshape(-1)])
        flat = lax.psum(flat, ('tp', 'dp'))
        split_size = split.shape[1]
        own_split = lax.dynamic_slice_in_dim(flat, tp_index * split_size, split_size, 0)
        d_b_qkv = own_split[:qkv_loc].reshape(b_qkv.shape)
        d_b_gate = own_split[qkv_loc:qkv_loc + wide_loc]
        d_b_lin = own_split[qkv_loc + wide_loc:]
        d_ln2_gain, d_b_down, d_ln1_bias, d_ln1_gain, d_b_out = flat[2 * split_size:].reshape(5, width)
        return (d_table, d_w_qkv, d_b_qkv, d_w_out, d_b_out, d_ln1_gain, d_ln1_bias, d_w_gate, d_b_gate, d_w_lin, d_b_lin, d_w_down, d_b_down, d_ln2_gain)

    return jax.shard_map(device_step, mesh=mesh, in_specs=in_specs, out_specs=out_specs, check_vma=False)
```

time: 4840 us -> 2260 us (0.47)
  waiting for transfers between devices: 3350 us -> 1170 us
  matrix products: 903 us -> 113 us
  Pallas kernels: 0 us -> 516 us
  other arithmetic: 404 us -> 134 us
  local copies, waits for them, and re-layouts: 134 us -> 256 us
    psum x6 -> x1, waiting for transfers between devices: 3350 us -> 499 us  [device_step(): d_table = lax.psum(d_table, 'dp')]
    dot_general x20 -> x8, matrix products: 858 us -> 113 us  [outer(): lax.dot_general(left, right, (((0,), (0,)), ((), ())), preferred_element_...]
    ppermute x0 -> x19, waiting for transfers between devices: none -> 560 us  [the longest x5 261 us: with_peer_half(): piece = lax.ppermute(piece, 'tp', SWAP)]
    pallas_call x0 -> x14, Pallas kernels: none -> 516 us  [the longest x1 226 us: ffn(): pl.pallas_call(ffn_kernel, grid=(count,), in_specs=specs, out_specs=[anyw...]
    reduce_sum x10 -> x3, other arithmetic: 189 us -> 0.14 us  [the longest x1 0.06 us: device_step(): d_bwide = jnp.sum(wide.reshape(2, 8, -1), axis=1).reshape(2, 2, -1)]
    reduce_scatter x0 -> x5, waiting for transfers between devices: none -> 106 us  [reduce_weight(): piece = lax.psum_scatter(grad, 'dp', scatter_dimension=1, tiled=True)]
    gather x1 -> x8, local copies, waits for them, and re-layouts: 47.8 us -> 126 us  [rows_of(): rows = jnp.take(emb_table, jnp.where(inside, ids, 0), axis=0)]
    convert_element_type x12 -> x14, other arithmetic: 92.8 us -> 32 us  [the longest x4 11.4 us: device_step(): (rows_of(own_ids[base:base + count], own_in[base:base + count]) + other)....]
  transfers between devices with their start and end apart: 6 -> 35, of which waited for: 6 -> 17; matrix products, arithmetic and copies ran while one was open for 3% -> 19% of each run, Pallas kernels for 0% -> 12%
where the time goes in v1:
time: 2260 us
  waiting for transfers between devices  1170 us (52%)
  Pallas kernels  516 us (23%)
  local copies, waits for them, and re-layouts  256 us (11%)
  other arithmetic  134 us (6%)
  matrix products  113 us (5%)
  blocking collectives  33 us (1%)
  starting transfers between devices  25.2 us (1%)
    psum x1, waiting for transfers between devices, device_step(): d_table = lax.psum(d_table, 'dp')  499 us
    ppermute x5, waiting for transfers between devices, with_peer_half(): piece = lax.ppermute(piece, 'tp', SWAP)  261 us
    ppermute x4, waiting for transfers between devices, device_step(): d_peer.append(lax.ppermute(d_emb, 'tp', SWAP))  252 us
    pallas_call x1, Pallas kernels, ffn(): pl.pallas_call(ffn_kernel, grid=(count,), in_specs=specs, out_specs=[anyw...  226 us
    pallas_call x4, Pallas kernels, attn_backward(): pl.pallas_call(functools.partial(attn_backward_kernel, head_dim, len(extr...  145 us
    gather x8, local copies, waits for them, and re-layouts, rows_of(): rows = jnp.take(emb_table, jnp.where(inside, ids, 0), axis=0)  126 us
    pallas_call x4, Pallas kernels, attn_forward(): pl.pallas_call(functools.partial(attn_forward_kernel, head_dim, len(extra...  115 us
    dot_general x8, matrix products, outer(): lax.dot_general(left, right, (((0,), (0,)), ((), ())), preferred_element_...  113 us
  transfers between devices with their start and end apart: 35, of which 17 were waited for; matrix products, arithmetic and copies ran while one was open for 19% of the time, Pallas kernels for 12%

profile of v1, /device:TPU:0, one launch (start us, length us, event | category | flops | bytes accessed | tf_op | source)
XLA Modules:
  0.0 2258.3 jit_solution(16820292801842681319)
XLA Ops:
  60.7 15.4 gather_fusion.5
  79.6 15.2 gather_fusion.3
  97.8 15.2 gather_fusion.1
  115.8 15.6 gather_fusion.7
  136.5 224.0 %collective-permute-done.9 = f32[192,768]{1,0:T(8,128)S(1)} collective-permute-done((f32[192,768]{1,0:T(8,128)S(1)}, f32[192,768]{1,0:T(8,128)S(1)}, u32[]{:S(2)}, u32[]{:S(2)}) %collective-permute-start.9) | collective-permute-done | bytes 589856 | tf_op jit(solution)/shard_map/ppermute | solution.py:381
  373.3 16.3 gather_fusion.6
  389.6 16.3 gather_fusion
  405.9 16.3 gather_fusion.2
  422.2 16.3 gather_fusion.4
  467.0 28.8 %attn_forward.4 = (bf16[8,512,2304]{2,1,0:T(8,128)(2,1)}, bf16[8,12,768,256]{3,2,1,0:T(8,128)(2,1)}, bf16[8,512,768]{2,1,0:T(8,128)(2,1)}, f32[8,512,768]{2,1,0:...) custom-call(bf16[2,512,768]{2,1,0:T(8,128)(2,1)} %copy-done.5, ...), custom_call_target="tpu_custom_call" | custom-call | flops 12884901888 | bytes 24000000 | tf_op jit(solution)/shard_map/attn_forward/pallas_call | solution.py:299
  495.7 28.7 %attn_forward.5 = (bf16[8,512,2304]{2,1,0:T(8,128)(2,1)}, bf16[8,12,768,256]{3,2,1,0:T(8,128)(2,1)}, bf16[8,512,768]{2,1,0:T(8,128)(2,1)}, f32[8,512,768]{2,1,0:...) custom-call(bf16[2,512,768]{2,1,0:T(8,128)(2,1)} %copy-done.3, ...), custom_call_target="tpu_custom_call", output_to_operand_aliasing={{0}: (9, {}), {1}: (10, {}), {2}: (11, {}), {3}: (12, {}), ... | custom-call | flops 12884901888 | bytes 24000000 | tf_op jit(solution)/shard_map/attn_forward/pallas_call | solution.py:299
  524.5 28.9 %attn_forward.6 = (bf16[8,512,2304]{2,1,0:T(8,128)(2,1)}, bf16[8,12,768,256]{3,2,1,0:T(8,128)(2,1)}, bf16[8,512,768]{2,1,0:T(8,128)(2,1)}, f32[8,512,768]{2,1,0:...) custom-call(bf16[2,512,768]{2,1,0:T(8,128)(2,1)} %copy-done.2, ...), custom_call_target="tpu_custom_call", output_to_operand_aliasing={{0}: (9, {}), {1}: (10, {}), {2}: (11, {}), {3}: (12, {}), ... | custom-call | flops 12884901888 | bytes 24000000 | tf_op jit(solution)/shard_map/attn_forward/pallas_call | solution.py:299
  553.4 28.8 %attn_forward.7 = (bf16[8,512,2304]{2,1,0:T(8,128)(2,1)}, bf16[8,12,768,256]{3,2,1,0:T(8,128)(2,1)}, bf16[8,512,768]{2,1,0:T(8,128)(2,1)}, f32[8,512,768]{2,1,0:...) custom-call(bf16[2,512,768]{2,1,0:T(8,128)(2,1)} %copy-done.1, ...), custom_call_target="tpu_custom_call", output_to_operand_aliasing={{0}: (9, {}), {1}: (10, {}), {2}: (11, {}), {3}: (12, {}), ... | custom-call | flops 12884901888 | bytes 24000000 | tf_op jit(solution)/shard_map/attn_forward/pallas_call | solution.py:299
  610.0 226.4 %ffn.1 = (bf16[4096,3072]{1,0:T(8,128)(2,1)}, bf16[4096,3072]{1,0:T(8,128)(2,1)}, bf16[4096,3072]{1,0:T(8,128)(2,1)}, bf16[8,512,768]{2,1,0:T(8,128)(2,1)}, f32[...) custom-call(bf16[8,512,768]{2,1,0:T(8,128)(2,1)} %get-tuple-element.76.hid_ref, ...), custom_call_target="tpu_custom_call" | custom-call | flops 173946175488 | bytes 112000000 | tf_op jit(solution)/shard_map/ffn/pallas_call | solution.py:321
  853.9 35.7 %attn_backward.4 = (f32[2,512,768]{2,1,0:T(8,128)}, bf16[8,512,2304]{2,1,0:T(8,128)(2,1)}, f32[8,2304]{1,0:T(8,128)}) custom-call(f32[8,512,768]{2,1,0:T(8,128)} %get-tuple-element.79.refs_0_, bf16[8,512,2304]{2,1,0:T(8,128)(2,1)} %get-tuple-element.80.refs_1_, bf16[8,12,768,256]{3,2,1,0:T(8,128)(2,1)} %get-tuple-element.81.refs_2_, ...), custom_call_target="tpu_custom_call" | custom-call | flops 16106127360 | bytes 24000000 | tf_op jit(solution)/shard_map/attn_backward/pallas_call | solution.py:345
  889.6 36.3 %attn_backward.5 = (f32[2,512,768]{2,1,0:T(8,128)}, bf16[8,512,2304]{2,1,0:T(8,128)(2,1)}, f32[8,2304]{1,0:T(8,128)}) custom-call(f32[8,512,768]{2,1,0:T(8,128)} %get-tuple-element.79.refs_0_, bf16[8,512,2304]{2,1,0:T(8,128)(2,1)} %get-tuple-element.80.refs_1_, bf16[8,12,768,256]{3,2,1,0:T(8,128)(2,1)} %get-tuple-element.81.refs_2_, ...), custom_call_target="tpu_custom_call", output_to_operand_aliasing={{1}: (7, {})} | custom-call | flops 16106127360 | bytes 24000000 | tf_op jit(solution)/shard_map/attn_backward/pallas_call | solution.py:345
  925.9 36.4 %attn_backward.6 = (f32[2,512,768]{2,1,0:T(8,128)}, bf16[8,512,2304]{2,1,0:T(8,128)(2,1)}, f32[8,2304]{1,0:T(8,128)}) custom-call(f32[8,512,768]{2,1,0:T(8,128)} %get-tuple-element.79.refs_0_, bf16[8,512,2304]{2,1,0:T(8,128)(2,1)} %get-tuple-element.80.refs_1_, bf16[8,12,768,256]{3,2,1,0:T(8,128)(2,1)} %get-tuple-element.81.refs_2_, ...), custom_call_target="tpu_custom_call", output_to_operand_aliasing={{1}: (7, {})} | custom-call | flops 16106127360 | bytes 24000000 | tf_op jit(solution)/shard_map/attn_backward/pallas_call | solution.py:345
  962.3 36.3 %attn_backward.7 = (f32[2,512,768]{2,1,0:T(8,128)}, bf16[8,512,2304]{2,1,0:T(8,128)(2,1)}, f32[8,2304]{1,0:T(8,128)}) custom-call(f32[8,512,768]{2,1,0:T(8,128)} %get-tuple-element.79.refs_0_, bf16[8,512,2304]{2,1,0:T(8,128)(2,1)} %get-tuple-element.80.refs_1_, bf16[8,12,768,256]{3,2,1,0:T(8,128)(2,1)} %get-tuple-element.81.refs_2_, ...), custom_call_target="tpu_custom_call", output_to_operand_aliasing={{1}: (7, {})} | custom-call | flops 16106127360 | bytes 24000000 | tf_op jit(solution)/shard_map/attn_backward/pallas_call | solution.py:345
  1025.5 14.9 fusion.23
  1057.5 14.5 fusion.29
  1089.1 32.6 %copy.55 = bf16[3072,4096]{1,0:T(8,128)(2,1)} copy(bf16[3072,4096]{0,1:T(8,128)(2,1)} %bitcast.133) | data formatting | bytes 50331648 | tf_op jit(solution)/shard_map/dot_general | solution.py:476
  1121.6 26.2 %fusion.64 = f32[2,1536,768]{2,1,0:T(8,128)} fusion(bf16[2,1536,4096]{2,1,0:T(8,128)(2,1)} %bitcast.134, bf16[4096,768,1]{1,0,2:T(8,128)(2,1)} %bitcast.168), kind=kOutput, calls=%fused_computation.165 | convolution fusion | flops 19327352832 | bytes 40894464 | tf_op jit(solution)/shard_map/dot_general | solution.py:476
  1181.3 50.4 %reduce-scatter.12.cloned.1.call-done = f32[2,96,1536]{2,1,0:T(8,128)} async-done(((f32[2,768,1536]{2,1,0:T(8,128)}), f32[2,96,1536]{2,1,0:T(8,128)}) %reduce-scatter.12.cloned.1.call-update) | async-done | bytes 1179664 | tf_op jit(solution)/shard_map/reduce_scatter | solution.py:404
  1249.7 55.5 %reduce-scatter.14.cloned.1.call-done = f32[2,192,768]{2,1,0:T(8,128)} async-done(((f32[2,1536,768]{2,1,0:T(8,128)}), f32[2,192,768]{2,1,0:T(8,128)}) %reduce-scatter.14.cloned.1.call-update) | async-done | bytes 1179664 | tf_op jit(solution)/shard_map/reduce_scatter | solution.py:404
  1337.1 57.1 %collective-permute-done.10 = f32[2,512,768]{2,1,0:T(8,128)S(1)} collective-permute-done((f32[2,512,768]{2,1,0:T(8,128)}, f32[2,512,768]{2,1,0:T(8,128)S(1)}, u32[]{:S(2)}, u32[]{:S(2)}) %collective-permute-start.10) | collective-permute-done | bytes 3145760 | tf_op jit(solution)/shard_map/ppermute | solution.py:489
  1396.0 65.6 %collective-permute-done.11 = f32[2,512,768]{2,1,0:T(8,128)S(1)} collective-permute-done((f32[2,512,768]{2,1,0:T(8,128)}, f32[2,512,768]{2,1,0:T(8,128)S(1)}, u32[]{:S(2)}, u32[]{:S(2)}) %collective-permute-start.11) | collective-permute-done | bytes 3145760 | tf_op jit(solution)/shard_map/ppermute | solution.py:489
  1463.5 65.6 %collective-permute-done.12 = f32[2,512,768]{2,1,0:T(8,128)S(1)} collective-permute-done((f32[2,512,768]{2,1,0:T(8,128)}, f32[2,512,768]{2,1,0:T(8,128)S(1)}, u32[]{:S(2)}, u32[]{:S(2)}) %collective-permute-start.12) | collective-permute-done | bytes 3145760 | tf_op jit(solution)/shard_map/ppermute | solution.py:489
  1530.9 63.3 %collective-permute-done.13 = f32[2,512,768]{2,1,0:T(8,128)S(1)} collective-permute-done((f32[2,512,768]{2,1,0:T(8,128)S(1)}, f32[2,512,768]{2,1,0:T(8,128)S(1)}, u32[]{:S(2)}, u32[]{:S(2)}) %collective-permute-start.13) | collective-permute-done | bytes 3145760 | tf_op jit(solution)/shard_map/ppermute | solution.py:489
  1596.1 72.9 %scatter_custom_fusion = f32[15296,768]{1,0:T(8,128)} fusion(s32[8192]{0:T(1024)S(1)} %bitcast.157, f32[8192,768]{1,0:T(8,128)} %bitcast.151, f32[]{:T(128)} %constant.28.clone.1), kind=kCustom, calls=%fused_computation.9 | custom fusion | flops 6291456 | bytes 46989824 | tf_op jit(solution)/shard_map/scatter-add | solution.py:493
  1671.2 33.0 %psum.15 = f32[12288]{0:T(1024)S(1)} all-reduce(f32[12288]{0:T(1024)S(1)} %pad_maximum_fusion.6), channel_id=1, replica_groups=mesh['tp'=2,'dp'=8] {'tp','dp'}, use_global_device_ids=true, to_apply=%region_6.8 | all-reduce | flops 12288 | bytes 98304 | tf_op jit(solution)/shard_map/psum | solution.py:506
  1706.4 499.3 %all-reduce.2.cloned.1.call-done = f32[15296,768]{1,0:T(8,128)} async-done(((f32[15296,768]{1,0:T(8,128)}), f32[15296,768]{1,0:T(8,128)}) %all-reduce.2.cloned.1.call-update) | async-done | bytes 46989328 | tf_op jit(solution)/shard_map/psum | solution.py:494
  2205.7 33.0 %copy.104 = f32[15296,768]{1,0:T(8,128)} copy(f32[15296,768]{1,0:T(8,128)} %all-reduce.2.cloned.1.call-done) | data formatting | bytes 93978624
  (293 shorter events, 322.4 us)
Async XLA Ops:
  7.2 433.2 %all-gather.13.cloned.1.call-start = ((), (), s32[]{:S(2)}) async-start(), calls=%async_computation.6 | async-start | bytes 1327104 | tf_op jit(solution)/shard_map/all_gather | solution.py:382
  16.0 446.2 %all-gather.11.cloned.1.call-start = ((), (), s32[]{:S(2)}) async-start(), calls=%async_computation.5 | async-start | bytes 3981312 | tf_op jit(solution)/shard_map/all_gather | solution.py:382
  17.0 11.4 collective-permute-start.1
  29.2 561.6 %all-gather.17.cloned.1.call-start = ((), (), s32[]{:S(2)}) async-start(), calls=%async_computation.8 | async-start | bytes 5308416 | tf_op jit(solution)/shard_map/all_gather | solution.py:382
  30.3 13.8 collective-permute-start.8
  44.9 551.5 %all-gather.15.cloned.1.call-start = ((), (), s32[]{:S(2)}) async-start(), calls=%async_computation.7 | async-start | bytes 5308416 | tf_op jit(solution)/shard_map/all_gather | solution.py:382
  46.0 12.9 collective-permute-start.7
  59.7 542.2 %all-gather.19.cloned.1.call-start = ((), (), s32[]{:S(2)}) async-start(), calls=%async_computation.9 | async-start | bytes 5308416 | tf_op jit(solution)/shard_map/all_gather | solution.py:382
  78.7 367.2 %collective-permute-start.5 = (f32[2,512,768]{2,1,0:T(8,128)}, f32[2,512,768]{2,1,0:T(8,128)}, u32[]{:S(2)}, u32[]{:S(2)}) collective-permute-start(f32[2,512,768]{2,1,0:T(8,128)} %fusion.33), channel_id=1, source_target_pairs={{0,8},{8,0},{1,9},{9,1},{2,10},{10,2},{3,11},{11,3},{4,12},{12,4},... | collective-permute-start | bytes 9437192 | tf_op jit(solution)/shard_map/ppermute | solution.py:440
  96.7 352.2 %collective-permute-start.4 = (f32[2,512,768]{2,1,0:T(8,128)}, f32[2,512,768]{2,1,0:T(8,128)}, u32[]{:S(2)}, u32[]{:S(2)}) collective-permute-start(f32[2,512,768]{2,1,0:T(8,128)} %fusion.34), channel_id=1, source_target_pairs={{0,8},{8,0},{1,9},{9,1},{2,10},{10,2},{3,11},{11,3},{4,12},{12,4},... | collective-permute-start | bytes 9437192 | tf_op jit(solution)/shard_map/ppermute | solution.py:440
  114.9 337.0 %collective-permute-start = (f32[2,512,768]{2,1,0:T(8,128)}, f32[2,512,768]{2,1,0:T(8,128)}, u32[]{:S(2)}, u32[]{:S(2)}) collective-permute-start(f32[2,512,768]{2,1,0:T(8,128)} %fusion.35), channel_id=1, source_target_pairs={{0,8},{8,0},{1,9},{9,1},{2,10},{10,2},{3,11},{11,3},{4,12},{12,4},... | collective-permute-start | bytes 9437192 | tf_op jit(solution)/shard_map/ppermute | solution.py:440
  133.4 321.4 %collective-permute-start.6 = (f32[2,512,768]{2,1,0:T(8,128)}, f32[2,512,768]{2,1,0:T(8,128)}, u32[]{:S(2)}, u32[]{:S(2)}) collective-permute-start(f32[2,512,768]{2,1,0:T(8,128)} %fusion.32), channel_id=1, source_target_pairs={{0,8},{8,0},{1,9},{9,1},{2,10},{10,2},{3,11},{11,3},{4,12},{12,4},... | collective-permute-start | bytes 9437192 | tf_op jit(solution)/shard_map/ppermute | solution.py:440
  135.5 225.0 %collective-permute-start.9 = (f32[192,768]{1,0:T(8,128)S(1)}, f32[192,768]{1,0:T(8,128)S(1)}, u32[]{:S(2)}, u32[]{:S(2)}) collective-permute-start(f32[192,768]{1,0:T(8,128)S(1)} %dynamic-slice_convert_fusion), channel_id=1, source_target_pairs={{0,8},{8,0},{1,9},{9,1},{2,10},{10,2},{3,11},{11,3},{4,12},{12,4},... | collective-permute-start | bytes 1769480 | tf_op jit(solution)/shard_map/ppermute | solution.py:381
  361.4 786.5 %reduce-scatter.8.cloned.1.call-start = ((), (), s32[]{:S(2)}) async-start(), calls=%async_computation.13 | async-start | bytes 2654208 | tf_op jit(solution)/shard_map/reduce_scatter | solution.py:404
  361.5 77.0 %collective-permute-start.2 = (f32[1,4224]{1,0:T(1,128)S(1)}, f32[1,4224]{1,0:T(1,128)S(1)}, u32[]{:S(2)}, u32[]{:S(2)}) collective-permute-start(f32[1,4224]{1,0:T(1,128)S(1)} %reshape.220), channel_id=1, source_target_pairs={{0,8},{8,0},{1,9},{9,1},{2,10},{10,2},{3,11},{11,3},{4,12},{12,4},... | collective-permute-start | bytes 50696 | tf_op jit(solution)/shard_map/ppermute | solution.py:435
  853.8 302.1 %reduce-scatter.6.cloned.1.call-start = ((), (), s32[]{:S(2)}) async-start(), calls=%async_computation.11 | async-start | bytes 7962624 | tf_op jit(solution)/shard_map/reduce_scatter | solution.py:404
  1025.4 142.8 %reduce-scatter.10.cloned.1.call-start = ((), (), s32[]{:S(2)}) async-start(), calls=%async_computation.15 | async-start | bytes 10616832 | tf_op jit(solution)/shard_map/reduce_scatter | solution.py:404
  1057.4 174.3 %reduce-scatter.12.cloned.1.call-start = ((), (), s32[]{:S(2)}) async-start(), calls=%async_computation.17 | async-start | bytes 10616832 | tf_op jit(solution)/shard_map/reduce_scatter | solution.py:404
  1089.0 216.2 %reduce-scatter.14.cloned.1.call-start = ((), (), s32[]{:S(2)}) async-start(), calls=%async_computation.19 | async-start | bytes 10616832 | tf_op jit(solution)/shard_map/reduce_scatter | solution.py:404
  1147.9 558.4 %all-gather.23.cloned.1.call-start = ((), (), s32[]{:S(2)}) async-start(), calls=%async_computation.14 | async-start | bytes 1327104 | tf_op jit(solution)/shard_map/all_gather | solution.py:406
  1155.8 550.5 %all-gather.21.cloned.1.call-start = ((), (), s32[]{:S(2)}) async-start(), calls=%async_computation.12 | async-start | bytes 3981312 | tf_op jit(solution)/shard_map/all_gather | solution.py:406
  1167.9 538.4 %all-gather.25.cloned.1.call-start = ((), (), s32[]{:S(2)}) async-start(), calls=%async_computation.16 | async-start | bytes 5308416 | tf_op jit(solution)/shard_map/all_gather | solution.py:406
  1169.4 9.9 collective-permute-start.16
  1181.3 525.1 %all-gather.27.cloned.1.call-start = ((), (), s32[]{:S(2)}) async-start(), calls=%async_computation.18 | async-start | bytes 5308416 | tf_op jit(solution)/shard_map/all_gather | solution.py:406
  1232.8 14.9 collective-permute-start.17
  1249.7 456.7 %all-gather.29.cloned.1.call-start = ((), (), s32[]{:S(2)}) async-start(), calls=%async_computation.20 | async-start | bytes 5308416 | tf_op jit(solution)/shard_map/all_gather | solution.py:406
  1306.3 14.9 collective-permute-start.18
  1323.1 882.6 %all-reduce.2.cloned.1.call-start = ((), (), s32[]{:S(2)}) async-start(), calls=%async_computation.10 | async-start | bytes 93978624 | tf_op jit(solution)/shard_map/psum | solution.py:494
  1323.2 71.0 %collective-permute-start.10 = (f32[2,512,768]{2,1,0:T(8,128)}, f32[2,512,768]{2,1,0:T(8,128)S(1)}, u32[]{:S(2)}, u32[]{:S(2)}) collective-permute-start(f32[2,512,768]{2,1,0:T(8,128)} %get-tuple-element.82), channel_id=1, source_target_pairs={{0,8},{8,0},{1,9},{9,1},{2,10},{10,2},{3,11},{11,3},{4,12},{12,4},... | collective-permute-start | bytes 9437192 | tf_op jit(solution)/shard_map/ppermute | solution.py:489
  1324.7 136.9 %collective-permute-start.11 = (f32[2,512,768]{2,1,0:T(8,128)}, f32[2,512,768]{2,1,0:T(8,128)S(1)}, u32[]{:S(2)}, u32[]{:S(2)}) collective-permute-start(f32[2,512,768]{2,1,0:T(8,128)} %get-tuple-element.84), channel_id=1, source_target_pairs={{0,8},{8,0},{1,9},{9,1},{2,10},{10,2},{3,11},{11,3},{4,12},{12,4},... | collective-permute-start | bytes 9437192 | tf_op jit(solution)/shard_map/ppermute | solution.py:489
  1325.2 203.8 %collective-permute-start.12 = (f32[2,512,768]{2,1,0:T(8,128)}, f32[2,512,768]{2,1,0:T(8,128)S(1)}, u32[]{:S(2)}, u32[]{:S(2)}) collective-permute-start(f32[2,512,768]{2,1,0:T(8,128)} %get-tuple-element.86), channel_id=1, source_target_pairs={{0,8},{8,0},{1,9},{9,1},{2,10},{10,2},{3,11},{11,3},{4,12},{12,4},... | collective-permute-start | bytes 9437192 | tf_op jit(solution)/shard_map/ppermute | solution.py:489
  1326.7 267.5 %collective-permute-start.13 = (f32[2,512,768]{2,1,0:T(8,128)S(1)}, f32[2,512,768]{2,1,0:T(8,128)S(1)}, u32[]{:S(2)}, u32[]{:S(2)}) collective-permute-start(f32[2,512,768]{2,1,0:T(8,128)S(1)} %copy-done.11), channel_id=1, source_target_pairs={{0,8},{8,0},{1,9},{9,1},{2,10},{10,2},{3,11},{11,3},{4,12},{12,4},... | collective-permute-start | bytes 9437192 | tf_op jit(solution)/shard_map/ppermute | solution.py:489
  (55 other events, 1237.7 us)
Sparse Core Ops, SparseCore 0:
  16.1 21.1 all-gather.12
  39.2 29.7 all-gather.10
  70.8 34.7 all-gather.16
  107.3 34.7 all-gather.14
  361.5 34.5 all-gather.18
  853.9 36.2 reduce-scatter.7
  1025.5 58.8 reduce-scatter.5
  1087.9 70.1 reduce-scatter.9
  1161.5 70.1 reduce-scatter.11
  1235.0 70.1 reduce-scatter.13
  1307.0 19.9 all-gather.22
  1328.7 29.7 all-gather.20
  1360.9 34.7 all-gather.24
  1398.0 34.7 all-gather.26
  1434.4 34.7 all-gather.28
  1669.2 536.4 all-reduce.1

commit v2 on v1

--- a/solution.py
+++ b/solution.py
@@ -6,6 +6,7 @@
 from jax.experimental import pallas as pl
 from jax.experimental.pallas import tpu as pltpu
 from jax.sharding import PartitionSpec as P
+
 
 ALPHA = 140.0 ** 0.5
 EPS = 1e-5
@@ -50,9 +51,11 @@
 
 
 def attn_forward_kernel(head_dim, alias_count, *refs):
-    (emb_ref, wqkv_ref, bqkv_ref, wo_ref, bo_ref, gain_ref, bias_ref, cos_ref, sin_ref) = refs[:9]
-    (qkv_ref, prob_ref, ctx_ref, hat_ref, rstd_ref, hid_ref) = refs[9 + alias_count:]
-    seq_len, width = emb_ref.shape[1], emb_ref.shape[2]
+    (own_ref, other_ref, wqkv_ref, bqkv_ref, wo_ref, bo_ref, gain_ref, bias_ref, cos_ref, sin_ref) = refs[:10]
+    (emb_ref, qkv_ref, prob_ref, ctx_ref, hat_ref, rstd_ref, hid_ref, token_ref) = refs[10 + alias_count:]
+    seq_len, width = own_ref.shape[1], own_ref.shape[2]
+    token_ref[...] = jnp.zeros_like(token_ref)
+    emb_ref[0] = (own_ref[0].astype(F32) + other_ref[0]).astype(BF16)
     low, mask_low, mask_high, first_half = lane_masks()
     score_scale = head_dim ** -0.5 * LOG2E
     causal = lax.broadcasted_iota(jnp.int32, (HALF_Q, HALF_Q), 0) <= lax.broadcasted_iota(jnp.int32, (HALF_Q, HALF_Q), 1)
@@ -112,17 +115,19 @@
     hid_ref[0] = (hat * gain_ref[...] + bias_ref[...]).astype(BF16)
 
 
-def ffn_kernel(hid_ref, cot_ref, hat_ref, rstd_ref, wg_ref, wl_ref, wd_ref, bg_ref, bl_ref, bd_ref, gain1_ref, gain2_ref,
-               inner_out, gate_out, lin_out, dffn_ref, dres_ref, narrow_ref, wide_ref,
-               act_buf, slope_buf, inner_buf, gate_buf, lin_buf, acc_buf, sems):
+def ffn_kernel(base, chunk_size, hid_ref, cot_ref, hat_ref, rstd_ref, wg_ref, wl_ref, wd_ref, bg_ref, bl_ref, bd_ref, gain1_ref, gain2_ref,
+               *refs):
+    (inner_out, gate_out, lin_out, dffn_ref, dres_ref, dattn_ref, narrow_ref, wide_ref, token_ref,
+     act_buf, slope_buf, inner_buf, gate_buf, lin_buf, acc_buf, sems) = refs[-16:]
     step = pl.program_id(0)
     last = pl.num_programs(0) - 1
-    rows, width = hid_ref.shape[1], hid_ref.shape[2]
-    chunks = wg_ref.shape[1] // CHUNK
+    token_ref[...] = jnp.zeros_like(token_ref)
+    rows = hid_ref.shape[1]
+    chunks = wg_ref.shape[1] // chunk_size
 
     def copy_out(buf, out, kind, chunk, block):
-        cols = pl.ds(pl.multiple_of(chunk * CHUNK, CHUNK), CHUNK)
-        return pltpu.make_async_copy(buf.at[:, cols], out.at[pl.ds(block * rows, rows), cols], sems.at[kind, chunk])
+        cols = pl.ds(pl.multiple_of(chunk * chunk_size, chunk_size), chunk_size)
+        return pltpu.make_async_copy(buf.at[:, cols], out.at[pl.ds((block + base) * rows, rows), cols], sems.at[kind, chunk])
 
     @pl.when(step == 0)
     def _():
@@ -132,7 +137,7 @@
     acc_buf[...] = jnp.zeros_like(acc_buf)
 
     def forward(chunk, carry):
-        cols = pl.ds(pl.multiple_of(chunk * CHUNK, CHUNK), CHUNK)
+        cols = pl.ds(pl.multiple_of(chunk * chunk_size, chunk_size), chunk_size)
         gate_pre = dot_nn(hid_ref[0], wg_ref[:, cols]) + bg_ref[:, cols]
         lin_pre = dot_nn(hid_ref[0], wl_ref[:, cols]) + bl_ref[:, cols]
         cdf = 0.5 + 0.5 * lax.erf(gate_pre * (0.5 ** 0.5))
@@ -166,7 +171,7 @@
     acc_buf[...] = ALPHA * d_resid
 
     def backward(chunk, carry):
-        cols = pl.ds(pl.multiple_of(chunk * CHUNK, CHUNK), CHUNK)
+        cols = pl.ds(pl.multiple_of(chunk * chunk_size, chunk_size), chunk_size)
         d_inner = dot_nt(dffn_ref[0], wd_ref[cols, :]).astype(BF16).astype(F32)
         d_gate = d_inner * slope_buf[:, cols]
         d_lin = d_inner * act_buf[:, cols]
@@ -196,6 +201,7 @@
     d_resid = rstd_ref[0][:, :1] * (d_hat - jnp.mean(d_hat, axis=-1, keepdims=True) - hat * jnp.mean(d_hat * hat, axis=-1, keepdims=True))
     narrow_ref[32:40] += row_sums(d_resid)
     dres_ref[0] = d_resid
+    dattn_ref[0] = d_resid.astype(BF16)
 
     @pl.when(step == last)
     def _():
@@ -209,8 +215,9 @@
 
 
 def attn_backward_kernel(head_dim, alias_count, *refs):
-    (dres_ref, qkv_ref, prob_ref, wqkv_ref, wo_ref, cos_ref, sin_ref) = refs[:7]
-    (demb_ref, dqkv_ref, acc_ref) = refs[7 + alias_count:]
+    (dres_ref, dattn_ref, qkv_ref, prob_ref, wqkv_ref, wo_ref, cos_ref, sin_ref) = refs[:8]
+    (demb_ref, dqkv_ref, dall_ref, acc_ref, token_ref) = refs[8 + alias_count:]
+    token_ref[...] = jnp.zeros_like(token_ref)
     width = dres_ref.shape[2]
     low, mask_low, mask_high, first_half = lane_masks()
     attn_scale = head_dim ** -0.5
@@ -220,12 +227,10 @@
     def _():
         acc_ref[...] = jnp.zeros_like(acc_ref)
 
-    d_attn = dres_ref[0].astype(BF16)
-
     def quad(index, carry):
         col = pl.multiple_of(index * step, step)
         ctx_row = pl.multiple_of(index * 4 * head_dim, 4 * head_dim)
-        d_ctx_quad = dot_nt(d_attn, wo_ref[pl.ds(ctx_row, 4 * head_dim), :]).astype(BF16)
+        d_ctx_quad = dot_nt(dattn_ref[0], wo_ref[pl.ds(ctx_row, 4 * head_dim), :]).astype(BF16)
         pieces = []
         for half in range(2):
             pair = index * 2 + half
@@ -270,7 +275,9 @@
         return carry
 
     lax.fori_loop(0, wqkv_ref.shape[1] // step, quad, 0)
-    demb_ref[0] = SHRINK * (ALPHA * dres_ref[0] + dot_nt(dqkv_ref[0], wqkv_ref[...]))
+    d_emb = SHRINK * (ALPHA * dres_ref[0] + dot_nt(dqkv_ref[0], wqkv_ref[...]))
+    demb_ref[0] = d_emb
+    dall_ref[0] = d_emb
 
 
 def whole(shape):
@@ -285,79 +292,120 @@
     return pltpu.CompilerParams(dimension_semantics=('arbitrary',), vmem_limit_bytes=VMEM_LIMIT)
 
 
-def attn_forward(base, total, emb, weights, tables, previous, head_dim):
-    count, seq_len, width = emb.shape
+TOKEN = (8, LANES)
+ANYWHERE = pl.BlockSpec(memory_space=pl.ANY)
+
+
+def token_spec():
+    return pl.BlockSpec(TOKEN, lambda i: (0, 0))
+
+
+def attn_forward(base, count, total, own, other, offset, weights, tables, previous, deps, head_dim):
+    seq_len, width = own.shape[1:]
     wqkv = weights[0]
     heads = width // head_dim
-    shapes = [((seq_len, 3 * width), BF16), ((heads, seq_len * 3 // 2, HALF_Q), BF16), ((seq_len, width), BF16),
+    shapes = [((seq_len, width), BF16), ((seq_len, 3 * width), BF16), ((heads, seq_len * 3 // 2, HALF_Q), BF16), ((seq_len, width), BF16),
               ((seq_len, width), F32), ((seq_len, LANES), F32), ((seq_len, width), BF16)]
-    operands = (emb,) + tuple(weights) + tuple(tables)
-    specs = [per_seq((seq_len, width))] + [whole(item.shape) for item in operands[1:]]
+    operands = (own, other) + tuple(weights) + tuple(tables)
+    specs = [per_seq((seq_len, width), base), per_seq((seq_len, width), offset)] + [whole(item.shape) for item in operands[2:]]
     extra = tuple(previous) if previous is not None else ()
-    specs += [pl.BlockSpec(memory_space=pl.ANY)] * len(extra)
+    specs += [ANYWHERE] * (len(extra) + len(deps))
     flops = count * (2 * seq_len * width * (wqkv.shape[1] + width) + 4 * heads * seq_len * seq_len * 64)
     return pl.pallas_call(
-        functools.partial(attn_forward_kernel, head_dim, len(extra)),
+        functools.partial(attn_forward_kernel, head_dim, len(extra) + len(deps)),
         grid=(count,),
         in_specs=specs,
-        out_specs=[per_seq(shape, base) for shape, _ in shapes],
-        out_shape=[jax.ShapeDtypeStruct((total,) + shape, dtype) for shape, dtype in shapes],
+        out_specs=[per_seq(shape, base) for shape, _ in shapes] + [token_spec()],
+        out_shape=[jax.ShapeDtypeStruct((total,) + shape, dtype) for shape, dtype in shapes] + [jax.ShapeDtypeStruct(TOKEN, F32)],
         input_output_aliases={len(operands) + num: num for num in range(len(extra))},
         compiler_params=params(),
         cost_estimate=pl.CostEstimate(flops=2 * flops, bytes_accessed=count * 12_000_000, transcendentals=0),
         name='attn_forward',
-    )(*operands, *extra)
-
-
-def ffn(hidden, cotangent, hat, rstd, weights):
-    count, seq_len, width = hidden.shape
+    )(*operands, *extra, *deps)
+
+
+def ffn(base, count, chunk_size, hidden, cotangent, hat, rstd, weights, previous, deps):
+    total, seq_len, width = hidden.shape
     wide = weights[0].shape[1]
-    rows = count * seq_len
     operands = (hidden, cotangent, hat, rstd) + tuple(weights)
-    specs = [per_seq(item.shape[1:]) for item in operands[:4]] + [whole(item.shape) for item in operands[4:]]
-    anywhere = pl.BlockSpec(memory_space=pl.ANY)
-    big = jax.ShapeDtypeStruct((rows, wide), BF16)
-    flops = 12 * rows * width * wide
+    extra = tuple(previous) if previous is not None else ()
+    specs = [per_seq(item.shape[1:], base) for item in operands[:4]] + [whole(item.shape) for item in operands[4:]]
+    specs += [ANYWHERE] * (len(extra) + len(deps))
+    big = jax.ShapeDtypeStruct((total * seq_len, wide), BF16)
+    narrow = jax.ShapeDtypeStruct((total, seq_len, width), BF16)
+    flops = 12 * count * seq_len * width * wide
     return pl.pallas_call(
-        ffn_kernel,
+        functools.partial(ffn_kernel, base, chunk_size),
         grid=(count,),
         in_specs=specs,
-        out_specs=[anywhere] * 3 + [per_seq((seq_len, width))] * 2 + [pl.BlockSpec((40, width), lambda i: (0, 0)), pl.BlockSpec((16, wide), lambda i: (0, 0))],
-        out_shape=[big] * 3 + [jax.ShapeDtypeStruct((count, seq_len, width), BF16), jax.ShapeDtypeStruct((count, seq_len, width), F32),
-                               jax.ShapeDtypeStruct((40, width), F32), jax.ShapeDtypeStruct((16, wide), F32)],
+        out_specs=[ANYWHERE] * 3 + [per_seq((seq_len, width), base)] * 3 + [pl.BlockSpec((40, width), lambda i: (0, 0)), pl.BlockSpec((16, wide), lambda i: (0, 0)), token_spec()],
+        out_shape=[big] * 3 + [narrow, jax.ShapeDtypeStruct((total, seq_len, width), F32), narrow,
+                               jax.ShapeDtypeStruct((40, width), F32), jax.ShapeDtypeStruct((16, wide), F32), jax.ShapeDtypeStruct(TOKEN, F32)],
         scratch_shapes=[pltpu.VMEM((seq_len, wide), F32)] * 2 + [pltpu.VMEM((seq_len, wide), BF16)] * 3
-        + [pltpu.VMEM((seq_len, width), F32), pltpu.SemaphoreType.DMA((3, wide // CHUNK))],
+        + [pltpu.VMEM((seq_len, width), F32), pltpu.SemaphoreType.DMA((3, wide // chunk_size))],
+        input_output_aliases={len(operands) + num: num for num in range(len(extra))},
         compiler_params=params(),
         cost_estimate=pl.CostEstimate(flops=int(1.5 * flops), bytes_accessed=count * 14_000_000, transcendentals=0),
         name='ffn',
-    )(*operands)
-
-
-def attn_backward(base, count, total, d_resid, qkv, probs, weights, tables, previous, head_dim):
+    )(*operands, *extra, *deps)
+
+
+def attn_backward(base, count, total, d_resid, d_attn, qkv, probs, weights, tables, previous, deps, head_dim):
     seq_len, width = d_resid.shape[1:]
     wqkv, wout = weights
     heads = width // head_dim
-    operands = (d_resid, qkv, probs, wqkv, wout) + tuple(tables)
-    specs = [per_seq(item.shape[1:], base) for item in operands[:3]] + [whole(item.shape) for item in operands[3:]]
-    extra = (previous,) if previous is not None else ()
-    specs += [pl.BlockSpec(memory_space=pl.ANY)] * len(extra)
+    operands = (d_resid, d_attn, qkv, probs, wqkv, wout) + tuple(tables)
+    specs = [per_seq(item.shape[1:], base) for item in operands[:4]] + [whole(item.shape) for item in operands[4:]]
+    extra = tuple(previous) if previous is not None else ()
+    specs += [ANYWHERE] * (len(extra) + len(deps))
     flops = count * (2 * seq_len * width * (wqkv.shape[1] + width) + 8 * heads * seq_len * seq_len * 64)
     return pl.pallas_call(
-        functools.partial(attn_backward_kernel, head_dim, len(extra)),
+        functools.partial(attn_backward_kernel, head_dim, len(extra) + len(deps)),
         grid=(count,),
         in_specs=specs,
-        out_specs=[per_seq((seq_len, width)), per_seq((seq_len, wqkv.shape[1]), base), pl.BlockSpec((8, wqkv.shape[1]), lambda i: (0, 0))],
+        out_specs=[per_seq((seq_len, width)), per_seq((seq_len, wqkv.shape[1]), base), per_seq((seq_len, width), base), pl.BlockSpec((8, wqkv.shape[1]), lambda i: (0, 0)), token_spec()],
         out_shape=[jax.ShapeDtypeStruct((count, seq_len, width), F32), jax.ShapeDtypeStruct((total, seq_len, wqkv.shape[1]), BF16),
-                   jax.ShapeDtypeStruct((8, wqkv.shape[1]), F32)],
-        input_output_aliases={len(operands): 1} if extra else {},
+                   jax.ShapeDtypeStruct((total, seq_len, width), F32),
+                   jax.ShapeDtypeStruct((8, wqkv.shape[1]), F32), jax.ShapeDtypeStruct(TOKEN, F32)],
+        input_output_aliases={len(operands) + num: 1 + num for num in range(len(extra))},
         compiler_params=params(),
         cost_estimate=pl.CostEstimate(flops=2 * flops, bytes_accessed=count * 12_000_000, transcendentals=0),
         name='attn_backward',
-    )(*operands, *extra)
-
-
-def groups_of(total, size):
-    return [(base, min(size, total - base)) for base in range(0, total, size)]
+    )(*operands, *extra, *deps)
+
+
+def outer_kernel(flip, left_ref, right_ref, *refs):
+    out_ref, token_ref, left_t = refs[-3:]
+    token_ref[...] = jnp.zeros_like(token_ref)
+
+    @pl.when(pl.program_id(0) == 0)
+    def _():
+        def turn(index, carry):
+            rows = pl.ds(pl.multiple_of(index * CHUNK, CHUNK), CHUNK)
+            left_t[:, rows] = left_ref[rows, :].astype(F32).T.astype(BF16)
+            return carry
+
+        lax.fori_loop(0, left_ref.shape[0] // CHUNK, turn, 0)
+
+    result = dot_nn(left_t[...], right_ref[...])
+    out_ref[...] = result.T if flip else result
+
+
+def outer(left, right, block, flip, deps):
+    rows, width = left.shape
+    wide = right.shape[1]
+    shape = (wide, width) if flip else (width, wide)
+    return pl.pallas_call(
+        functools.partial(outer_kernel, flip),
+        grid=(wide // block,),
+        in_specs=[whole((rows, width)), pl.BlockSpec((rows, block), lambda i: (0, i))] + [ANYWHERE] * len(deps),
+        out_specs=[pl.BlockSpec((block, width), lambda i: (i, 0)) if flip else pl.BlockSpec((width, block), lambda i: (0, i)), token_spec()],
+        out_shape=[jax.ShapeDtypeStruct(shape, F32), jax.ShapeDtypeStruct(TOKEN, F32)],
+        scratch_shapes=[pltpu.VMEM((width, rows), BF16)],
+        compiler_params=params(),
+        cost_estimate=pl.CostEstimate(flops=2 * rows * width * wide, bytes_accessed=4 * width * wide + 2 * rows * (width + wide), transcendentals=0),
+        name='outer',
+    )(left, right, *deps)
 
 
 def join_kernel(axis, blocks, own_ref, peer_ref, out_ref):
@@ -400,10 +448,21 @@
     )(own, peer)
 
 
-def reduce_weight(grad, parts):
-    piece = lax.psum_scatter(grad, 'dp', scatter_dimension=1, tiled=True)
+def reduce_columns(grad):
+    piece = lax.psum_scatter(grad, 'dp', scatter_dimension=0, tiled=True)
+    half = piece.shape[1] // 2
+    mine = piece[:, :half] + lax.ppermute(piece[:, half:], 'tp', SWAP)
+    return lax.all_gather(mine, 'dp', axis=0, tiled=True)
+
+
+def reduce_rows(grad):
+    piece = lax.psum_scatter(grad.reshape(2, grad.shape[0] // 2, grad.shape[1]), 'dp', scatter_dimension=1, tiled=True)
     mine = piece[0] + lax.ppermute(piece[1], 'tp', SWAP)
     return lax.all_gather(mine, 'dp', axis=0, tiled=True)
+
+
+def tie(value, token):
+    return lax.optimization_barrier((value, token))[0]
 
 
 def solution(mesh):
@@ -434,19 +493,19 @@
         def small_of(own):
             return jnp.concatenate([own, lax.ppermute(own, 'tp', SWAP)])
 
-        fwd_groups = groups_of(total, 2)
-        arrived = []
-        for base, count in fwd_groups:
-            arrived.append(lax.ppermute(rows_of(peer_ids[base:base + count], peer_in[base:base + count]), 'tp', SWAP))
-            if base == 0:
-                wqkv_full = with_peer_half(w_qkv, 1, dp_index, parts)
-                wout_full = with_peer_half(w_out, 0, dp_index, parts)
-                packed = small_of(jnp.concatenate([b_qkv.astype(F32).reshape(-1), b_gate.astype(F32), b_lin.astype(F32)]).reshape(1, -1))
-                own_size = b_qkv.size
-                wide_loc = b_gate.shape[0]
-                bqkv_full = packed[:, :own_size].reshape(1, -1)
-                bgate_full = packed[:, own_size:own_size + wide_loc].reshape(1, -1)
-                blin_full = packed[:, own_size + wide_loc:].reshape(1, -1)
+        size = total // 4
+        quarters = [(num * size, size) for num in range(4)]
+        first = rows_of(peer_ids[:size], peer_in[:size])
+        rest = rows_of(peer_ids[size:], peer_in[size:])
+        wqkv_full = with_peer_half(w_qkv, 1, dp_index, parts)
+        wout_full = with_peer_half(w_out, 0, dp_index, parts)
+        arrived = [lax.ppermute(first, 'tp', SWAP)] + [lax.ppermute(rest[num * size:(num + 1) * size], 'tp', SWAP) for num in range(3)]
+        packed = small_of(jnp.concatenate([b_qkv.astype(F32).reshape(-1), b_gate.astype(F32), b_lin.astype(F32)]).reshape(1, -1))
+        own_size = b_qkv.size
+        wide_loc = b_gate.shape[0]
+        bqkv_full = packed[:, :own_size].reshape(1, -1)
+        bgate_full = packed[:, own_size:own_size + wide_loc].reshape(1, -1)
+        blin_full = packed[:, own_size + wide_loc:].reshape(1, -1)
         wgate_full = with_peer_half(w_gate, 1, dp_index, parts)
         wlin_full = with_peer_half(w_lin, 1, dp_index, parts)
         wdown_full = with_peer_half(w_down, 0, dp_index, parts)
@@ -460,44 +519,63 @@
         def row_of(vector):
             return vector.astype(F32).reshape(1, -1)
 
+        own_rows = jnp.where(own_in[:, :, None], jnp.take(emb_table, jnp.where(own_in, own_ids, 0), axis=0), 0.0)
         front = (wqkv_full, bqkv_full, wout_full, row_of(b_out), row_of(ln1_gain), row_of(ln1_bias))
-        saved, embs = None, []
-        for (base, count), other in zip(fwd_groups, arrived):
-            emb = (rows_of(own_ids[base:base + count], own_in[base:base + count]) + other).astype(BF16)
-            embs.append(emb)
-            saved = attn_forward(base, total, emb, front, tables, saved, head_dim)
-        qkv, probs, context, hat, rstd, hidden = saved
-        emb_rows = jnp.concatenate(embs, axis=0).reshape(-1, width)
-
-        (inner, d_gate, d_lin, d_ffn, d_resid, narrow, wide) = ffn(
-            hidden, own_cot, hat, rstd, (wgate_full, wlin_full, wdown_full, bgate_full, blin_full, row_of(b_down), row_of(ln1_gain), row_of(ln2_gain)))
-
-        def outer(left, right):
-            return lax.dot_general(left, right, (((0,), (0,)), ((), ())), preferred_element_type=F32)
-
-        hid_rows, ffn_rows = hidden.reshape(-1, width), d_ffn.reshape(-1, width)
-        wide_loc = w_gate.shape[1]
-        d_w_down = reduce_weight(outer(inner, ffn_rows).reshape(2, wide_loc, width), parts)
-        d_w_gate = reduce_weight(jnp.stack([outer(hid_rows, d_gate[:, :wide_loc]), outer(hid_rows, d_gate[:, wide_loc:])]), parts)
-        d_w_lin = reduce_weight(jnp.stack([outer(hid_rows, d_lin[:, :wide_loc]), outer(hid_rows, d_lin[:, wide_loc:])]), parts)
-
-        d_qkv, bias_parts, d_own, d_peer = None, [], [], []
-        for base, count in groups_of(total, 2):
-            d_emb, d_qkv, bias_part = attn_backward(base, count, total, d_resid, qkv, probs, (wqkv_full, wout_full), tables, d_qkv, head_dim)
+        middle = (wgate_full, wlin_full, wdown_full, bgate_full, blin_full, row_of(b_down), row_of(ln1_gain), row_of(ln2_gain))
+        saved, ffn_saved, d_kept, deps = None, None, None, ()
+        narrow_parts, wide_parts, bias_parts, d_peer = [], [], [], []
+
+        def run_attention(num):
+            nonlocal saved, deps
+            base, count = quarters[num]
+            out = attn_forward(base, count, total, own_rows, arrived[num], 0, front, tables, saved, deps, head_dim)
+            saved, deps = out[:-1], (out[-1],)
+
+        def run_ffn(base, count, chunk_size):
+            nonlocal ffn_saved, deps
+            out = ffn(base, count, chunk_size, saved[6], own_cot, saved[4], saved[5], middle, ffn_saved, deps)
+            ffn_saved, deps = out[:6], (out[-1],)
+            narrow_parts.append(out[6])
+            wide_parts.append(out[7])
+
+        def run_backward(base, count):
+            nonlocal d_kept, deps
+            d_emb, d_qkv, d_all, bias_part, token = attn_backward(base, count, total, ffn_saved[4], ffn_saved[5], saved[1], saved[2], (wqkv_full, wout_full), tables, d_kept, deps, head_dim)
+            d_kept, deps = (d_qkv, d_all), (token,)
             bias_parts.append(bias_part)
-            d_own.append(d_emb)
             d_peer.append(lax.ppermute(d_emb, 'tp', SWAP))
 
-        d_rows = jnp.concatenate(d_own + d_peer, axis=0).reshape(-1, width)
-        row_ids = jnp.concatenate([jnp.where(own_in, own_ids, vocab_loc), jnp.where(peer_in, peer_ids, vocab_loc)], axis=0).reshape(-1)
-        d_table = jnp.zeros((vocab_loc, width), F32).at[row_ids].add(d_rows, mode='drop')
+        def run_outer(left, right, block, flip=False):
+            nonlocal deps
+            out, token = outer(left.reshape(-1, left.shape[-1]), right.reshape(-1, right.shape[-1]), block, flip, deps)
+            deps = (token,)
+            return out
+
+        for num in range(4):
+            run_attention(num)
+        run_ffn(0, 2 * size, CHUNK)
+        run_backward(0, 2 * size)
+        run_ffn(2 * size, 2 * size, 768)
+        d_w_gate = reduce_columns(run_outer(saved[6], ffn_saved[1], CHUNK))
+        d_w_lin = reduce_columns(run_outer(saved[6], ffn_saved[2], CHUNK))
+        d_w_down = reduce_rows(run_outer(ffn_saved[3], ffn_saved[0], CHUNK, True))
+        run_backward(2 * size, size)
+        run_backward(3 * size, size)
+        d_w_out = reduce_rows(run_outer(saved[3], ffn_saved[5], width))
+        d_w_qkv = reduce_columns(run_outer(saved[0], d_kept[0], width))
+
+        own_row_ids = jnp.where(own_in, own_ids, vocab_loc)
+        peer_row_ids = jnp.where(peer_in, peer_ids, vocab_loc)
+
+        def add_rows(grad, ids, rows):
+            return grad.at[ids.reshape(-1)].add(rows.reshape(-1, width), mode='drop')
+
+        d_table = add_rows(jnp.zeros((vocab_loc, width), F32), tie(own_row_ids, deps[0]), d_kept[1])
+        d_table = add_rows(d_table, peer_row_ids, jnp.concatenate(d_peer, axis=0))
         d_table = lax.psum(d_table, 'dp')
 
-        qkv_rows = d_qkv.reshape(-1, d_qkv.shape[-1])
-        qkv_loc = w_qkv.shape[1]
-        d_w_qkv = reduce_weight(jnp.stack([outer(emb_rows, qkv_rows[:, :qkv_loc]), outer(emb_rows, qkv_rows[:, qkv_loc:])]), parts)
-        d_w_out = reduce_weight(outer(context.reshape(-1, width), d_resid.astype(BF16).reshape(-1, width)).reshape(2, w_out.shape[0], width), parts)
-
+        narrow, wide = sum(narrow_parts), sum(wide_parts)
+        qkv_loc = own_size
         d_bqkv = jnp.sum(sum(bias_parts), axis=0).reshape(2, -1)
         d_bwide = jnp.sum(wide.reshape(2, 8, -1), axis=1).reshape(2, 2, -1)
         split = jnp.concatenate([d_bqkv, d_bwide[0], d_bwide[1]], axis=1)
@@ -512,4 +590,8 @@
         d_ln2_gain, d_b_down, d_ln1_bias, d_ln1_gain, d_b_out = flat[2 * split_size:].reshape(5, width)
         return (d_table, d_w_qkv, d_b_qkv, d_w_out, d_b_out, d_ln1_gain, d_ln1_bias, d_w_gate, d_b_gate, d_w_lin, d_b_lin, d_w_down, d_b_down, d_ln2_gain)
 
-    return jax.shard_map(device_step, mesh=mesh, in_specs=in_specs, out_specs=out_specs, check_vma=False)
+    return shard(device_step, mesh, in_specs, out_specs)
+
+
+def shard(step, mesh, in_specs, out_specs):
+    return jax.shard_map(step, mesh=mesh, in_specs=in_specs, out_specs=out_specs, check_vma=False)

time: 2260 us -> 2140 us (0.947)
  Pallas kernels: 516 us -> 635 us
  matrix products: 113 us -> 0 us
  local copies, waits for them, and re-layouts: 256 us -> 145 us
  waiting for transfers between devices: 1170 us -> 1140 us
    ppermute x5, waiting for transfers between devices: 261 us -> 37.4 us  [with_peer_half(): piece = lax.ppermute(piece, 'tp', SWAP)]
    reduce_scatter x5, waiting for transfers between devices: 106 us -> 240 us  [the longest x3 169 us: reduce_columns(): piece = lax.psum_scatter(grad, 'dp', scatter_dimension=0, tiled=True)]
    pallas_call x1 -> x7, Pallas kernels: 226 us -> 352 us  [the longest x2 229 us: ffn(): pl.pallas_call(functools.partial(ffn_kernel, base, chunk_size), grid=(cou...]
    dot_general x8 -> x0, matrix products: 113 us -> none  [outer(): lax.dot_general(left, right, (((0,), (0,)), ((), ())), preferred_element_...]
    gather x8 -> x2, local copies, waits for them, and re-layouts: 126 us -> 40.7 us  [rows_of(): rows = jnp.take(emb_table, jnp.where(inside, ids, 0), axis=0)]
    ppermute x13 -> x12, waiting for transfers between devices: 299 us -> 360 us  [the longest x3 221 us: run_backward(): d_peer.append(lax.ppermute(d_emb, 'tp', SWAP))]
    dot_general x2 -> x0, local copies, waits for them, and re-layouts: 41.3 us -> none  [outer(): lax.dot_general(left, right, (((0,), (0,)), ((), ())), preferred_element_...]
    scatter-add x1 -> x2, other arithmetic: 72.9 us -> 105 us  [add_rows(): return grad.at[ids.reshape(-1)].add(rows.reshape(-1, width), mode='drop')]
  transfers between devices with their start and end apart: 35 -> 34, of which waited for: 17 -> 20; matrix products, arithmetic and copies ran while one was open for 19% -> 11% of each run, Pallas kernels for 12% -> 8%
where the time goes in v2:
time: 2140 us; the launch traced here: 2130 us
  waiting for transfers between devices  1140 us (53%)
  Pallas kernels  635 us (30%)
  local copies, waits for them, and re-layouts  145 us (7%)
  other arithmetic  142 us (7%)
  blocking collectives  33.7 us (2%)
  starting transfers between devices  25.8 us (1%)
    psum x1, waiting for transfers between devices, device_step(): d_table = lax.psum(d_table, 'dp')  499 us
    pallas_call x2, Pallas kernels, ffn(): pl.pallas_call(functools.partial(ffn_kernel, base, chunk_size), grid=(cou...  229 us
    ppermute x3, waiting for transfers between devices, run_backward(): d_peer.append(lax.ppermute(d_emb, 'tp', SWAP))  221 us
    reduce_scatter x3, waiting for transfers between devices, reduce_columns(): piece = lax.psum_scatter(grad, 'dp', scatter_dimension=0, tiled=True)  169 us
    pallas_call x3, Pallas kernels, attn_backward(): pl.pallas_call(functools.partial(attn_backward_kernel, head_dim, len(extr...  137 us
    pallas_call x5, Pallas kernels, outer(): pl.pallas_call(functools.partial(outer_kernel, flip), grid=(wide // block...  123 us
    pallas_call x4, Pallas kernels, attn_forward(): pl.pallas_call(functools.partial(attn_forward_kernel, head_dim, len(extra...  116 us
    scatter-add x2, other arithmetic, add_rows(): return grad.at[ids.reshape(-1)].add(rows.reshape(-1, width), mode='drop')  105 us
  transfers between devices with their start and end apart: 34, of which 20 were waited for; matrix products, arithmetic and copies ran while one was open for 11% of the time, Pallas kernels for 8%

profile of v2, /device:TPU:0, one launch (start us, length us, event | category | flops | bytes accessed | tf_op | source)
XLA Modules:
  0.0 2134.3 jit_solution(13202704559105160189)
XLA Ops:
  62.6 15.4 gather_fusion.2
  82.2 25.3 %gather_fusion.1 = bf16[3072,768]{1,0:T(8,128)(2,1)} fusion(bf16[15296,768]{1,0:T(8,128)(2,1)} %param.18, s32[3072]{0:T(1024)S(1)} %broadcast_clamp_fusion.1), kind=kCustom, calls=%fused_computation.1 | custom fusion | bytes 9449472 | tf_op jit(solution)/shard_map/jit(_take)/gather | solution.py:490
  119.9 29.9 %gather_fusion = bf16[4096,768]{1,0:T(8,128)(2,1)} fusion(bf16[15296,768]{1,0:T(8,128)(2,1)} %param.18, s32[4096]{0:T(1024)S(1)} %broadcast_clamp_fusion), kind=kCustom, calls=%fused_computation | custom fusion | bytes 12599296 | tf_op jit(solution)/shard_map/jit(_take)/gather | solution.py:522
  177.2 29.1 %attn_forward.4 = (bf16[8,512,768]{2,1,0:T(8,128)(2,1)}, bf16[8,512,2304]{2,1,0:T(8,128)(2,1)}, bf16[8,12,768,256]{3,2,1,0:T(8,128)(2,1)}, bf16[8,512,768]{2,1,0...) custom-call(bf16[8,512,768]{2,1,0:T(8,128)(2,1)} %select_select_fusi, ...), custom_call_target="tpu_custom_call" | custom-call | flops 12884901888 | bytes 24000000 | tf_op jit(solution)/shard_map/attn_forward/pallas_call | solution.py:314
  219.0 29.2 %attn_forward.5 = (bf16[8,512,768]{2,1,0:T(8,128)(2,1)}, bf16[8,512,2304]{2,1,0:T(8,128)(2,1)}, bf16[8,12,768,256]{3,2,1,0:T(8,128)(2,1)}, bf16[8,512,768]{2,1,0...) custom-call(bf16[8,512,768]{2,1,0:T(8,128)(2,1)} %select_select_fusi, ...), custom_call_target="tpu_custom_call", output_to_operand_aliasing={{0}: (10, {}), {1}: (11, {}), {2}: (12, {}), {3}: (13, {}),... | custom-call | flops 12884901888 | bytes 24000000 | tf_op jit(solution)/shard_map/attn_forward/pallas_call | solution.py:314
  248.2 38.2 %collective-permute-done.4.refs_1_ = f32[2,512,768]{2,1,0:T(8,128)} collective-permute-done((f32[2,512,768]{2,1,0:T(8,128)}, f32[2,512,768]{2,1,0:T(8,128)}, u32[]{:S(2)}, u32[]{:S(2)}) %collective-permute-start.4) | collective-permute-done | bytes 3145760 | tf_op jit(solution)/shard_map/ppermute | solution.py:502
  286.4 29.0 %attn_forward.6 = (bf16[8,512,768]{2,1,0:T(8,128)(2,1)}, bf16[8,512,2304]{2,1,0:T(8,128)(2,1)}, bf16[8,12,768,256]{3,2,1,0:T(8,128)(2,1)}, bf16[8,512,768]{2,1,0...) custom-call(bf16[8,512,768]{2,1,0:T(8,128)(2,1)} %select_select_fusi, ...), custom_call_target="tpu_custom_call", output_to_operand_aliasing={{0}: (10, {}), {1}: (11, {}), {2}: (12, {}), {3}: (13, {}),... | custom-call | flops 12884901888 | bytes 24000000 | tf_op jit(solution)/shard_map/attn_forward/pallas_call | solution.py:314
  315.4 33.7 %collective-permute-done.refs_1_ = f32[2,512,768]{2,1,0:T(8,128)} collective-permute-done((f32[2,512,768]{2,1,0:T(8,128)}, f32[2,512,768]{2,1,0:T(8,128)}, u32[]{:S(2)}, u32[]{:S(2)}) %collective-permute-start) | collective-permute-done | bytes 3145760 | tf_op jit(solution)/shard_map/ppermute | solution.py:502
  349.0 28.9 %attn_forward.7 = (bf16[8,512,768]{2,1,0:T(8,128)(2,1)}, bf16[8,512,2304]{2,1,0:T(8,128)(2,1)}, bf16[8,12,768,256]{3,2,1,0:T(8,128)(2,1)}, bf16[8,512,768]{2,1,0...) custom-call(bf16[8,512,768]{2,1,0:T(8,128)(2,1)} %select_select_fusi, ...), custom_call_target="tpu_custom_call", output_to_operand_aliasing={{0}: (10, {}), {1}: (11, {}), {2}: (12, {}), {3}: (13, {}),... | custom-call | flops 12884901888 | bytes 24000000 | tf_op jit(solution)/shard_map/attn_forward/pallas_call | solution.py:314
  397.6 117.4 %ffn.2 = (bf16[4096,3072]{1,0:T(8,128)(2,1)}, bf16[4096,3072]{1,0:T(8,128)(2,1)}, bf16[4096,3072]{1,0:T(8,128)(2,1)}, bf16[8,512,768]{2,1,0:T(8,128)(2,1)}, f32[...) custom-call(bf16[8,512,768]{2,1,0:T(8,128)(2,1)} %get-tuple-element., ...), custom_call_target="tpu_custom_call" | custom-call | flops 86973087744 | bytes 56000000 | tf_op jit(solution)/shard_map/ffn/pallas_call | solution.py:337
  515.0 64.8 %attn_backward.3 = (f32[4,512,768]{2,1,0:T(8,128)}, bf16[8,512,2304]{2,1,0:T(8,128)(2,1)}, f32[8,512,768]{2,1,0:T(8,128)}, f32[8,2304]{1,0:T(8,128)}, f32[8,128]{1,0:T(8,128)}) custom-call(f32[8,512,768]{2,1,0:T(8,128)} %get-tuple-element.120.refs_0_.refs_4_, bf16[8,512,768]{2,1,0:T(8,128)(2,1)} %get-tuple-element.121.refs_1_.refs_5_, ...), custom_call_target="tpu_custom_call" | custom-call | flops 32212254720 | bytes 48000000 | tf_op jit(solution)/shard_map/attn_backward/pallas_call | solution.py:362
  579.8 112.1 %ffn.3 = (bf16[4096,3072]{1,0:T(8,128)(2,1)}, bf16[4096,3072]{1,0:T(8,128)(2,1)}, bf16[4096,3072]{1,0:T(8,128)(2,1)}, bf16[8,512,768]{2,1,0:T(8,128)(2,1)}, f32[...) custom-call(bf16[8,512,768]{2,1,0:T(8,128)(2,1)} %get-tuple-element., ...), custom_call_target="tpu_custom_call", output_to_operand_aliasing={{0}: (12, {}), {1}: (13, {}), {2}: (14, {}), {3}: (15, {}),... | custom-call | flops 86973087744 | bytes 56000000 | tf_op jit(solution)/shard_map/ffn/pallas_call | solution.py:337
  691.9 28.1 %outer.5 = (f32[768,3072]{1,0:T(8,128)}, f32[8,128]{1,0:T(8,128)}) custom-call(bf16[4096,768]{1,0:T(8,128)(2,1)} %bitcast.61, bf16[4096,3072]{1,0:T(8,128)(2,1)} %get-tuple-element.133.right_ref, f32[8,128]{1,0:T(8,128)} %get-tuple-element.134.refs_0_), custom_call_target="tpu_custom_call" | custom-call | flops 19327352832 | bytes 40894464 | tf_op jit(solution)/shard_map/outer/pallas_call | solution.py:398
  720.0 28.1 %outer.6 = (f32[768,3072]{1,0:T(8,128)}, f32[8,128]{1,0:T(8,128)}) custom-call(bf16[4096,768]{1,0:T(8,128)(2,1)} %bitcast.62, bf16[4096,3072]{1,0:T(8,128)(2,1)} %get-tuple-element.132.right_ref, f32[8,128]{1,0:T(8,128)} %get-tuple-element.135.refs_0_), custom_call_target="tpu_custom_call" | custom-call | flops 19327352832 | bytes 40894464 | tf_op jit(solution)/shard_map/outer/pallas_call | solution.py:398
  748.1 29.8 %outer.7 = (f32[3072,768]{1,0:T(8,128)}, f32[8,128]{1,0:T(8,128)}) custom-call(bf16[4096,768]{1,0:T(8,128)(2,1)} %bitcast.88, bf16[4096,3072]{1,0:T(8,128)(2,1)} %get-tuple-element.131.right_ref, f32[8,128]{1,0:T(8,128)} %get-tuple-element.136.refs_0_), custom_call_target="tpu_custom_call" | custom-call | flops 19327352832 | bytes 40894464 | tf_op jit(solution)/shard_map/outer/pallas_call | solution.py:398
  778.0 35.8 %attn_backward.4 = (f32[2,512,768]{2,1,0:T(8,128)}, bf16[8,512,2304]{2,1,0:T(8,128)(2,1)}, f32[8,512,768]{2,1,0:T(8,128)}, f32[8,2304]{1,0:T(8,128)}, f32[8,128]{1,0:T(8,128)}) custom-call(f32[8,512,768]{2,1,0:T(8,128)} %get-tuple-element.126.refs_0_, bf16[8,512,768]{2,1,0:T(8,128)(2,1)} %get-tuple-element.127.refs_1_, ...), custom_call_target="tpu_custom_call", output_to_operand_aliasing={{1}: (8, {}), {2}: (9, {})} | custom-call | flops 16106127360 | bytes 24000000 | tf_op jit(solution)/shard_map/attn_backward/pallas_call | solution.py:362
  813.7 36.3 %attn_backward.5 = (f32[2,512,768]{2,1,0:T(8,128)}, bf16[8,512,2304]{2,1,0:T(8,128)(2,1)}, f32[8,512,768]{2,1,0:T(8,128)}, f32[8,2304]{1,0:T(8,128)}, f32[8,128]{1,0:T(8,128)}) custom-call(f32[8,512,768]{2,1,0:T(8,128)} %get-tuple-element.126.refs_0_, bf16[8,512,768]{2,1,0:T(8,128)(2,1)} %get-tuple-element.127.refs_1_, ...), custom_call_target="tpu_custom_call", output_to_operand_aliasing={{1}: (8, {}), {2}: (9, {})} | custom-call | flops 16106127360 | bytes 24000000 | tf_op jit(solution)/shard_map/attn_backward/pallas_call | solution.py:362
  863.4 23.6 %outer.9 = (f32[768,2304]{1,0:T(8,128)}, f32[8,128]{1,0:T(8,128)}) custom-call(bf16[4096,768]{1,0:T(8,128)(2,1)} %bitcast.59, bf16[4096,2304]{1,0:T(8,128)(2,1)} %bitcast.58, f32[8,128]{1,0:T(8,128)} %get-tuple-element.149.refs_0_), custom_call_target="tpu_custom_call" | custom-call | flops 14495514624 | bytes 32243712 | tf_op jit(solution)/shard_map/outer/pallas_call | solution.py:398
  908.3 55.9 %reduce-scatter.6.cloned.1.call-done = f32[96,2304]{1,0:T(8,128)} async-done(((f32[768,2304]{1,0:T(8,128)}), f32[96,2304]{1,0:T(8,128)}) %reduce-scatter.6.cloned.1.call-update) | async-done | bytes 884752 | tf_op jit(solution)/shard_map/reduce_scatter | solution.py:452
  979.1 59.7 %reduce-scatter.14.cloned.1.call-done = f32[2,192,768]{2,1,0:T(8,128)} async-done(((f32[2,1536,768]{2,1,0:T(8,128)}), f32[2,192,768]{2,1,0:T(8,128)}) %reduce-scatter.14.cloned.1.call-update) | async-done | bytes 1179664 | tf_op jit(solution)/shard_map/reduce_scatter | solution.py:459
  1041.4 13.4 collective-permute-done.17
  1057.0 56.5 %reduce-scatter.12.cloned.1.call-done = f32[96,3072]{1,0:T(8,128)} async-done(((f32[768,3072]{1,0:T(8,128)}), f32[96,3072]{1,0:T(8,128)}) %reduce-scatter.12.cloned.1.call-update) | async-done | bytes 1179664 | tf_op jit(solution)/shard_map/reduce_scatter | solution.py:452
  1116.1 13.4 collective-permute-done.16
  1131.6 56.4 %reduce-scatter.10.cloned.1.call-done = f32[96,3072]{1,0:T(8,128)} async-done(((f32[768,3072]{1,0:T(8,128)}), f32[96,3072]{1,0:T(8,128)}) %reduce-scatter.10.cloned.1.call-update) | async-done | bytes 1179664 | tf_op jit(solution)/shard_map/reduce_scatter | solution.py:452
  1190.7 13.4 collective-permute-done.15
  1209.8 46.8 %scatter_custom_fusion = f32[15296,768]{1,0:T(8,128)} fusion(s32[4096]{0:T(1024)S(1)} %bitcast.82, f32[4096,768]{1,0:T(8,128)} %bitcast.63, f32[]{:T(128)} %constant.24.clone.1), kind=kCustom, calls=%fused_computation.5 | custom fusion | flops 3145728 | bytes 46989824 | tf_op jit(solution)/shard_map/scatter-add | solution.py:571
  1256.6 155.6 %collective-permute-done.12 = f32[2,512,768]{2,1,0:T(8,128)S(1)} collective-permute-done((f32[2,512,768]{2,1,0:T(8,128)}, f32[2,512,768]{2,1,0:T(8,128)S(1)}, u32[]{:S(2)}, u32[]{:S(2)}) %collective-permute-start.12) | collective-permute-done | bytes 3145760 | tf_op jit(solution)/shard_map/ppermute | solution.py:546
  1412.2 65.5 %collective-permute-done.11 = f32[2,512,768]{2,1,0:T(8,128)} collective-permute-done((f32[2,512,768]{2,1,0:T(8,128)}, f32[2,512,768]{2,1,0:T(8,128)}, u32[]{:S(2)}, u32[]{:S(2)}) %collective-permute-start.11) | collective-permute-done | bytes 3145760 | tf_op jit(solution)/shard_map/ppermute | solution.py:546
  1486.9 58.0 %scatter_fusion = f32[15296,768]{1,0:T(8,128)} fusion(f32[15296,768]{1,0:T(8,128)} %scatter_custom_fusion, s32[4096]{0:T(1024)S(1)} %bitcast.81, f32[4096,768]{1,0:T(8,128)} %bitcast.64), kind=kCustom, calls=%fused_computation.4 | custom fusion | flops 3145728 | bytes 37765120 | tf_op jit(solution)/shard_map/scatter-add | solution.py:571
  1547.2 33.7 %psum.15 = f32[12288]{0:T(1024)S(1)} all-reduce(f32[12288]{0:T(1024)S(1)} %pad_maximum_fusion.3), channel_id=1, replica_groups=mesh['tp'=2,'dp'=8] {'tp','dp'}, use_global_device_ids=true, to_apply=%region_7.8 | all-reduce | flops 12288 | bytes 98304 | tf_op jit(solution)/shard_map/psum | solution.py:584
  1583.0 498.8 %all-reduce.2.cloned.1.call-done = f32[15296,768]{1,0:T(8,128)} async-done(((f32[15296,768]{1,0:T(8,128)}), f32[15296,768]{1,0:T(8,128)}) %all-reduce.2.cloned.1.call-update) | async-done | bytes 46989328 | tf_op jit(solution)/shard_map/psum | solution.py:575
  2081.8 33.0 %copy.108 = f32[15296,768]{1,0:T(8,128)} copy(f32[15296,768]{1,0:T(8,128)} %all-reduce.2.cloned.1.call-done) | data formatting | bytes 93978624
  (214 shorter events, 224.7 us)
Async XLA Ops:
  7.2 159.7 %all-gather.13.cloned.1.call-start = ((), (), s32[]{:S(2)}) async-start(), calls=%async_computation.6 | async-start | bytes 1327104 | tf_op jit(solution)/shard_map/all_gather | solution.py:430
  16.0 156.4 %all-gather.11.cloned.1.call-start = ((), (), s32[]{:S(2)}) async-start(), calls=%async_computation.5 | async-start | bytes 3981312 | tf_op jit(solution)/shard_map/all_gather | solution.py:430
  17.0 11.4 collective-permute-start.1
  29.2 348.8 %all-gather.15.cloned.1.call-start = ((), (), s32[]{:S(2)}) async-start(), calls=%async_computation.7 | async-start | bytes 5308416 | tf_op jit(solution)/shard_map/all_gather | solution.py:430
  30.2 13.8 collective-permute-start.7
  44.9 338.6 %all-gather.17.cloned.1.call-start = ((), (), s32[]{:S(2)}) async-start(), calls=%async_computation.8 | async-start | bytes 5308416 | tf_op jit(solution)/shard_map/all_gather | solution.py:430
  46.0 12.9 collective-permute-start.8
  59.7 329.8 %all-gather.19.cloned.1.call-start = ((), (), s32[]{:S(2)}) async-start(), calls=%async_computation.9 | async-start | bytes 5308416 | tf_op jit(solution)/shard_map/all_gather | solution.py:430
  60.8 46.6 %collective-permute-start.9 = (f32[192,768]{1,0:T(8,128)S(1)}, f32[192,768]{1,0:T(8,128)S(1)}, u32[]{:S(2)}, u32[]{:S(2)}) collective-permute-start(f32[192,768]{1,0:T(8,128)S(1)} %dynamic-slice_convert_fusion), channel_id=1, source_target_pairs={{0,8},{8,0},{1,9},{9,1},{2,10},{10,2},{3,11},{11,3},{4,12},{12,4},... | collective-permute-start | bytes 1769480 | tf_op jit(solution)/shard_map/ppermute | solution.py:429
  79.9 97.2 %collective-permute-start.6 = (f32[2,512,768]{2,1,0:T(8,128)}, f32[2,512,768]{2,1,0:T(8,128)}, u32[]{:S(2)}, u32[]{:S(2)}) collective-permute-start(f32[2,512,768]{2,1,0:T(8,128)} %select_convert_fusion.1), channel_id=1, source_target_pairs={{0,8},{8,0},{1,9},{9,1},{2,10},{10,2},{3,11},{11,3},{4,12},{12,4},... | collective-permute-start | bytes 9437192 | tf_op jit(solution)/shard_map/ppermute | solution.py:502
  81.2 83.8 %collective-permute-start.2 = (f32[1,4224]{1,0:T(1,128)S(1)}, f32[1,4224]{1,0:T(1,128)S(1)}, u32[]{:S(2)}, u32[]{:S(2)}) collective-permute-start(f32[1,4224]{1,0:T(1,128)S(1)} %reshape.266), channel_id=1, source_target_pairs={{0,8},{8,0},{1,9},{9,1},{2,10},{10,2},{3,11},{11,3},{4,12},{12,4},... | collective-permute-start | bytes 50696 | tf_op jit(solution)/shard_map/ppermute | solution.py:494
  108.3 791.9 %reduce-scatter.8.cloned.1.call-start = ((), (), s32[]{:S(2)}) async-start(), calls=%async_computation.13 | async-start | bytes 2654208 | tf_op jit(solution)/shard_map/reduce_scatter | solution.py:459
  116.1 102.9 %collective-permute-start.5 = (f32[2,512,768]{2,1,0:T(8,128)}, f32[2,512,768]{2,1,0:T(8,128)}, u32[]{:S(2)}, u32[]{:S(2)}) collective-permute-start(f32[2,512,768]{2,1,0:T(8,128)} %get-tuple-element.168), channel_id=1, source_target_pairs={{0,8},{8,0},{1,9},{9,1},{2,10},{10,2},{3,11},{11,3},{4,12},{12,4},... | collective-permute-start | bytes 9437192 | tf_op jit(solution)/shard_map/ppermute | solution.py:502
  117.2 169.2 %collective-permute-start.4 = (f32[2,512,768]{2,1,0:T(8,128)}, f32[2,512,768]{2,1,0:T(8,128)}, u32[]{:S(2)}, u32[]{:S(2)}) collective-permute-start(f32[2,512,768]{2,1,0:T(8,128)} %get-tuple-element.169), channel_id=1, source_target_pairs={{0,8},{8,0},{1,9},{9,1},{2,10},{10,2},{3,11},{11,3},{4,12},{12,4},... | collective-permute-start | bytes 9437192 | tf_op jit(solution)/shard_map/ppermute | solution.py:502
  118.1 230.9 %collective-permute-start = (f32[2,512,768]{2,1,0:T(8,128)}, f32[2,512,768]{2,1,0:T(8,128)}, u32[]{:S(2)}, u32[]{:S(2)}) collective-permute-start(f32[2,512,768]{2,1,0:T(8,128)} %get-tuple-element.170), channel_id=1, source_target_pairs={{0,8},{8,0},{1,9},{9,1},{2,10},{10,2},{3,11},{11,3},{4,12},{12,4},... | collective-permute-start | bytes 9437192 | tf_op jit(solution)/shard_map/ppermute | solution.py:502
  863.3 100.9 %reduce-scatter.6.cloned.1.call-start = ((), (), s32[]{:S(2)}) async-start(), calls=%async_computation.11 | async-start | bytes 7962624 | tf_op jit(solution)/shard_map/reduce_scatter | solution.py:452
  887.1 151.7 %reduce-scatter.14.cloned.1.call-start = ((), (), s32[]{:S(2)}) async-start(), calls=%async_computation.19 | async-start | bytes 10616832 | tf_op jit(solution)/shard_map/reduce_scatter | solution.py:459
  887.8 225.7 %reduce-scatter.12.cloned.1.call-start = ((), (), s32[]{:S(2)}) async-start(), calls=%async_computation.17 | async-start | bytes 10616832 | tf_op jit(solution)/shard_map/reduce_scatter | solution.py:452
  888.5 299.5 %reduce-scatter.10.cloned.1.call-start = ((), (), s32[]{:S(2)}) async-start(), calls=%async_computation.15 | async-start | bytes 10616832 | tf_op jit(solution)/shard_map/reduce_scatter | solution.py:452
  889.1 693.8 %all-gather.23.cloned.1.call-start = ((), (), s32[]{:S(2)}) async-start(), calls=%async_computation.14 | async-start | bytes 1327104 | tf_op jit(solution)/shard_map/all_gather | solution.py:461
  908.2 674.7 %all-gather.21.cloned.1.call-start = ((), (), s32[]{:S(2)}) async-start(), calls=%async_computation.12 | async-start | bytes 3981312 | tf_op jit(solution)/shard_map/all_gather | solution.py:455
  965.3 11.8 collective-permute-start.13
  979.0 603.9 %all-gather.29.cloned.1.call-start = ((), (), s32[]{:S(2)}) async-start(), calls=%async_computation.20 | async-start | bytes 5308416 | tf_op jit(solution)/shard_map/all_gather | solution.py:461
  1039.9 14.9 collective-permute-start.17
  1057.0 526.0 %all-gather.27.cloned.1.call-start = ((), (), s32[]{:S(2)}) async-start(), calls=%async_computation.18 | async-start | bytes 5308416 | tf_op jit(solution)/shard_map/all_gather | solution.py:455
  1114.6 14.9 collective-permute-start.16
  1131.6 451.4 %all-gather.25.cloned.1.call-start = ((), (), s32[]{:S(2)}) async-start(), calls=%async_computation.16 | async-start | bytes 5308416 | tf_op jit(solution)/shard_map/all_gather | solution.py:455
  1189.2 14.9 collective-permute-start.15
  1206.1 875.7 %all-reduce.2.cloned.1.call-start = ((), (), s32[]{:S(2)}) async-start(), calls=%async_computation.10 | async-start | bytes 93978624 | tf_op jit(solution)/shard_map/psum | solution.py:575
  1206.1 271.6 %collective-permute-start.10 = (f32[4,512,768]{2,1,0:T(8,128)}, f32[4,512,768]{2,1,0:T(8,128)}, u32[]{:S(2)}, u32[]{:S(2)}) collective-permute-start(f32[4,512,768]{2,1,0:T(8,128)} %get-tuple-element.142), channel_id=1, source_target_pairs={{0,8},{8,0},{1,9},{9,1},{2,10},{10,2},{3,11},{11,3},{4,12},{12,4},... | collective-permute-start | bytes 18874376 | tf_op jit(solution)/shard_map/ppermute | solution.py:546
  1207.6 204.5 %collective-permute-start.12 = (f32[2,512,768]{2,1,0:T(8,128)}, f32[2,512,768]{2,1,0:T(8,128)S(1)}, u32[]{:S(2)}, u32[]{:S(2)}) collective-permute-start(f32[2,512,768]{2,1,0:T(8,128)} %get-tuple-element.144), channel_id=1, source_target_pairs={{0,8},{8,0},{1,9},{9,1},{2,10},{10,2},{3,11},{11,3},{4,12},{12,4},... | collective-permute-start | bytes 9437192 | tf_op jit(solution)/shard_map/ppermute | solution.py:546
  1208.2 269.5 %collective-permute-start.11 = (f32[2,512,768]{2,1,0:T(8,128)}, f32[2,512,768]{2,1,0:T(8,128)}, u32[]{:S(2)}, u32[]{:S(2)}) collective-permute-start(f32[2,512,768]{2,1,0:T(8,128)} %get-tuple-element.143), channel_id=1, source_target_pairs={{0,8},{8,0},{1,9},{9,1},{2,10},{10,2},{3,11},{11,3},{4,12},{12,4},... | collective-permute-start | bytes 9437192 | tf_op jit(solution)/shard_map/ppermute | solution.py:546
  (31 other events, 666.6 us)
Sparse Core Ops, SparseCore 0:
  16.1 21.4 all-gather.12
  40.0 30.0 all-gather.10
  71.9 35.0 all-gather.14
  108.7 35.0 all-gather.16
  145.4 35.0 all-gather.18
  863.5 36.6 reduce-scatter.7
  904.3 59.8 reduce-scatter.5
  967.7 71.0 reduce-scatter.13
  1042.3 71.2 reduce-scatter.11
  1116.8 71.2 reduce-scatter.9
  1189.9 20.1 all-gather.22
  1211.8 30.0 all-gather.20
  1244.3 35.0 all-gather.28
  1281.6 35.0 all-gather.26
  1319.0 35.0 all-gather.24
  1545.1 536.7 all-reduce.1

commit v3 on v2

v3 whole, which is shorter than its diff:
```python
import functools

import jax
import jax.numpy as jnp
from jax import lax
from jax.experimental import pallas as pl
from jax.experimental.pallas import tpu as pltpu
from jax.sharding import PartitionSpec as P


ALPHA = 140.0 ** 0.5
EPS = 1e-5
SHRINK = 0.1
ROPE_BASE = 10000.0
COLS, ROWS, ALL = P(None, 'tp'), P('tp'), P()
WEIGHT_SPECS = (COLS, ROWS, ROWS, ALL, ALL, ALL, COLS, ROWS, COLS, ROWS, ROWS, ALL, ALL)

F32 = jnp.float32
BF16 = jnp.bfloat16
LANES = 128
HALF_Q = 256
CHUNK = 512
FFN_CHUNK = 768
TILE = 8
PIECES = 3
VMEM_LIMIT = 66 * 1024 * 1024 - 512 * 1024
LOG2E = 1.4426950408889634
MASKED = -8e30
NT = (((1,), (1,)), ((), ()))
NN = (((1,), (0,)), ((), ()))
SWAP = ((0, 1), (1, 0))


def dot_nn(left, right):
    return lax.dot_general(left, right, NN, preferred_element_type=F32)


def dot_nt(left, right):
    return lax.dot_general(left, right, NT, preferred_element_type=F32)


def row_sums(values):
    return jnp.sum(values.reshape(-1, TILE, values.shape[1]), axis=0)


def row_mean(values):
    return jnp.mean(values, axis=-1, keepdims=True)


def col_sum(values):
    return jnp.sum(values, axis=0, keepdims=True)


def add_sums(ref, slot, values):
    ref[slot * TILE:(slot + 1) * TILE] += row_sums(values)


def full(ref):
    return ref[...]


def clear(ref):
    ref[...] = jnp.zeros_like(ref)


def normalize(values):
    centered = values - row_mean(values)
    rstd = lax.rsqrt(row_mean(centered * centered) + EPS)
    return centered * rstd, rstd


def normalize_back(d_hat, hat, rstd):
    return rstd * (d_hat - row_mean(d_hat) - hat * row_mean(d_hat * hat))


def rope(values, cos_tab, sin_tab, first_half):
    partner = jnp.where(first_half, pltpu.roll(values, 96, 1), pltpu.roll(values, 32, 1))
    return values * cos_tab + partner * sin_tab


def lane_masks():
    lane = lax.broadcasted_iota(jnp.int32, (1, LANES), 1)
    low = lane < 64
    return low, low.astype(F32).astype(BF16), (1.0 - low.astype(F32)).astype(BF16), (lane % 64) < 32


def attn_forward_kernel(head_dim, alias_count, *refs):
    (own_ref, other_ref, wqkv_ref, bqkv_ref, wo_ref, bo_ref, gain_ref, bias_ref, cos_ref, sin_ref) = refs[:10]
    (emb_ref, qkv_ref, prob_ref, ctx_ref, hat_ref, rstd_ref, hid_ref, token_ref) = refs[10 + alias_count:]
    seq_len, width = own_ref.shape
    clear(token_ref)
    emb_ref[...] = (full(own_ref).astype(F32) + full(other_ref)).astype(BF16)
    low, mask_low, mask_high, first_half = lane_masks()
    score_scale = head_dim ** -0.5 * LOG2E
    causal = lax.broadcasted_iota(jnp.int32, (HALF_Q, HALF_Q), 0) <= lax.broadcasted_iota(jnp.int32, (HALF_Q, HALF_Q), 1)
    step = 4 * 3 * head_dim

    def quad(index, carry):
        col = pl.multiple_of(index * step, step)
        pre = dot_nn(full(emb_ref), wqkv_ref[:, pl.ds(col, step)]) + bqkv_ref[:, pl.ds(col, step)]
        pre = pre.astype(BF16).astype(F32)
        for half in range(2):
            parts = [pre[:, (half * 3 + part) * LANES:(half * 3 + part + 1) * LANES] for part in range(3)]
            pair = index * 2 + half
            pair_col = pl.multiple_of(pair * LANES, LANES)
            q_pair = jnp.where(low, parts[0], parts[1])
            k_pair = pltpu.roll(jnp.where(low, parts[2], parts[0]), 64, 1)
            v_pair = jnp.where(low, parts[1], parts[2])
            q_rot = rope(q_pair, full(cos_ref), full(sin_ref), first_half).astype(BF16)
            k_rot = rope(k_pair, full(cos_ref), full(sin_ref), first_half).astype(BF16)
            qkv_ref[:, pl.ds(pair_col, LANES)] = q_rot
            qkv_ref[:, pl.ds(width + pair_col, LANES)] = k_rot
            qkv_ref[:, pl.ds(2 * width + pair_col, LANES)] = v_pair.astype(BF16)
            v_trans = v_pair.T.astype(BF16)
            ctx_rows = []
            for head in range(2):
                k_one = k_rot * (mask_low if head == 0 else mask_high)
                v_one = v_trans[head * 64:(head + 1) * 64]
                blocks = []
                for block in range(2):
                    q_block = q_rot[block * HALF_Q:(block + 1) * HALF_Q]
                    diag = jnp.where(causal, dot_nt(k_one[block * HALF_Q:(block + 1) * HALF_Q], q_block), MASKED)
                    pieces = [diag] if block == 0 else [dot_nt(k_one[:HALF_Q], q_block), diag]
                    peak = functools.reduce(jnp.maximum, [jnp.max(piece, axis=0, keepdims=True) for piece in pieces])
                    exps = [jnp.exp2((piece - peak) * score_scale) for piece in pieces]
                    total = functools.reduce(jnp.add, [col_sum(piece) for piece in exps])
                    inverse = 1.0 / total
                    ctx = None
                    for num, piece in enumerate(exps):
                        prob = (piece * inverse).astype(BF16)
                        prob_ref[pair * 2 + head, (block + num) * HALF_Q:(block + num + 1) * HALF_Q, :] = prob
                        term = dot_nn(v_one[:, num * HALF_Q:(num + 1) * HALF_Q], prob)
                        ctx = term if ctx is None else ctx + term
                    blocks.append(ctx)
                ctx_rows.append(jnp.concatenate(blocks, axis=1))
            ctx_pair = jnp.concatenate(ctx_rows, axis=0)
            ctx_ref[:, pl.ds(pair_col, LANES)] = ctx_pair.T.astype(BF16)
        return carry

    lax.fori_loop(0, wqkv_ref.shape[1] // step, quad, 0)
    attn = dot_nt(full(ctx_ref), full(wo_ref)) + full(bo_ref)
    resid = ALPHA * full(emb_ref).astype(F32) + attn
    hat, rstd = normalize(resid)
    hat_ref[...] = hat
    rstd_ref[...] = jnp.broadcast_to(rstd, (seq_len, LANES))
    hid_ref[...] = (hat * full(gain_ref) + full(bias_ref)).astype(BF16)


def ffn_kernel(base, hid_ref, cot_ref, hat_ref, rstd_ref, wg_ref, wl_ref, wd_ref, bg_ref, bl_ref, bd_ref, gain1_ref, gain2_ref,
               *refs):
    (inner_out, gate_out, lin_out, dffn_ref, dres_ref, dattn_ref, narrow_ref, wide_ref, token_ref,
     act_buf, slope_buf, inner_buf, gate_buf, lin_buf, acc_buf, sems) = refs[-16:]
    step = pl.program_id(0)
    last = pl.num_programs(0) - 1
    clear(token_ref)
    rows, _ = hid_ref.shape
    chunks = wg_ref.shape[1] // FFN_CHUNK

    def copy_out(buf, out, kind, chunk, block):
        cols = pl.ds(pl.multiple_of(chunk * FFN_CHUNK, FFN_CHUNK), FFN_CHUNK)
        return pltpu.make_async_copy(buf.at[:, cols], out.at[pl.ds((block + base) * rows, rows), cols], sems.at[kind, chunk])

    @pl.when(step == 0)
    def _():
        clear(narrow_ref)
        clear(wide_ref)

    clear(acc_buf)

    def forward(chunk, carry):
        cols = pl.ds(pl.multiple_of(chunk * FFN_CHUNK, FFN_CHUNK), FFN_CHUNK)
        gate_pre = dot_nn(full(hid_ref), wg_ref[:, cols]) + bg_ref[:, cols]
        lin_pre = dot_nn(full(hid_ref), wl_ref[:, cols]) + bl_ref[:, cols]
        cdf = 0.5 + 0.5 * lax.erf(gate_pre * (0.5 ** 0.5))
        act = gate_pre * cdf
        pdf = jnp.exp2(gate_pre * gate_pre * (-0.5 * LOG2E)) * 0.3989422804014327
        act_buf[:, cols] = act
        slope_buf[:, cols] = lin_pre * (cdf + gate_pre * pdf)

        @pl.when(step > 0)
        def _():
            copy_out(inner_buf, inner_out, 0, chunk, step - 1).wait()

        inner = (act * lin_pre).astype(BF16)
        inner_buf[:, cols] = inner
        acc_buf[...] += dot_nt(inner, wd_ref[:, cols])
        copy_out(inner_buf, inner_out, 0, chunk, step).start()
        return carry

    lax.fori_loop(0, chunks, forward, 0)
    resid = ALPHA * full(hid_ref).astype(F32) + (full(acc_buf) + full(bd_ref))
    hat, rstd = normalize(resid)
    cot = full(cot_ref).astype(F32)
    add_sums(narrow_ref, 0, cot * hat)
    d_hat = cot * full(gain2_ref)
    d_resid = normalize_back(d_hat, hat, rstd)
    add_sums(narrow_ref, 1, d_resid)
    dffn_ref[...] = d_resid.astype(BF16)
    acc_buf[...] = ALPHA * d_resid

    def backward(chunk, carry):
        cols = pl.ds(pl.multiple_of(chunk * FFN_CHUNK, FFN_CHUNK), FFN_CHUNK)
        d_inner = dot_nn(full(dffn_ref), wd_ref[:, cols]).astype(BF16).astype(F32)
        d_gate = d_inner * slope_buf[:, cols]
        d_lin = d_inner * act_buf[:, cols]
        add_sums(wide_ref.at[:, cols], 0, d_gate)
        add_sums(wide_ref.at[:, cols], 1, d_lin)

        @pl.when(step > 0)
        def _():
            copy_out(gate_buf, gate_out, 1, chunk, step - 1).wait()
            copy_out(lin_buf, lin_out, 2, chunk, step - 1).wait()

        d_gate = d_gate.astype(BF16)
        d_lin = d_lin.astype(BF16)
        gate_buf[:, cols] = d_gate
        lin_buf[:, cols] = d_lin
        acc_buf[...] += dot_nt(d_gate, wg_ref[:, cols]) + dot_nt(d_lin, wl_ref[:, cols])
        copy_out(gate_buf, gate_out, 1, chunk, step).start()
        copy_out(lin_buf, lin_out, 2, chunk, step).start()
        return carry

    lax.fori_loop(0, chunks, backward, 0)
    d_hid = full(acc_buf)
    hat = full(hat_ref)
    add_sums(narrow_ref, 2, d_hid)
    add_sums(narrow_ref, 3, d_hid * hat)
    d_hat = d_hid * full(gain1_ref)
    d_resid = normalize_back(d_hat, hat, rstd_ref[:, :1])
    add_sums(narrow_ref, 4, d_resid)
    dres_ref[...] = d_resid
    dattn_ref[...] = d_resid.astype(BF16)

    @pl.when(step == last)
    def _():
        def drain(chunk, carry):
            copy_out(inner_buf, inner_out, 0, chunk, step).wait()
            copy_out(gate_buf, gate_out, 1, chunk, step).wait()
            copy_out(lin_buf, lin_out, 2, chunk, step).wait()
            return carry

        lax.fori_loop(0, chunks, drain, 0)


def attn_backward_kernel(head_dim, alias_count, *refs):
    (dres_ref, dattn_ref, qkv_ref, prob_ref, wqkv_ref, wo_ref, cos_ref, sin_ref) = refs[:8]
    (demb_ref, dqkv_ref, dall_ref, acc_ref, token_ref) = refs[8 + alias_count:]
    clear(token_ref)
    width = dres_ref.shape[1]
    low, mask_low, mask_high, first_half = lane_masks()
    attn_scale = head_dim ** -0.5
    step = 4 * 3 * head_dim

    @pl.when(pl.program_id(0) == 0)
    def _():
        clear(acc_ref)

    def quad(index, carry):
        col = pl.multiple_of(index * step, step)
        ctx_row = pl.multiple_of(index * 4 * head_dim, 4 * head_dim)
        d_ctx_quad = dot_nn(full(dattn_ref), wo_ref[:, pl.ds(ctx_row, 4 * head_dim)]).astype(BF16)
        pieces = []
        for half in range(2):
            pair = index * 2 + half
            pair_col = pl.multiple_of(pair * LANES, LANES)
            d_ctx = d_ctx_quad[:, half * LANES:(half + 1) * LANES]
            q_rot = qkv_ref[:, pl.ds(pair_col, LANES)]
            k_rot = qkv_ref[:, pl.ds(width + pair_col, LANES)]
            v_pair = qkv_ref[:, pl.ds(2 * width + pair_col, LANES)]
            k_trans = k_rot.astype(F32).T.astype(BF16)
            dq_rows, dk_heads, dv_heads = [], [], []
            for head in range(2):
                v_one = v_pair * (mask_low if head == 0 else mask_high)
                k_one = k_trans[head * 64:(head + 1) * 64]
                d_v, d_k, d_q = [None, None], [None, None], []
                for block in range(2):
                    rows = slice(block * HALF_Q, (block + 1) * HALF_Q)
                    keys = range(block + 1)
                    probs = [prob_ref[pair * 2 + head, (block + num) * HALF_Q:(block + num + 1) * HALF_Q, :] for num in keys]
                    d_probs = [dot_nt(v_one[num * HALF_Q:(num + 1) * HALF_Q], d_ctx[rows]) for num in keys]
                    wide = [prob.astype(F32) for prob in probs]
                    inner = functools.reduce(jnp.add, [col_sum(d_prob * prob) for d_prob, prob in zip(d_probs, wide)])
                    d_q_block = None
                    for num in keys:
                        d_score = (wide[num] * (d_probs[num] - inner) * attn_scale).astype(BF16)
                        terms = (dot_nn(probs[num], d_ctx[rows]), dot_nn(d_score, q_rot[rows]), dot_nn(k_one[:, num * HALF_Q:(num + 1) * HALF_Q], d_score))
                        d_v[num] = terms[0] if d_v[num] is None else d_v[num] + terms[0]
                        d_k[num] = terms[1] if d_k[num] is None else d_k[num] + terms[1]
                        d_q_block = terms[2] if d_q_block is None else d_q_block + terms[2]
                    d_q.append(d_q_block)
                dq_rows.append(jnp.concatenate(d_q, axis=1))
                dk_heads.append(jnp.concatenate(d_k, axis=0))
                dv_heads.append(jnp.concatenate(d_v, axis=0))
            d_q = rope(jnp.concatenate(dq_rows, axis=0).T, full(cos_ref), -full(sin_ref), first_half)
            d_k = rope(jnp.where(low, dk_heads[0], dk_heads[1]), full(cos_ref), -full(sin_ref), first_half)
            d_v = jnp.where(low, dv_heads[0], dv_heads[1])
            d_k = pltpu.roll(d_k, 64, 1)
            pieces += [jnp.where(low, d_q, d_k), jnp.where(low, d_v, d_q), jnp.where(low, d_k, d_v)]
        for num, piece in enumerate(pieces):
            lanes = pl.ds(col + num * LANES, LANES)
            acc_ref[:, lanes] += row_sums(piece)
            dqkv_ref[:, lanes] = piece.astype(BF16)
        return carry

    lax.fori_loop(0, wqkv_ref.shape[1] // step, quad, 0)
    d_emb = SHRINK * (ALPHA * full(dres_ref) + dot_nt(full(dqkv_ref), full(wqkv_ref)))
    demb_ref[...] = d_emb
    dall_ref[...] = d_emb


def whole(shape):
    return pl.BlockSpec(shape, lambda i: (0,) * len(shape), pipeline_mode=pl.Buffered(1))


def per_seq(shape, base=0):
    return pl.BlockSpec((None,) + tuple(shape), lambda i: (i + base,) + (0,) * len(shape))


def cost(flops, moved):
    return pl.CostEstimate(flops=flops, bytes_accessed=moved, transcendentals=0)


def params():
    return pltpu.CompilerParams(dimension_semantics=('arbitrary',), vmem_limit_bytes=VMEM_LIMIT)


TOKEN = (8, LANES)
ANYWHERE = pl.BlockSpec(memory_space=pl.ANY)


def token_spec():
    return pl.BlockSpec(TOKEN, lambda i: (0, 0))


def attn_forward(base, count, total, own, other, weights, tables, previous, deps, head_dim):
    seq_len, width = own.shape[1:]
    wqkv = weights[0]
    heads = width // head_dim
    shapes = [((seq_len, width), BF16), ((seq_len, 3 * width), BF16), ((heads, seq_len * 3 // 2, HALF_Q), BF16), ((seq_len, width), BF16),
              ((seq_len, width), F32), ((seq_len, LANES), F32), ((seq_len, width), BF16)]
    operands = (own, other) + tuple(weights) + tuple(tables)
    specs = [per_seq((seq_len, width), base), per_seq((seq_len, width))] + [whole(item.shape) for item in operands[2:]]
    extra = tuple(previous) if previous is not None else ()
    specs += [ANYWHERE] * (len(extra) + len(deps))
    flops = count * (2 * seq_len * width * (wqkv.shape[1] + width) + 4 * heads * seq_len * seq_len * 64)
    return pl.pallas_call(
        functools.partial(attn_forward_kernel, head_dim, len(extra) + len(deps)),
        grid=(count,),
        in_specs=specs,
        out_specs=[per_seq(shape, base) for shape, _ in shapes] + [token_spec()],
        out_shape=[jax.ShapeDtypeStruct((total,) + shape, dtype) for shape, dtype in shapes] + [jax.ShapeDtypeStruct(TOKEN, F32)],
        input_output_aliases={len(operands) + num: num for num in range(len(extra))},
        compiler_params=params(),
        cost_estimate=cost(2 * flops, count * 12_000_000),
        name='attn_forward',
    )(*operands, *extra, *deps)


def ffn(base, count, hidden, cotangent, hat, rstd, weights, previous, deps):
    total, seq_len, width = hidden.shape
    wide = weights[0].shape[1]
    operands = (hidden, cotangent, hat, rstd) + tuple(weights)
    extra = tuple(previous) if previous is not None else ()
    specs = [per_seq(item.shape[1:], base) for item in operands[:4]] + [whole(item.shape) for item in operands[4:]]
    specs += [ANYWHERE] * (len(extra) + len(deps))
    big = jax.ShapeDtypeStruct((total * seq_len, wide), BF16)
    narrow = jax.ShapeDtypeStruct((total, seq_len, width), BF16)
    flops = 12 * count * seq_len * width * wide
    return pl.pallas_call(
        functools.partial(ffn_kernel, base),
        grid=(count,),
        in_specs=specs,
        out_specs=[ANYWHERE] * 3 + [per_seq((seq_len, width), base)] * 3 + [pl.BlockSpec((40, width), lambda i: (0, 0)), pl.BlockSpec((16, wide), lambda i: (0, 0)), token_spec()],
        out_shape=[big] * 3 + [narrow, jax.ShapeDtypeStruct((total, seq_len, width), F32), narrow,
                               jax.ShapeDtypeStruct((40, width), F32), jax.ShapeDtypeStruct((16, wide), F32), jax.ShapeDtypeStruct(TOKEN, F32)],
        scratch_shapes=[pltpu.VMEM((seq_len, wide), F32)] * 2 + [pltpu.VMEM((seq_len, wide), BF16)] * 3
        + [pltpu.VMEM((seq_len, width), F32), pltpu.SemaphoreType.DMA((3, wide // FFN_CHUNK))],
        input_output_aliases={len(operands) + num: num for num in range(len(extra))},
        compiler_params=params(),
        cost_estimate=cost(int(1.5 * flops), count * 14_000_000),
        name='ffn',
    )(*operands, *extra, *deps)


def attn_backward(base, count, total, d_resid, d_attn, qkv, probs, weights, tables, previous, deps, head_dim):
    seq_len, width = d_resid.shape[1:]
    wqkv, wout = weights
    heads = width // head_dim
    operands = (d_resid, d_attn, qkv, probs, wqkv, wout) + tuple(tables)
    specs = [per_seq(item.shape[1:], base) for item in operands[:4]] + [whole(item.shape) for item in operands[4:]]
    extra = tuple(previous) if previous is not None else ()
    specs += [ANYWHERE] * (len(extra) + len(deps))
    flops = count * (2 * seq_len * width * (wqkv.shape[1] + width) + 8 * heads * seq_len * seq_len * 64)
    return pl.pallas_call(
        functools.partial(attn_backward_kernel, head_dim, len(extra) + len(deps)),
        grid=(count,),
        in_specs=specs,
        out_specs=[per_seq((seq_len, width)), per_seq((seq_len, wqkv.shape[1]), base), per_seq((seq_len, width), base), pl.BlockSpec((8, wqkv.shape[1]), lambda i: (0, 0)), token_spec()],
        out_shape=[jax.ShapeDtypeStruct((count, seq_len, width), F32), jax.ShapeDtypeStruct((total, seq_len, wqkv.shape[1]), BF16),
                   jax.ShapeDtypeStruct((total, seq_len, width), F32),
                   jax.ShapeDtypeStruct((8, wqkv.shape[1]), F32), jax.ShapeDtypeStruct(TOKEN, F32)],
        input_output_aliases={len(operands) + num: 1 + num for num in range(len(extra))},
        compiler_params=params(),
        cost_estimate=cost(2 * flops, count * 12_000_000),
        name='attn_backward',
    )(*operands, *extra, *deps)


def outer_kernel(left_ref, right_ref, *refs):
    out_ref, token_ref, left_t = refs[-3:]
    clear(token_ref)

    @pl.when(pl.program_id(0) == 0)
    def _():
        def turn(index, carry):
            rows = pl.ds(pl.multiple_of(index * CHUNK, CHUNK), CHUNK)
            left_t[:, rows] = left_ref[rows, :].astype(F32).T.astype(BF16)
            return carry

        lax.fori_loop(0, left_ref.shape[0] // CHUNK, turn, 0)

    out_ref[...] = dot_nn(full(left_t), full(right_ref))


def outer(left, right, block, shape, slot, previous, deps):
    rows, width = left.shape
    wide = right.shape[1]
    per_half = wide // (2 * block)
    half_blocks = shape[1] // (2 * block)
    extra = (previous,) if previous is not None else ()
    return pl.pallas_call(
        outer_kernel,
        grid=(wide // block,),
        in_specs=[whole((rows, width)), pl.BlockSpec((rows, block), lambda i: (0, i))] + [ANYWHERE] * (len(extra) + len(deps)),
        out_specs=[pl.BlockSpec((width, block), lambda i: (0, slot + i % per_half + half_blocks * (i // per_half))), token_spec()],
        out_shape=[jax.ShapeDtypeStruct(shape, F32), jax.ShapeDtypeStruct(TOKEN, F32)],
        input_output_aliases={2 + num: num for num in range(len(extra))},
        scratch_shapes=[pltpu.VMEM((width, rows), BF16)],
        compiler_params=params(),
        cost_estimate=cost(2 * rows * width * wide, 4 * width * wide + 2 * rows * (width + wide)),
        name='outer',
    )(left, right, *extra, *deps)


def join_kernel(plain, peer_ref, *refs):
    owns, outs = refs[:len(refs) // 2], refs[len(refs) // 2:]
    start = 0
    for num, (own_ref, out_ref) in enumerate(zip(owns, outs)):
        half = out_ref.shape[1] // 2
        out_ref[:, :half] = full(own_ref) if num < plain else full(own_ref).astype(F32).T.astype(BF16)
        out_ref[:, half:] = peer_ref[:, start:start + half].astype(BF16)
        start += half


def join(peer, plain, flipped):
    owns = tuple(plain) + tuple(flipped)
    rows = peer.shape[0]
    halves = [item.shape[1] for item in plain] + [item.shape[0] for item in flipped]
    return pl.pallas_call(
        functools.partial(join_kernel, len(plain)),
        grid=(rows // LANES,),
        in_specs=[pl.BlockSpec((LANES, peer.shape[1]), lambda i: (i, 0))] + [pl.BlockSpec((LANES, item.shape[1]), lambda i: (i, 0)) for item in plain]
        + [pl.BlockSpec((item.shape[0], LANES), lambda i: (0, i)) for item in flipped],
        out_specs=[pl.BlockSpec((LANES, 2 * half), lambda i: (i, 0)) for half in halves],
        out_shape=[jax.ShapeDtypeStruct((rows, 2 * half), BF16) for half in halves],
        compiler_params=params(),
        cost_estimate=cost(peer.size * 64, peer.size * 10),
        name='join_weights',
    )(peer, *owns)


def shared_slice(plain, flipped, index, parts):
    rows = plain[0].shape[0] // parts
    pieces = [lax.dynamic_slice_in_dim(item, index * rows, rows, 0) for item in plain]
    pieces += [lax.dynamic_slice_in_dim(item, index * rows, rows, 1).T for item in flipped]
    return jnp.concatenate(pieces, axis=1).astype(F32)


def row_pieces(rows):
    tiles = rows // TILE
    cuts = [num * tiles // PIECES * TILE for num in range(PIECES + 1)]
    return [(first, last - first) for first, last in zip(cuts, cuts[1:])]


def table_kernel(src, out, away, keep, got_one, got_two, stage, load_sems, store_sems, swap_sems, one_sems, two_sems, near_sems, far_sems, back_sems):
    me = lax.axis_index('dp')
    core, col, line = me % 2, me // 2 % 2, me // 4
    partner, x_peer, y_peer = me + 1 - 2 * core, me + 2 - 4 * col, me + 4 - 8 * line
    first_peer = x_peer + core * (y_peer - x_peer)
    second_peer = y_peer + core * (x_peer - y_peer)
    one = col + core * (line - col)
    two = line + core * (col - line)
    eighth = src.shape[0] // 8
    pieces = row_pieces(eighth)
    jobs = [(part, num) for part in range(4) for num in range(PIECES)]

    barrier = pltpu.get_barrier_semaphore()
    for peer in (partner, x_peer, y_peer):
        pl.semaphore_signal(barrier, inc=1, device_id={'dp': peer}, device_id_type=pl.DeviceIdType.MESH)
    pl.semaphore_wait(barrier, 3)

    def send(source, target, sems, slot, peer):
        return pltpu.make_async_remote_copy(src_ref=source, dst_ref=target, send_sem=sems.at[0, slot], recv_sem=sems.at[1, slot],
                                            device_id={'dp': peer}, device_id_type=pl.DeviceIdType.MESH)

    def table_rows(ref, half, quarter, last, num):
        start, size = pieces[num]
        return ref.at[pl.ds(pl.multiple_of((half * 4 + quarter * 2 + last) * eighth + start, TILE), size)]

    def part_rows(ref, half, quarter, last, part, num):
        return table_rows(ref, half, 1 - quarter if part < 2 else quarter, last if part % 2 else 1 - last, num)

    def buffer_rows(ref, part, num):
        start, size = pieces[num]
        return ref.at[pl.ds(part % 2 * eighth + start, size)]

    def holder(part):
        return away if part < 2 else keep

    def add_into(target, part, source, source_part, num):
        start, size = pieces[num]
        to, of = part % 2 * eighth + start, source_part * eighth + start

        def body(index, carry):
            offset = index * TILE
            target[pl.ds(pl.multiple_of(to + offset, TILE), TILE)] += source[pl.ds(pl.multiple_of(of + offset, TILE), TILE)]
            return carry

        lax.fori_loop(0, size // TILE, body, 0)

    swaps = [send(part_rows(src, 1 - core, two, one, part, num), buffer_rows(holder(part), part, num), swap_sems, slot, partner)
             for slot, (part, num) in enumerate(jobs)]
    loads = [pltpu.make_async_copy(part_rows(src, core, one, two, part, num), stage.at[slot % 2, pl.ds(0, pieces[num][1])], load_sems.at[slot % 2])
             for slot, (part, num) in enumerate(jobs)]
    firsts = [send(buffer_rows(away, part, num), buffer_rows(got_one, part, num), one_sems, slot, first_peer)
              for slot, (part, num) in enumerate(jobs[:2 * PIECES])]
    seconds = [send(buffer_rows(keep, 0, num), buffer_rows(got_two, 0, num), two_sems, num, second_peer) for num in range(PIECES)]

    for copy in swaps:
        copy.start()
    loads[0].start()
    for slot, (part, num) in enumerate(jobs):
        if slot + 1 < len(jobs):
            loads[slot + 1].start()
        loads[slot].wait()
        swaps[slot].wait_recv()
        start, size = pieces[num]
        target, held, to = holder(part), stage.at[slot % 2], part % 2 * eighth + start

        def body(index, carry, target=target, held=held, to=to):
            offset = index * TILE
            target[pl.ds(pl.multiple_of(to + offset, TILE), TILE)] += held[pl.ds(pl.multiple_of(offset, TILE), TILE)]
            return carry

        lax.fori_loop(0, size // TILE, body, 0)
        if 0 < slot <= len(firsts):
            firsts[slot - 1].start()

    for slot in range(2 * PIECES):
        firsts[slot].wait_recv()
        add_into(keep, slot // PIECES, got_one, slot // PIECES, slot % PIECES)
        if 0 < slot <= PIECES:
            seconds[slot - 1].start()

    done = []

    def publish(num):
        mine = buffer_rows(keep, 1, num)
        place = table_rows(out, core, one, two, num)
        copies = [pltpu.make_async_copy(mine, place, store_sems.at[num]), send(mine, place, near_sems, num, second_peer),
                  send(mine, place, far_sems, num, first_peer), send(mine, place, back_sems, num, partner)]
        for copy in copies:
            copy.start()
        done.append(copies)

    for num in range(PIECES):
        seconds[num].wait_recv()
        add_into(keep, 1, got_two, 0, num)
        if num:
            publish(num - 1)
    publish(PIECES - 1)

    def forward(quarter, last, num, sems, slot, peer, start=True):
        place = table_rows(out, core, quarter, last, num)
        copy = send(place, place, sems, slot, peer)
        if start:
            copy.start()
        return copy

    relays = []
    for num in range(PIECES):
        forward(one, 1 - two, num, near_sems, num, second_peer, False).wait_recv()
        relays.append(forward(one, 1 - two, num, far_sems, PIECES + num, first_peer))
        relays.append(forward(one, 1 - two, num, back_sems, PIECES + num, partner))
        forward(1 - one, two, num, far_sems, num, first_peer, False).wait_recv()
        relays.append(forward(1 - one, two, num, back_sems, 2 * PIECES + num, partner))
    for num in range(PIECES):
        forward(1 - one, 1 - two, num, far_sems, PIECES + num, first_peer, False).wait_recv()
        relays.append(forward(1 - one, 1 - two, num, back_sems, 3 * PIECES + num, partner))
    for slot, (part, num) in enumerate(jobs):
        place = table_rows(out, 1 - core, two if part < 2 else 1 - two, 1 - one if part % 2 else one, num)
        send(place, place, back_sems, slot, partner).wait_recv()
    for copy in swaps + firsts + seconds + relays:
        copy.wait_send()
    for local, *remote in done:
        local.wait()
        for copy in remote:
            copy.wait_send()


def reduce_table(table):
    rows, width = table.shape
    eighth = rows // 8
    largest = max(size for _, size in row_pieces(eighth))
    buffers = [pltpu.VMEM((count * eighth, width), F32) for count in (2, 2, 2, 1)]
    counts = (4 * PIECES, 2 * PIECES, PIECES, PIECES, 2 * PIECES, 4 * PIECES)
    return pl.pallas_call(
        table_kernel,
        in_specs=[ANYWHERE],
        out_specs=ANYWHERE,
        out_shape=jax.ShapeDtypeStruct(table.shape, F32),
        scratch_shapes=buffers + [pltpu.VMEM((2, largest, width), F32), pltpu.SemaphoreType.DMA((2,)), pltpu.SemaphoreType.DMA((PIECES,))]
        + [pltpu.SemaphoreType.DMA((2, count)) for count in counts],
        compiler_params=pltpu.CompilerParams(collective_id=0, has_side_effects=True, vmem_limit_bytes=VMEM_LIMIT),
        cost_estimate=cost(400_000_000_000, rows * width * 8),
        name='reduce_table',
    )(table)


def reduce_gradient(grad):
    piece = lax.psum_scatter(grad, 'dp', scatter_dimension=0, tiled=True)
    half = piece.shape[1] // 2
    other = lax.ppermute(piece[:, half:], 'tp', SWAP)
    return lax.all_gather(piece[:, :half] + other, 'dp', axis=0, tiled=True)


def tie(value, token):
    return lax.optimization_barrier((value, token))[0]


def solution(mesh):
    in_specs = (P('dp'), P('dp'), ROWS) + WEIGHT_SPECS
    out_specs = (ROWS,) + WEIGHT_SPECS
    parts = mesh.shape['dp']

    def device_step(tokens, cotangent, emb_table, *weights):
        (w_qkv, b_qkv, w_out, b_out, ln1_gain, ln1_bias, w_gate, b_gate, w_lin, b_lin, w_down, b_down, ln2_gain) = weights
        tp_index, dp_index = lax.axis_index('tp'), lax.axis_index('dp')
        vocab_loc, width = emb_table.shape
        head_dim = b_qkv.shape[1] // 3
        seq_len = tokens.shape[1]
        total = tokens.shape[0] // 2

        local_ids = tokens - tp_index * vocab_loc
        in_shard = (local_ids >= 0) & (local_ids < vocab_loc)
        own_ids = lax.dynamic_slice_in_dim(local_ids, tp_index * total, total)
        own_in = lax.dynamic_slice_in_dim(in_shard, tp_index * total, total)
        peer_ids = lax.dynamic_slice_in_dim(local_ids, (1 - tp_index) * total, total)
        peer_in = lax.dynamic_slice_in_dim(in_shard, (1 - tp_index) * total, total)
        own_cot = lax.dynamic_slice_in_dim(cotangent, tp_index * total, total)

        def rows_of(ids, inside):
            rows = jnp.take(emb_table, jnp.where(inside, ids, 0), axis=0)
            return jnp.where(inside[:, :, None], rows, 0.0)

        def exchange(value):
            return lax.ppermute(value, 'tp', SWAP)

        def collect(value):
            value = exchange(value)
            return lax.all_gather(value, 'dp', axis=0, tiled=True)

        def row_of(vector):
            return vector.astype(F32).reshape(1, -1)

        size = total // 4
        qkv_loc, wide_loc = b_qkv.size, b_gate.shape[0]
        first = rows_of(peer_ids[:size], peer_in[:size]).astype(F32)
        rest = rows_of(peer_ids[size:], peer_in[size:]).astype(F32)
        own_rows = rows_of(own_ids, own_in)
        front_peer = collect(shared_slice((w_qkv,), (w_out,), dp_index, parts))
        wide_peer = collect(shared_slice((w_gate, w_lin), (w_down,), dp_index, parts))
        arrived = [exchange(first)] + [exchange(rest[num * size:(num + 1) * size]) for num in range(3)]
        own_bias = jnp.concatenate([row_of(b_qkv), row_of(b_gate), row_of(b_lin)], axis=1)
        biases = jnp.concatenate([own_bias, exchange(own_bias)])
        bqkv_full = biases[:, :qkv_loc].reshape(1, -1)
        bgate_full = biases[:, qkv_loc:qkv_loc + wide_loc].reshape(1, -1)
        blin_full = biases[:, qkv_loc + wide_loc:].reshape(1, -1)
        wqkv_full, wout_full = join(front_peer, (w_qkv,), (w_out,))
        wide_full = join(wide_peer, (w_gate, w_lin), (w_down,))

        half_dim = head_dim // 2
        inv_freq = ROPE_BASE ** (-2.0 * jnp.arange(half_dim, dtype=F32) / head_dim)
        angles = jnp.arange(seq_len, dtype=F32)[:, None] * inv_freq[None, :]
        cos_half, sin_half = jnp.cos(angles), jnp.sin(angles)
        tables = (jnp.concatenate([cos_half] * 4, axis=1), jnp.concatenate([-sin_half, sin_half] * 2, axis=1))

        front = (wqkv_full, bqkv_full, wout_full, row_of(b_out), row_of(ln1_gain), row_of(ln1_bias))
        middle = tuple(wide_full) + (bgate_full, blin_full, row_of(b_down), row_of(ln1_gain), row_of(ln2_gain))
        saved, ffn_saved, d_kept, deps = None, None, None, ()
        narrow_parts, wide_parts, bias_parts, d_peer = [], [], [], []

        def run_attention(num):
            nonlocal saved, deps
            out = attn_forward(num * size, size, total, own_rows, arrived[num], front, tables, saved, deps, head_dim)
            *kept, token = out
            saved, deps = kept, (token,)

        def run_ffn(base, count):
            nonlocal ffn_saved, deps
            *_, hat, rstd, hidden = saved
            *kept, narrow, wide, token = ffn(base, count, hidden, own_cot, hat, rstd, middle, ffn_saved, deps)
            ffn_saved, deps = kept, (token,)
            narrow_parts.append(narrow)
            wide_parts.append(wide)

        def run_backward(base, count):
            nonlocal d_kept, deps
            _, qkv, probs, *_ = saved
            *_, d_resid, d_attn = ffn_saved
            d_emb, d_qkv, d_all, bias_part, token = attn_backward(base, count, total, d_resid, d_attn, qkv, probs, (wqkv_full, wout_full), tables, d_kept, deps, head_dim)
            d_kept, deps = (d_qkv, d_all), (token,)
            bias_parts.append(bias_part)
            d_peer.append(exchange(d_emb))

        def run_outer(left, right, block, shape, slot, previous):
            nonlocal deps
            out, token = outer(left.reshape(-1, left.shape[-1]), right.reshape(-1, right.shape[-1]), block, shape, slot, previous, deps)
            deps = (token,)
            return out

        run_attention(0)
        run_attention(1)
        run_ffn(0, 2 * size)
        run_attention(2)
        run_attention(3)
        run_backward(0, 2 * size)
        run_ffn(2 * size, 2 * size)
        inner, d_gate, d_lin, d_ffn, _, d_attn = ffn_saved
        emb, _, _, context, _, _, hidden = saved
        shape = (width, 6 * wide_loc)
        step = wide_loc // CHUNK
        grads = run_outer(hidden, d_gate, CHUNK, shape, 0, None)
        grads = run_outer(hidden, d_lin, CHUNK, shape, step, grads)
        grads = run_outer(d_ffn, inner, CHUNK, shape, 2 * step, grads)
        wide_grads = reduce_gradient(grads)
        run_backward(2 * size, size)
        run_backward(3 * size, size)
        block = w_out.shape[0]
        shape = (width + parts * TILE, 2 * (qkv_loc + block))
        d_qkv, d_all = d_kept
        grads = run_outer(d_attn, context, block, shape, qkv_loc // block, None)
        grads = run_outer(emb, d_qkv, block, shape, 0, grads)

        narrow = jnp.sum(sum(narrow_parts).reshape(5, 8, -1), axis=1).reshape(1, -1)
        d_bwide = jnp.sum(sum(wide_parts).reshape(2, 8, -1), axis=1).reshape(2, 2, -1)
        small = jnp.concatenate([jnp.sum(sum(bias_parts), axis=0).reshape(2, -1), d_bwide[0], d_bwide[1], jnp.concatenate([narrow] * 2)], axis=1)
        used = small.shape[1]
        small = jnp.pad(small, ((0, 0), (0, TILE * (qkv_loc + block) - used))).reshape(2, TILE, -1)
        grads = lax.dynamic_update_slice(grads, jnp.concatenate([small[0], small[1]], axis=1), (width, 0))
        front_grads = reduce_gradient(grads)

        own_row_ids = jnp.where(own_in, own_ids, vocab_loc)
        peer_row_ids = jnp.where(peer_in, peer_ids, vocab_loc)

        def add_rows(grad, ids, rows):
            return grad.at[ids.reshape(-1)].add(rows.reshape(-1, width), mode='drop')

        d_table = add_rows(jnp.zeros((vocab_loc, width), F32), tie(own_row_ids, *deps), d_all)
        d_table = add_rows(d_table, peer_row_ids, jnp.concatenate(d_peer, axis=0))
        d_table = reduce_table(d_table)

        small = front_grads[width:width + TILE].reshape(-1)
        d_b_qkv = small[:qkv_loc].reshape(b_qkv.shape)
        d_b_gate = small[qkv_loc:qkv_loc + wide_loc]
        d_b_lin = small[qkv_loc + wide_loc:qkv_loc + 2 * wide_loc]
        d_ln2_gain, d_b_down, d_ln1_bias, d_ln1_gain, d_b_out = small[qkv_loc + 2 * wide_loc:used].reshape(5, width)
        d_w_gate, d_w_lin, d_w_down = (wide_grads[:, num * wide_loc:(num + 1) * wide_loc] for num in range(3))
        d_w_qkv, d_w_out = front_grads[:width, :qkv_loc], front_grads[:width, qkv_loc:]
        return (d_table, d_w_qkv, d_b_qkv, d_w_out.T, d_b_out, d_ln1_gain, d_ln1_bias, d_w_gate, d_b_gate, d_w_lin, d_b_lin, d_w_down.T, d_b_down, d_ln2_gain)

    return jax.shard_map(device_step, mesh=mesh, in_specs=in_specs, out_specs=out_specs, check_vma=False)
```

time: 2140 us -> 1790 us (0.84)
  waiting for transfers between devices: 1140 us -> 378 us
  Pallas kernels: 635 us -> 1070 us
  blocking collectives: 33.7 us -> 0 us
    psum x1 -> x0, waiting for transfers between devices: 499 us -> none  [device_step(): d_table = lax.psum(d_table, 'dp')]
    pallas_call x12 -> x10, Pallas kernels: 382 us -> 824 us  [the longest x1 453 us: reduce_table(): pl.pallas_call(table_kernel, in_specs=[ANYWHERE], out_specs=ANYWHERE, out...]
    ppermute x18 -> x12, waiting for transfers between devices: 398 us -> 153 us  [the longest x10 138 us: exchange(): return lax.ppermute(value, 'tp', SWAP)]
    psum x1 -> x0, blocking collectives: 33.7 us -> none  [device_step(): flat = lax.psum(flat, ('tp', 'dp'))]
    gather x2 -> x3, local copies, waits for them, and re-layouts: 40.7 us -> 72.5 us  [rows_of(): rows = jnp.take(emb_table, jnp.where(inside, ids, 0), axis=0)]
    gather x1 -> x0, local copies, waits for them, and re-layouts: 29.9 us -> none  [device_step(): jnp.take(emb_table, jnp.where(own_in, own_ids, 0), axis=0)]
    reduce_scatter x5 -> x2, waiting for transfers between devices: 240 us -> 225 us  [reduce_gradient(): piece = lax.psum_scatter(grad, 'dp', scatter_dimension=0, tiled=True)]
    unnamed x73 -> x45, local copies, waits for them, and re-layouts: 52.6 us -> 44.9 us
  transfers between devices with their start and end apart: 34 -> 18, of which waited for: 20 -> 8; matrix products, arithmetic and copies ran while one was open for 11% -> 13% of each run, Pallas kernels for 8% -> 38%
where the time goes in v3:
time: 1790 us; the launch traced here: 1780 us
  Pallas kernels  1070 us (60%)
  waiting for transfers between devices  378 us (21%)
  local copies, waits for them, and re-layouts  160 us (9%)
  other arithmetic  137 us (8%)
    pallas_call x1, Pallas kernels, reduce_table(): pl.pallas_call(table_kernel, in_specs=[ANYWHERE], out_specs=ANYWHERE, out...  453 us
    pallas_call x2, Pallas kernels, ffn(): pl.pallas_call(functools.partial(ffn_kernel, base), grid=(count,), in_spe...  226 us
    reduce_scatter x2, waiting for transfers between devices, reduce_gradient(): piece = lax.psum_scatter(grad, 'dp', scatter_dimension=0, tiled=True)  225 us
    ppermute x10, waiting for transfers between devices, exchange(): return lax.ppermute(value, 'tp', SWAP)  138 us
    pallas_call x3, Pallas kernels, attn_backward(): pl.pallas_call(functools.partial(attn_backward_kernel, head_dim, len(extr...  134 us
    pallas_call x5, Pallas kernels, outer(): pl.pallas_call(outer_kernel, grid=(wide // block,), in_specs=[whole((rows...  127 us
    pallas_call x4, Pallas kernels, attn_forward(): pl.pallas_call(functools.partial(attn_forward_kernel, head_dim, len(extra...  116 us
    scatter-add x2, other arithmetic, add_rows(): return grad.at[ids.reshape(-1)].add(rows.reshape(-1, width), mode='drop')  105 us
  transfers between devices with their start and end apart: 18, of which 8 were waited for; matrix products, arithmetic and copies ran while one was open for 13% of the time, Pallas kernels for 38%

profile of v3, /device:TPU:0, one launch (start us, length us, event | category | flops | bytes accessed | tf_op | source)
XLA Modules:
  0.0 1781.7 jit_solution(10449449506746321176)
XLA Ops:
  12.8 13.3 collective-permute-done.1
  31.5 38.0 %collective-permute-done.6 = f32[96,4608]{1,0:T(8,128)S(1)} collective-permute-done((f32[96,4608]{1,0:T(8,128)S(1)}, f32[96,4608]{1,0:T(8,128)S(1)}, u32[]{:S(2)}, u32[]{:S(2)}) %collective-permute-start.6) | collective-permute-done | bytes 1769504 | tf_op jit(solution)/shard_map/ppermute | solution.py:667
  72.5 17.1 gather_fusion.2
  91.7 25.3 %gather_fusion.1 = bf16[3072,768]{1,0:T(8,128)(2,1)} fusion(bf16[15296,768]{1,0:T(8,128)(2,1)} %param.18, s32[3072]{0:T(1024)S(1)} %broadcast_clamp_fusion.1), kind=kCustom, calls=%fused_computation.1 | custom fusion | bytes 9449472 | tf_op jit(solution)/shard_map/jit(_take)/gather | solution.py:663
  129.2 30.1 %gather_fusion = bf16[4096,768]{1,0:T(8,128)(2,1)} fusion(bf16[15296,768]{1,0:T(8,128)(2,1)} %param.18, s32[4096]{0:T(1024)S(1)} %broadcast_clamp_fusion), kind=kCustom, calls=%fused_computation | custom fusion | bytes 12599296 | tf_op jit(solution)/shard_map/jit(_take)/gather | solution.py:663
  176.0 6.4 join_weights.2
  182.4 29.2 %attn_forward.4 = (bf16[8,512,768]{2,1,0:T(8,128)(2,1)}, bf16[8,512,2304]{2,1,0:T(8,128)(2,1)}, bf16[8,12,768,256]{3,2,1,0:T(8,128)(2,1)}, bf16[8,512,768]{2,1,0...) custom-call(bf16[8,512,768]{2,1,0:T(8,128)(2,1)} %select_select_fusi, ...), custom_call_target="tpu_custom_call" | custom-call | flops 12884901888 | bytes 24000000 | tf_op jit(solution)/shard_map/attn_forward/pallas_call | solution.py:346
  211.6 18.8 %collective-permute-done.4.refs_1_ = f32[2,512,768]{2,1,0:T(8,128)} collective-permute-done((f32[2,512,768]{2,1,0:T(8,128)}, f32[2,512,768]{2,1,0:T(8,128)}, u32[]{:S(2)}, u32[]{:S(2)}) %collective-permute-start.4) | collective-permute-done | bytes 3145760 | tf_op jit(solution)/shard_map/ppermute | solution.py:667
  230.3 29.0 %attn_forward.5 = (bf16[8,512,768]{2,1,0:T(8,128)(2,1)}, bf16[8,512,2304]{2,1,0:T(8,128)(2,1)}, bf16[8,12,768,256]{3,2,1,0:T(8,128)(2,1)}, bf16[8,512,768]{2,1,0...) custom-call(bf16[8,512,768]{2,1,0:T(8,128)(2,1)} %select_select_fusi, ...), custom_call_target="tpu_custom_call", output_to_operand_aliasing={{0}: (10, {}), {1}: (11, {}), {2}: (12, {}), {3}: (13, {}),... | custom-call | flops 12884901888 | bytes 24000000 | tf_op jit(solution)/shard_map/attn_forward/pallas_call | solution.py:346
  259.4 12.4 join_weights.3
  271.8 112.9 %ffn.2 = (bf16[4096,3072]{1,0:T(8,128)(2,1)}, bf16[4096,3072]{1,0:T(8,128)(2,1)}, bf16[4096,3072]{1,0:T(8,128)(2,1)}, bf16[8,512,768]{2,1,0:T(8,128)(2,1)}, f32[...) custom-call(bf16[8,512,768]{2,1,0:T(8,128)(2,1)} %get-tuple-element., ...), custom_call_target="tpu_custom_call" | custom-call | flops 86973087744 | bytes 56000000 | tf_op jit(solution)/shard_map/ffn/pallas_call | solution.py:369
  384.7 29.0 %attn_forward.6 = (bf16[8,512,768]{2,1,0:T(8,128)(2,1)}, bf16[8,512,2304]{2,1,0:T(8,128)(2,1)}, bf16[8,12,768,256]{3,2,1,0:T(8,128)(2,1)}, bf16[8,512,768]{2,1,0...) custom-call(bf16[8,512,768]{2,1,0:T(8,128)(2,1)} %select_select_fusi, ...), custom_call_target="tpu_custom_call", output_to_operand_aliasing={{0}: (10, {}), {1}: (11, {}), {2}: (12, {}), {3}: (13, {}),... | custom-call | flops 12884901888 | bytes 24000000 | tf_op jit(solution)/shard_map/attn_forward/pallas_call | solution.py:346
  413.8 29.2 %attn_forward.7 = (bf16[8,512,768]{2,1,0:T(8,128)(2,1)}, bf16[8,512,2304]{2,1,0:T(8,128)(2,1)}, bf16[8,12,768,256]{3,2,1,0:T(8,128)(2,1)}, bf16[8,512,768]{2,1,0...) custom-call(bf16[8,512,768]{2,1,0:T(8,128)(2,1)} %select_select_fusi, ...), custom_call_target="tpu_custom_call", output_to_operand_aliasing={{0}: (10, {}), {1}: (11, {}), {2}: (12, {}), {3}: (13, {}),... | custom-call | flops 12884901888 | bytes 24000000 | tf_op jit(solution)/shard_map/attn_forward/pallas_call | solution.py:346
  442.9 63.6 %attn_backward.3 = (f32[4,512,768]{2,1,0:T(8,128)}, bf16[8,512,2304]{2,1,0:T(8,128)(2,1)}, f32[8,512,768]{2,1,0:T(8,128)}, f32[8,2304]{1,0:T(8,128)}, f32[8,128]{1,0:T(8,128)}) custom-call(f32[8,512,768]{2,1,0:T(8,128)} %get-tuple-element.130.refs_0_.refs_4_, bf16[8,512,768]{2,1,0:T(8,128)(2,1)} %get-tuple-element.131.refs_1_.refs_5_, ...), custom_call_target="tpu_custom_call" | custom-call | flops 32212254720 | bytes 48000000 | tf_op jit(solution)/shard_map/attn_backward/pallas_call | solution.py:394
  506.5 112.6 %ffn.3 = (bf16[4096,3072]{1,0:T(8,128)(2,1)}, bf16[4096,3072]{1,0:T(8,128)(2,1)}, bf16[4096,3072]{1,0:T(8,128)(2,1)}, bf16[8,512,768]{2,1,0:T(8,128)(2,1)}, f32[...) custom-call(bf16[8,512,768]{2,1,0:T(8,128)(2,1)} %get-tuple-element., ...), custom_call_target="tpu_custom_call", output_to_operand_aliasing={{0}: (12, {}), {1}: (13, {}), {2}: (14, {}), {3}: (15, {}),... | custom-call | flops 86973087744 | bytes 56000000 | tf_op jit(solution)/shard_map/ffn/pallas_call | solution.py:369
  623.1 28.1 %outer.5 = (f32[768,9216]{1,0:T(8,128)}, f32[8,128]{1,0:T(8,128)}) custom-call(bf16[4096,768]{1,0:T(8,128)(2,1)} %bitcast.56, bf16[4096,3072]{1,0:T(8,128)(2,1)} %get-tuple-element.143.right_ref, f32[8,128]{1,0:T(8,128)} %get-tuple-element.144.refs_0_), custom_call_target="tpu_custom_call" | custom-call | flops 19327352832 | bytes 40894464 | tf_op jit(solution)/shard_map/outer/pallas_call | solution.py:431
  651.3 28.2 %outer.6 = (f32[768,9216]{1,0:T(8,128)}, f32[8,128]{1,0:T(8,128)}) custom-call(bf16[4096,768]{1,0:T(8,128)(2,1)} %bitcast.57, bf16[4096,3072]{1,0:T(8,128)(2,1)} %get-tuple-element.142.right_ref, f32[768,9216]{1,0:T(8,128)} %get-tuple-element.145.refs_0_, f32[8,128]{1,0:T(8,128)} %get-tuple-element.146.refs_1_), custom_call_target="tpu_custom_call", output_to_operand_aliasing={{0}: (2, {})} | custom-call | flops 19327352832 | bytes 40894464 | tf_op jit(solution)/shard_map/outer/pallas_call | solution.py:431
  679.5 28.7 %outer.7 = (f32[768,9216]{1,0:T(8,128)}, f32[8,128]{1,0:T(8,128)}) custom-call(bf16[4096,768]{1,0:T(8,128)(2,1)} %bitcast.85, bf16[4096,3072]{1,0:T(8,128)(2,1)} %get-tuple-element.141.right_ref, f32[768,9216]{1,0:T(8,128)} %get-tuple-element.147.refs_0_, f32[8,128]{1,0:T(8,128)} %get-tuple-element.148.refs_1_), custom_call_target="tpu_custom_call", output_to_operand_aliasing={{0}: (2, {})} | custom-call | flops 19327352832 | bytes 40894464 | tf_op jit(solution)/shard_map/outer/pallas_call | solution.py:431
  708.2 35.4 %attn_backward.4 = (f32[2,512,768]{2,1,0:T(8,128)}, bf16[8,512,2304]{2,1,0:T(8,128)(2,1)}, f32[8,512,768]{2,1,0:T(8,128)}, f32[8,2304]{1,0:T(8,128)}, f32[8,128]{1,0:T(8,128)}) custom-call(f32[8,512,768]{2,1,0:T(8,128)} %get-tuple-element.136.refs_0_, bf16[8,512,768]{2,1,0:T(8,128)(2,1)} %get-tuple-element.137.refs_1_, ...), custom_call_target="tpu_custom_call", output_to_operand_aliasing={{1}: (8, {}), {2}: (9, {})} | custom-call | flops 16106127360 | bytes 24000000 | tf_op jit(solution)/shard_map/attn_backward/pallas_call | solution.py:394
  743.5 35.5 %attn_backward.5 = (f32[2,512,768]{2,1,0:T(8,128)}, bf16[8,512,2304]{2,1,0:T(8,128)(2,1)}, f32[8,512,768]{2,1,0:T(8,128)}, f32[8,2304]{1,0:T(8,128)}, f32[8,128]{1,0:T(8,128)}) custom-call(f32[8,512,768]{2,1,0:T(8,128)} %get-tuple-element.136.refs_0_, bf16[8,512,768]{2,1,0:T(8,128)(2,1)} %get-tuple-element.137.refs_1_, ...), custom_call_target="tpu_custom_call", output_to_operand_aliasing={{1}: (8, {}), {2}: (9, {})} | custom-call | flops 16106127360 | bytes 24000000 | tf_op jit(solution)/shard_map/attn_backward/pallas_call | solution.py:394
  782.4 13.9 outer.8
  796.2 27.6 %outer.9 = (f32[832,3072]{1,0:T(8,128)}, f32[8,128]{1,0:T(8,128)}) custom-call(bf16[4096,768]{1,0:T(8,128)(2,1)} %bitcast.54, bf16[4096,2304]{1,0:T(8,128)(2,1)} %bitcast.53, f32[832,3072]{1,0:T(8,128)} %get-tuple-element.161.refs_0_, f32[8,128]{1,0:T(8,128)} %get-tuple-element.162.refs_1_), custom_call_target="tpu_custom_call", output_to_operand_aliasing={{0}: (2, {})} | custom-call | flops 14495514624 | bytes 32243712 | tf_op jit(solution)/shard_map/outer/pallas_call | solution.py:431
  826.0 74.2 %reduce-scatter.3.cloned.1.call-done = f32[104,3072]{1,0:T(8,128)} async-done(((f32[832,3072]{1,0:T(8,128)}), f32[104,3072]{1,0:T(8,128)}) %reduce-scatter.3.cloned.1.call-update) | async-done | bytes 1277968 | tf_op jit(solution)/shard_map/reduce_scatter | solution.py:631
  902.8 14.5 collective-permute-done.10
  923.1 150.5 %reduce-scatter.5.cloned.1.call-done = f32[96,9216]{1,0:T(8,128)} async-done(((f32[768,9216]{1,0:T(8,128)}), f32[96,9216]{1,0:T(8,128)}) %reduce-scatter.5.cloned.1.call-update) | async-done | bytes 3538960 | tf_op jit(solution)/shard_map/reduce_scatter | solution.py:631
  1077.9 46.9 %scatter_custom_fusion = f32[15296,768]{1,0:T(8,128)} fusion(s32[4096]{0:T(1024)S(1)} %bitcast.79, f32[4096,768]{1,0:T(8,128)} %bitcast.58, f32[]{:T(128)} %constant.31.clone.1), kind=kCustom, calls=%fused_computation.5 | custom fusion | flops 3145728 | bytes 46989824 | tf_op jit(solution)/shard_map/scatter-add | solution.py:767
  1125.5 67.5 %collective-permute-done.8 = f32[2,512,768]{2,1,0:T(8,128)} collective-permute-done((f32[2,512,768]{2,1,0:T(8,128)}, f32[2,512,768]{2,1,0:T(8,128)}, u32[]{:S(2)}, u32[]{:S(2)}) %collective-permute-start.8) | collective-permute-done | bytes 3145760 | tf_op jit(solution)/shard_map/ppermute | solution.py:667
  1193.0 9.2 pad_maximum_fusion
  1202.3 58.1 %scatter_fusion = f32[15296,768]{1,0:T(8,128)} fusion(f32[15296,768]{1,0:T(8,128)} %scatter_custom_fusion, s32[4096]{0:T(1024)S(1)} %bitcast.77, f32[4096,768]{1,0:T(8,128)} %bitcast.59), kind=kCustom, calls=%fused_computation.4 | custom fusion | flops 3145728 | bytes 37765120 | tf_op jit(solution)/shard_map/scatter-add | solution.py:767
  1263.2 452.6 %reduce_table.1 = f32[15296,768]{1,0:T(8,128)} custom-call(f32[15296,768]{1,0:T(8,128)} %scatter_fusion), custom_call_target="tpu_custom_call" | custom-call | flops 399999991808 | bytes 93978624 | tf_op jit(solution)/shard_map/reduce_table/pallas_call | solution.py:617
  1725.4 10.6 slice_bitcast_fusion
  1742.0 32.6 %copy.115 = f32[15296,768]{1,0:T(8,128)} copy(f32[15296,768]{1,0:T(8,128)} %reduce_table.1) | data formatting | bytes 93978624
  (141 shorter events, 85.9 us)
Async XLA Ops:
  7.2 63.6 %copy-start.6 = (bf16[6,192]{1,0:T(8,128)(2,1)S(1)}, bf16[6,192]{1,0:T(8,128)(2,1)}, u32[]{:S(2)}) copy-start(bf16[6,192]{1,0:T(8,128)(2,1)} %param.20) | copy-start | bytes 6916
  7.2 63.7 %copy-start.7 = (bf16[1536]{0:T(1024)(128)(2,1)S(1)}, bf16[1536]{0:T(1024)(128)(2,1)}, u32[]{:S(2)}) copy-start(bf16[1536]{0:T(1024)(128)(2,1)} %param.26) | copy-start | bytes 9220
  7.2 63.7 %copy-start.8 = (bf16[1536]{0:T(1024)(128)(2,1)S(1)}, bf16[1536]{0:T(1024)(128)(2,1)}, u32[]{:S(2)}) copy-start(bf16[1536]{0:T(1024)(128)(2,1)} %param.28) | copy-start | bytes 9220
  7.2 65.3 %copy-start.5 = (s32[16,512]{1,0:T(8,128)S(1)}, s32[16,512]{1,0:T(8,128)}, u32[]{:S(2)}) copy-start(s32[16,512]{1,0:T(8,128)} %param.16) | copy-start | bytes 98308
  7.2 168.7 %all-gather.5.cloned.1.call-start = ((), (), s32[]{:S(2)}) async-start(), calls=%async_computation.2 | async-start | bytes 5308416 | tf_op jit(solution)/shard_map/all_gather | solution.py:671
  9.4 16.6 collective-permute-start.1
  26.9 232.4 %all-gather.7.cloned.1.call-start = ((), (), s32[]{:S(2)}) async-start(), calls=%async_computation.3 | async-start | bytes 15925248 | tf_op jit(solution)/shard_map/all_gather | solution.py:671
  29.7 39.8 %collective-permute-start.6 = (f32[96,4608]{1,0:T(8,128)S(1)}, f32[96,4608]{1,0:T(8,128)S(1)}, u32[]{:S(2)}, u32[]{:S(2)}) collective-permute-start(f32[96,4608]{1,0:T(8,128)S(1)} %maximum_convert_fusion), channel_id=1, source_target_pairs={{0,8},{8,0},{1,9},{9,1},{2,10},{10,2},{3,11},{11,3},{4,12},{12,4},... | collective-permute-start | bytes 5308424 | tf_op jit(solution)/shard_map/ppermute | solution.py:667
  70.8 829.4 %reduce-scatter.3.cloned.1.call-start = ((), (), s32[]{:S(2)}) async-start(), calls=%async_computation.4 | async-start | bytes 11501568 | tf_op jit(solution)/shard_map/reduce_scatter | solution.py:631
  71.0 103.1 %collective-permute-start.2 = (f32[1,4224]{1,0:T(1,128)S(1)}, f32[1,4224]{1,0:T(1,128)S(1)}, u32[]{:S(2)}, u32[]{:S(2)}) collective-permute-start(f32[1,4224]{1,0:T(1,128)S(1)} %maximum_convert_fusion.2), channel_id=1, source_target_pairs={{0,8},{8,0},{1,9},{9,1},{2,10},{10,2},{3,11},{11,3},{4,12},{12,4},... | collective-permute-start | bytes 50696 | tf_op jit(solution)/shard_map/ppermute | solution.py:667
  91.6 90.7 %collective-permute-start.5 = (f32[2,512,768]{2,1,0:T(8,128)}, f32[2,512,768]{2,1,0:T(8,128)}, u32[]{:S(2)}, u32[]{:S(2)}) collective-permute-start(f32[2,512,768]{2,1,0:T(8,128)} %select_convert_fusion.1), channel_id=1, source_target_pairs={{0,8},{8,0},{1,9},{9,1},{2,10},{10,2},{3,11},{11,3},{4,12},{12,4},... | collective-permute-start | bytes 9437192 | tf_op jit(solution)/shard_map/ppermute | solution.py:667
  124.5 105.8 %collective-permute-start.4 = (f32[2,512,768]{2,1,0:T(8,128)}, f32[2,512,768]{2,1,0:T(8,128)}, u32[]{:S(2)}, u32[]{:S(2)}) collective-permute-start(f32[2,512,768]{2,1,0:T(8,128)} %get-tuple-element.197), channel_id=1, source_target_pairs={{0,8},{8,0},{1,9},{9,1},{2,10},{10,2},{3,11},{11,3},{4,12},{12,4},... | collective-permute-start | bytes 9437192 | tf_op jit(solution)/shard_map/ppermute | solution.py:667
  126.5 258.2 %collective-permute-start.3 = (f32[2,512,768]{2,1,0:T(8,128)}, f32[2,512,768]{2,1,0:T(8,128)}, u32[]{:S(2)}, u32[]{:S(2)}) collective-permute-start(f32[2,512,768]{2,1,0:T(8,128)} %get-tuple-element.198), channel_id=1, source_target_pairs={{0,8},{8,0},{1,9},{9,1},{2,10},{10,2},{3,11},{11,3},{4,12},{12,4},... | collective-permute-start | bytes 9437192 | tf_op jit(solution)/shard_map/ppermute | solution.py:667
  126.5 287.2 %collective-permute-start = (f32[2,512,768]{2,1,0:T(8,128)}, f32[2,512,768]{2,1,0:T(8,128)}, u32[]{:S(2)}, u32[]{:S(2)}) collective-permute-start(f32[2,512,768]{2,1,0:T(8,128)} %get-tuple-element.199), channel_id=1, source_target_pairs={{0,8},{8,0},{1,9},{9,1},{2,10},{10,2},{3,11},{11,3},{4,12},{12,4},... | collective-permute-start | bytes 9437192 | tf_op jit(solution)/shard_map/ppermute | solution.py:667
  159.2 7.1 slice-start
  160.2 6.1 slice-start.1
  166.3 4.8 copy-start.9
  166.3 5.4 copy-start.10
  166.3 6.0 copy-start.11
  166.4 6.6 copy-start.12
  166.4 7.1 copy-start.13
  825.4 248.2 %reduce-scatter.5.cloned.1.call-start = ((), (), s32[]{:S(2)}) async-start(), calls=%async_computation.6 | async-start | bytes 31850496 | tf_op jit(solution)/shard_map/reduce_scatter | solution.py:631
  825.4 97.6 %copy-start.4 = (s32[1,1,8,512]{3,2,1,0:T(8,128)S(1)}, s32[1,1,8,512]{3,2,1,0:T(8,128)}, u32[]{:S(2)}) copy-start(s32[1,1,8,512]{3,2,1,0:T(8,128)} %get-tuple-element.207) | copy-start | bytes 49156
  825.9 251.9 %copy-start.3 = (s32[8,512]{1,0:T(8,128)S(1)}, s32[8,512]{1,0:T(8,128)}, u32[]{:S(2)}) copy-start(s32[8,512]{1,0:T(8,128)} %get-tuple-element.209) | copy-start | bytes 49156
  825.9 890.0 %all-gather.9.cloned.1.call-start = ((), (), s32[]{:S(2)}) async-start(), calls=%async_computation.5 | async-start | bytes 5750784 | tf_op jit(solution)/shard_map/all_gather | solution.py:634
  901.3 16.0 collective-permute-start.10
  919.4 806.0 %all-gather.11.cloned.1.call-start = ((), (), s32[]{:S(2)}) async-start(), calls=%async_computation.7 | async-start | bytes 15925248 | tf_op jit(solution)/shard_map/all_gather | solution.py:634
  919.5 273.6 %collective-permute-start.7 = (f32[4,512,768]{2,1,0:T(8,128)}, f32[4,512,768]{2,1,0:T(8,128)}, u32[]{:S(2)}, u32[]{:S(2)}) collective-permute-start(f32[4,512,768]{2,1,0:T(8,128)} %get-tuple-element.154), channel_id=1, source_target_pairs={{0,8},{8,0},{1,9},{9,1},{2,10},{10,2},{3,11},{11,3},{4,12},{12,4},... | collective-permute-start | bytes 18874376 | tf_op jit(solution)/shard_map/ppermute | solution.py:667
  921.0 204.5 %collective-permute-start.9 = (f32[2,512,768]{2,1,0:T(8,128)}, f32[2,512,768]{2,1,0:T(8,128)S(1)}, u32[]{:S(2)}, u32[]{:S(2)}) collective-permute-start(f32[2,512,768]{2,1,0:T(8,128)} %get-tuple-element.156), channel_id=1, source_target_pairs={{0,8},{8,0},{1,9},{9,1},{2,10},{10,2},{3,11},{11,3},{4,12},{12,4},... | collective-permute-start | bytes 9437192 | tf_op jit(solution)/shard_map/ppermute | solution.py:667
  921.5 271.5 %collective-permute-start.8 = (f32[2,512,768]{2,1,0:T(8,128)}, f32[2,512,768]{2,1,0:T(8,128)}, u32[]{:S(2)}, u32[]{:S(2)}) collective-permute-start(f32[2,512,768]{2,1,0:T(8,128)} %get-tuple-element.155), channel_id=1, source_target_pairs={{0,8},{8,0},{1,9},{9,1},{2,10},{10,2},{3,11},{11,3},{4,12},{12,4},... | collective-permute-start | bytes 9437192 | tf_op jit(solution)/shard_map/ppermute | solution.py:667
  1076.4 184.0 %collective-permute-start.11 = (f32[96,4608]{1,0:T(8,128)}, f32[96,4608]{1,0:T(8,128)}, u32[]{:S(2)}, u32[]{:S(2)}) collective-permute-start(f32[96,4608]{1,0:T(8,128)} %slice.147), channel_id=1, source_target_pairs={{0,8},{8,0},{1,9},{9,1},{2,10},{10,2},{3,11},{11,3},{4,12},{12,4},... | collective-permute-start | bytes 5308424 | tf_op jit(solution)/shard_map/ppermute | solution.py:633
  1202.3 58.1 %copy-start = (f32[96,9216]{1,0:T(8,128)S(1)}, f32[96,9216]{1,0:T(8,128)}, u32[]{:S(2)}) copy-start(f32[96,9216]{1,0:T(8,128)} %reduce-scatter.5.cloned.1.call-done) | copy-start | bytes 10616836
  (2 other events, 2.0 us)
Sparse Core Ops, SparseCore 0:
  27.0 36.2 all-gather.4
  70.9 75.6 all-gather.6
  825.5 74.6 reduce-scatter.2
  903.7 169.8 reduce-scatter.4
  1075.8 36.6 all-gather.8
  1263.4 103.4 all-gather.10

commit v4 on v3

--- a/solution.py
+++ b/solution.py
@@ -165,6 +165,20 @@
         clear(narrow_ref)
         clear(wide_ref)
 
+    outputs = ((inner_buf, inner_out, 0), (gate_buf, gate_out, 1), (lin_buf, lin_out, 2))
+
+    def drain(copies, block):
+        def body(chunk, carry):
+            for buf, out, kind in copies:
+                copy_out(buf, out, kind, chunk, block).wait()
+            return carry
+
+        lax.fori_loop(0, chunks, body, 0)
+
+    @pl.when(step > 0)
+    def _():
+        drain(outputs, step - 1)
+
     clear(acc_buf)
 
     def forward(chunk, carry):
@@ -176,10 +190,6 @@
         pdf = jnp.exp2(gate_pre * gate_pre * (-0.5 * LOG2E)) * 0.3989422804014327
         act_buf[:, cols] = act
         slope_buf[:, cols] = lin_pre * (cdf + gate_pre * pdf)
-
-        @pl.when(step > 0)
-        def _():
-            copy_out(inner_buf, inner_out, 0, chunk, step - 1).wait()
 
         inner = (act * lin_pre).astype(BF16)
         inner_buf[:, cols] = inner
@@ -206,11 +216,6 @@
         add_sums(wide_ref.at[:, cols], 0, d_gate)
         add_sums(wide_ref.at[:, cols], 1, d_lin)
 
-        @pl.when(step > 0)
-        def _():
-            copy_out(gate_buf, gate_out, 1, chunk, step - 1).wait()
-            copy_out(lin_buf, lin_out, 2, chunk, step - 1).wait()
-
         d_gate = d_gate.astype(BF16)
         d_lin = d_lin.astype(BF16)
         gate_buf[:, cols] = d_gate
@@ -233,13 +238,7 @@
 
     @pl.when(step == last)
     def _():
-        def drain(chunk, carry):
-            copy_out(inner_buf, inner_out, 0, chunk, step).wait()
-            copy_out(gate_buf, gate_out, 1, chunk, step).wait()
-            copy_out(lin_buf, lin_out, 2, chunk, step).wait()
-            return carry
-
-        lax.fori_loop(0, chunks, drain, 0)
+        drain(outputs, step)
 
 
 def attn_backward_kernel(head_dim, alias_count, *refs):
@@ -332,14 +331,14 @@
     return pl.BlockSpec(TOKEN, lambda i: (0, 0))
 
 
-def attn_forward(base, count, total, own, other, weights, tables, previous, deps, head_dim):
+def attn_forward(base, count, total, own, own_base, other, weights, tables, previous, deps, head_dim):
     seq_len, width = own.shape[1:]
     wqkv = weights[0]
     heads = width // head_dim
     shapes = [((seq_len, width), BF16), ((seq_len, 3 * width), BF16), ((heads, seq_len * 3 // 2, HALF_Q), BF16), ((seq_len, width), BF16),
               ((seq_len, width), F32), ((seq_len, LANES), F32), ((seq_len, width), BF16)]
     operands = (own, other) + tuple(weights) + tuple(tables)
-    specs = [per_seq((seq_len, width), base), per_seq((seq_len, width))] + [whole(item.shape) for item in operands[2:]]
+    specs = [per_seq((seq_len, width), own_base), per_seq((seq_len, width))] + [whole(item.shape) for item in operands[2:]]
     extra = tuple(previous) if previous is not None else ()
     specs += [ANYWHERE] * (len(extra) + len(deps))
     flops = count * (2 * seq_len * width * (wqkv.shape[1] + width) + 4 * heads * seq_len * seq_len * 64)
@@ -442,6 +441,10 @@
     )(left, right, *extra, *deps)
 
 
+def groups_of(start, stop, size):
+    return [(base, size) for base in range(start, stop, size)]
+
+
 def join_kernel(plain, peer_ref, *refs):
     owns, outs = refs[:len(refs) // 2], refs[len(refs) // 2:]
     start = 0
@@ -673,14 +676,19 @@
         def row_of(vector):
             return vector.astype(F32).reshape(1, -1)
 
-        size = total // 4
+        half = total // 2
         qkv_loc, wide_loc = b_qkv.size, b_gate.shape[0]
-        first = rows_of(peer_ids[:size], peer_in[:size]).astype(F32)
-        rest = rows_of(peer_ids[size:], peer_in[size:]).astype(F32)
-        own_rows = rows_of(own_ids, own_in)
+        groups = [(num, 1) for num in range(half)] + groups_of(half, total, 2)
+
+        def both_halves(ids, inside, kind):
+            head = rows_of(ids[:half], inside[:half]).astype(kind)
+            return head, rows_of(tie(ids[half:], head), inside[half:]).astype(kind)
+
+        peer_halves = both_halves(peer_ids, peer_in, F32)
+        own_halves = both_halves(own_ids, own_in, BF16)
         front_peer = collect(shared_slice((w_qkv,), (w_out,), dp_index, parts))
         wide_peer = collect(shared_slice((w_gate, w_lin), (w_down,), dp_index, parts))
-        arrived = [exchange(first)] + [exchange(rest[num * size:(num + 1) * size]) for num in range(3)]
+        arrived = [exchange(peer_halves[base // half][base % half:base % half + count]) for base, count in groups]
         own_bias = jnp.concatenate([row_of(b_qkv), row_of(b_gate), row_of(b_lin)], axis=1)
         biases = jnp.concatenate([own_bias, exchange(own_bias)])
         bqkv_full = biases[:, :qkv_loc].reshape(1, -1)
@@ -702,7 +710,8 @@
 
         def run_attention(num):
             nonlocal saved, deps
-            out = attn_forward(num * size, size, total, own_rows, arrived[num], front, tables, saved, deps, head_dim)
+            base, count = groups[num]
+            out = attn_forward(base, count, total, own_halves[base // half], base % half, arrived[num], front, tables, saved, deps, head_dim)
             *kept, token = out
             saved, deps = kept, (token,)
 
@@ -729,13 +738,12 @@
             deps = (token,)
             return out
 
-        run_attention(0)
-        run_attention(1)
-        run_ffn(0, 2 * size)
-        run_attention(2)
-        run_attention(3)
-        run_backward(0, 2 * size)
-        run_ffn(2 * size, 2 * size)
+        for num in range(half + 2):
+            run_attention(num)
+            if num % 2 and num < half:
+                run_ffn(num - 1, 2)
+        run_backward(0, half)
+        run_ffn(half, half)
         inner, d_gate, d_lin, d_ffn, _, d_attn = ffn_saved
         emb, _, _, context, _, _, hidden = saved
         shape = (width, 6 * wide_loc)
@@ -744,8 +752,8 @@
         grads = run_outer(hidden, d_lin, CHUNK, shape, step, grads)
         grads = run_outer(d_ffn, inner, CHUNK, shape, 2 * step, grads)
         wide_grads = reduce_gradient(grads)
-        run_backward(2 * size, size)
-        run_backward(3 * size, size)
+        for base, count in groups_of(half, total, 2):
+            run_backward(base, count)
         block = w_out.shape[0]
         shape = (width + parts * TILE, 2 * (qkv_loc + block))
         d_qkv, d_all = d_kept

time: 1790 us -> 1910 us (1.067)
  waiting for transfers between devices: 378 us -> 501 us
    ppermute x10 -> x12, waiting for transfers between devices: 138 us -> 261 us  [exchange(): return lax.ppermute(value, 'tp', SWAP)]
    pallas_call x2 -> x3, Pallas kernels: 226 us -> 204 us  [ffn(): pl.pallas_call(functools.partial(ffn_kernel, base), grid=(count,), in_spe...]
    pallas_call x4 -> x6, Pallas kernels: 116 us -> 125 us  [attn_forward(): pl.pallas_call(functools.partial(attn_forward_kernel, head_dim, len(extra...]
    gather x3 -> x4, local copies, waits for them, and re-layouts: 72.5 us -> 80.6 us  [rows_of(): rows = jnp.take(emb_table, jnp.where(inside, ids, 0), axis=0)]
    unnamed x45 -> x51, local copies, waits for them, and re-layouts: 44.9 us -> 44.9 us
  transfers between devices with their start and end apart: 18 -> 20, of which waited for: 8 -> 9; matrix products, arithmetic and copies ran while one was open for 13% -> 13% of each run, Pallas kernels for 38% -> 35%
where the time goes in v4:
time: 1910 us; the launch traced here: 1900 us
  Pallas kernels  1060 us (55%)
  waiting for transfers between devices  501 us (26%)
  local copies, waits for them, and re-layouts  170 us (9%)
  other arithmetic  137 us (7%)
    pallas_call x1, Pallas kernels, reduce_table(): pl.pallas_call(table_kernel, in_specs=[ANYWHERE], out_specs=ANYWHERE, out...  453 us
    ppermute x12, waiting for transfers between devices, exchange(): return lax.ppermute(value, 'tp', SWAP)  261 us
    reduce_scatter x2, waiting for transfers between devices, reduce_gradient(): piece = lax.psum_scatter(grad, 'dp', scatter_dimension=0, tiled=True)  225 us
    pallas_call x3, Pallas kernels, ffn(): pl.pallas_call(functools.partial(ffn_kernel, base), grid=(count,), in_spe...  204 us
    pallas_call x3, Pallas kernels, attn_backward(): pl.pallas_call(functools.partial(attn_backward_kernel, head_dim, len(extr...  134 us
    pallas_call x5, Pallas kernels, outer(): pl.pallas_call(outer_kernel, grid=(wide // block,), in_specs=[whole((rows...  126 us
    pallas_call x6, Pallas kernels, attn_forward(): pl.pallas_call(functools.partial(attn_forward_kernel, head_dim, len(extra...  125 us
    scatter-add x2, other arithmetic, add_rows(): return grad.at[ids.reshape(-1)].add(rows.reshape(-1, width), mode='drop')  105 us
  transfers between devices with their start and end apart: 20, of which 9 were waited for; matrix products, arithmetic and copies ran while one was open for 13% of the time, Pallas kernels for 35%

profile of v4, /device:TPU:0, one launch (start us, length us, event | category | flops | bytes accessed | tf_op | source)
XLA Modules:
  0.0 1902.1 jit_solution(5551237657661133885)
XLA Ops:
  31.5 38.0 %collective-permute-done.8 = f32[96,4608]{1,0:T(8,128)S(1)} collective-permute-done((f32[96,4608]{1,0:T(8,128)S(1)}, f32[96,4608]{1,0:T(8,128)S(1)}, u32[]{:S(2)}, u32[]{:S(2)}) %collective-permute-start.8) | collective-permute-done | bytes 1769504 | tf_op jit(solution)/shard_map/ppermute | solution.py:670
  72.6 21.3 %gather_fusion = bf16[2048,768]{1,0:T(8,128)(2,1)S(1)} fusion(bf16[15296,768]{1,0:T(8,128)(2,1)} %param.20, s32[2048]{0:T(1024)S(1)} %broadcast_clamp_fusion.3), kind=kCustom, calls=%fused_computation.clone | custom fusion | bytes 6299648 | tf_op jit(solution)/shard_map/jit(_take)/gather | solution.py:666
  93.9 20.8 %gather_fusion.2 = bf16[2048,768]{1,0:T(8,128)(2,1)} fusion(bf16[15296,768]{1,0:T(8,128)(2,1)} %param.20, s32[2048]{0:T(1024)S(1)} %broadcast_clamp_fusion.1), kind=kCustom, calls=%fused_computation.2.clone | custom fusion | bytes 6299648 | tf_op jit(solution)/shard_map/jit(_take)/gather | solution.py:666
  121.2 19.5 %gather_fusion.3 = bf16[2048,768]{1,0:T(8,128)(2,1)S(1)} fusion(bf16[15296,768]{1,0:T(8,128)(2,1)} %param.20, s32[2048]{0:T(1024)S(1)} %broadcast_clamp_fusion), kind=kCustom, calls=%fused_computation.3.clone | custom fusion | bytes 6299648 | tf_op jit(solution)/shard_map/jit(_take)/gather | solution.py:666
  152.4 19.2 %gather_fusion.1 = bf16[2048,768]{1,0:T(8,128)(2,1)S(1)} fusion(bf16[15296,768]{1,0:T(8,128)(2,1)} %param.20, s32[2048]{0:T(1024)S(1)} %broadcast_clamp_fusion.2), kind=kCustom, calls=%fused_computation.1.clone | custom fusion | bytes 6299648 | tf_op jit(solution)/shard_map/jit(_take)/gather | solution.py:666
  192.9 125.0 %collective-permute-done.7.refs_1_ = f32[1,512,768]{2,1,0:T(8,128)} collective-permute-done((f32[1,512,768]{2,1,0:T(8,128)}, f32[1,512,768]{2,1,0:T(8,128)}, u32[]{:S(2)}, u32[]{:S(2)}) %collective-permute-start.7) | collective-permute-done | bytes 1572896 | tf_op jit(solution)/shard_map/ppermute | solution.py:670
  317.9 17.3 attn_forward.6
  335.2 16.4 collective-permute-done.6.refs_1_
  351.6 16.7 attn_forward.7
  380.7 52.9 %ffn.3 = (bf16[4096,3072]{1,0:T(8,128)(2,1)}, bf16[4096,3072]{1,0:T(8,128)(2,1)}, bf16[4096,3072]{1,0:T(8,128)(2,1)}, bf16[8,512,768]{2,1,0:T(8,128)(2,1)}, f32[...) custom-call(bf16[8,512,768]{2,1,0:T(8,128)(2,1)} %get-tuple-element., ...), custom_call_target="tpu_custom_call" | custom-call | flops 43486543872 | bytes 28000000 | tf_op jit(solution)/shard_map/ffn/pallas_call | solution.py:368
  433.6 16.7 attn_forward.8
  450.3 16.5 attn_forward.9
  466.8 53.2 %ffn.4 = (bf16[4096,3072]{1,0:T(8,128)(2,1)}, bf16[4096,3072]{1,0:T(8,128)(2,1)}, bf16[4096,3072]{1,0:T(8,128)(2,1)}, bf16[8,512,768]{2,1,0:T(8,128)(2,1)}, f32[...) custom-call(bf16[8,512,768]{2,1,0:T(8,128)(2,1)} %get-tuple-element., ...), custom_call_target="tpu_custom_call", output_to_operand_aliasing={{0}: (12, {}), {1}: (13, {}), {2}: (14, {}), {3}: (15, {}),... | custom-call | flops 43486543872 | bytes 28000000 | tf_op jit(solution)/shard_map/ffn/pallas_call | solution.py:368
  520.1 29.0 %attn_forward.10 = (bf16[8,512,768]{2,1,0:T(8,128)(2,1)}, bf16[8,512,2304]{2,1,0:T(8,128)(2,1)}, bf16[8,12,768,256]{3,2,1,0:T(8,128)(2,1)}, bf16[8,512,768]{2,1,...) custom-call(bf16[4,512,768]{2,1,0:T(8,128)(2,1)} %select_select_fusi, ...), custom_call_target="tpu_custom_call", output_to_operand_aliasing={{0}: (10, {}), {1}: (11, {}), {2}: (12, {}), {3}: (13, {}),... | custom-call | flops 12884901888 | bytes 24000000 | tf_op jit(solution)/shard_map/attn_forward/pallas_call | solution.py:345
  549.1 29.2 %attn_forward.11 = (bf16[8,512,768]{2,1,0:T(8,128)(2,1)}, bf16[8,512,2304]{2,1,0:T(8,128)(2,1)}, bf16[8,12,768,256]{3,2,1,0:T(8,128)(2,1)}, bf16[8,512,768]{2,1,...) custom-call(bf16[4,512,768]{2,1,0:T(8,128)(2,1)} %select_select_fusi, ...), custom_call_target="tpu_custom_call", output_to_operand_aliasing={{0}: (10, {}), {1}: (11, {}), {2}: (12, {}), {3}: (13, {}),... | custom-call | flops 12884901888 | bytes 24000000 | tf_op jit(solution)/shard_map/attn_forward/pallas_call | solution.py:345
  578.3 63.6 %attn_backward.3 = (f32[4,512,768]{2,1,0:T(8,128)}, bf16[8,512,2304]{2,1,0:T(8,128)(2,1)}, f32[8,512,768]{2,1,0:T(8,128)}, f32[8,2304]{1,0:T(8,128)}, f32[8,128]{1,0:T(8,128)}) custom-call(f32[8,512,768]{2,1,0:T(8,128)} %get-tuple-element.183.refs_0_.refs_4_, bf16[8,512,768]{2,1,0:T(8,128)(2,1)} %get-tuple-element.184.refs_1_.refs_5_, ...), custom_call_target="tpu_custom_call" | custom-call | flops 32212254720 | bytes 48000000 | tf_op jit(solution)/shard_map/attn_backward/pallas_call | solution.py:393
  641.9 97.7 %ffn.5 = (bf16[4096,3072]{1,0:T(8,128)(2,1)}, bf16[4096,3072]{1,0:T(8,128)(2,1)}, bf16[4096,3072]{1,0:T(8,128)(2,1)}, bf16[8,512,768]{2,1,0:T(8,128)(2,1)}, f32[...) custom-call(bf16[8,512,768]{2,1,0:T(8,128)(2,1)} %get-tuple-element., ...), custom_call_target="tpu_custom_call", output_to_operand_aliasing={{0}: (12, {}), {1}: (13, {}), {2}: (14, {}), {3}: (15, {}),... | custom-call | flops 86973087744 | bytes 56000000 | tf_op jit(solution)/shard_map/ffn/pallas_call | solution.py:368
  743.8 28.1 %outer.5 = (f32[768,9216]{1,0:T(8,128)}, f32[8,128]{1,0:T(8,128)}) custom-call(bf16[4096,768]{1,0:T(8,128)(2,1)} %bitcast.62, bf16[4096,3072]{1,0:T(8,128)(2,1)} %get-tuple-element.196.right_ref, f32[8,128]{1,0:T(8,128)} %get-tuple-element.197.refs_0_), custom_call_target="tpu_custom_call" | custom-call | flops 19327352832 | bytes 40894464 | tf_op jit(solution)/shard_map/outer/pallas_call | solution.py:430
  772.0 28.1 %outer.6 = (f32[768,9216]{1,0:T(8,128)}, f32[8,128]{1,0:T(8,128)}) custom-call(bf16[4096,768]{1,0:T(8,128)(2,1)} %bitcast.63, bf16[4096,3072]{1,0:T(8,128)(2,1)} %get-tuple-element.195.right_ref, f32[768,9216]{1,0:T(8,128)} %get-tuple-element.198.refs_0_, f32[8,128]{1,0:T(8,128)} %get-tuple-element.199.refs_1_), custom_call_target="tpu_custom_call", output_to_operand_aliasing={{0}: (2, {})} | custom-call | flops 19327352832 | bytes 40894464 | tf_op jit(solution)/shard_map/outer/pallas_call | solution.py:430
  800.1 28.5 %outer.7 = (f32[768,9216]{1,0:T(8,128)}, f32[8,128]{1,0:T(8,128)}) custom-call(bf16[4096,768]{1,0:T(8,128)(2,1)} %bitcast.99, bf16[4096,3072]{1,0:T(8,128)(2,1)} %get-tuple-element.194.right_ref, f32[768,9216]{1,0:T(8,128)} %get-tuple-element.200.refs_0_, f32[8,128]{1,0:T(8,128)} %get-tuple-element.201.refs_1_), custom_call_target="tpu_custom_call", output_to_operand_aliasing={{0}: (2, {})} | custom-call | flops 19327352832 | bytes 40894464 | tf_op jit(solution)/shard_map/outer/pallas_call | solution.py:430
  828.6 35.4 %attn_backward.4 = (f32[2,512,768]{2,1,0:T(8,128)}, bf16[8,512,2304]{2,1,0:T(8,128)(2,1)}, f32[8,512,768]{2,1,0:T(8,128)}, f32[8,2304]{1,0:T(8,128)}, f32[8,128]{1,0:T(8,128)}) custom-call(f32[8,512,768]{2,1,0:T(8,128)} %get-tuple-element.189.refs_0_, bf16[8,512,768]{2,1,0:T(8,128)(2,1)} %get-tuple-element.190.refs_1_, ...), custom_call_target="tpu_custom_call", output_to_operand_aliasing={{1}: (8, {}), {2}: (9, {})} | custom-call | flops 16106127360 | bytes 24000000 | tf_op jit(solution)/shard_map/attn_backward/pallas_call | solution.py:393
  864.0 35.5 %attn_backward.5 = (f32[2,512,768]{2,1,0:T(8,128)}, bf16[8,512,2304]{2,1,0:T(8,128)(2,1)}, f32[8,512,768]{2,1,0:T(8,128)}, f32[8,2304]{1,0:T(8,128)}, f32[8,128]{1,0:T(8,128)}) custom-call(f32[8,512,768]{2,1,0:T(8,128)} %get-tuple-element.189.refs_0_, bf16[8,512,768]{2,1,0:T(8,128)(2,1)} %get-tuple-element.190.refs_1_, ...), custom_call_target="tpu_custom_call", output_to_operand_aliasing={{1}: (8, {}), {2}: (9, {})} | custom-call | flops 16106127360 | bytes 24000000 | tf_op jit(solution)/shard_map/attn_backward/pallas_call | solution.py:393
  902.8 13.9 outer.8
  916.7 27.6 %outer.9 = (f32[832,3072]{1,0:T(8,128)}, f32[8,128]{1,0:T(8,128)}) custom-call(bf16[4096,768]{1,0:T(8,128)(2,1)} %bitcast.60, bf16[4096,2304]{1,0:T(8,128)(2,1)} %bitcast.64, f32[832,3072]{1,0:T(8,128)} %get-tuple-element.214.refs_0_, f32[8,128]{1,0:T(8,128)} %get-tuple-element.215.refs_1_), custom_call_target="tpu_custom_call", output_to_operand_aliasing={{0}: (2, {})} | custom-call | flops 14495514624 | bytes 32243712 | tf_op jit(solution)/shard_map/outer/pallas_call | solution.py:430
  946.4 74.2 %reduce-scatter.3.cloned.1.call-done = f32[104,3072]{1,0:T(8,128)} async-done(((f32[832,3072]{1,0:T(8,128)}), f32[104,3072]{1,0:T(8,128)}) %reduce-scatter.3.cloned.1.call-update) | async-done | bytes 1277968 | tf_op jit(solution)/shard_map/reduce_scatter | solution.py:634
  1023.3 14.5 collective-permute-done.12
  1043.5 150.5 %reduce-scatter.5.cloned.1.call-done = f32[96,9216]{1,0:T(8,128)} async-done(((f32[768,9216]{1,0:T(8,128)}), f32[96,9216]{1,0:T(8,128)}) %reduce-scatter.5.cloned.1.call-update) | async-done | bytes 3538960 | tf_op jit(solution)/shard_map/reduce_scatter | solution.py:634
  1198.3 46.9 %scatter_custom_fusion = f32[15296,768]{1,0:T(8,128)} fusion(s32[4096]{0:T(1024)S(1)} %bitcast.92, f32[4096,768]{1,0:T(8,128)} %bitcast.65, f32[]{:T(128)} %constant.22.clone.1), kind=kCustom, calls=%fused_computation.6 | custom fusion | flops 3145728 | bytes 46989824 | tf_op jit(solution)/shard_map/scatter-add | solution.py:775
  1246.0 67.5 %collective-permute-done.10 = f32[2,512,768]{2,1,0:T(8,128)} collective-permute-done((f32[2,512,768]{2,1,0:T(8,128)}, f32[2,512,768]{2,1,0:T(8,128)}, u32[]{:S(2)}, u32[]{:S(2)}) %collective-permute-start.10) | collective-permute-done | bytes 3145760 | tf_op jit(solution)/shard_map/ppermute | solution.py:670
  1322.7 58.1 %scatter_fusion = f32[15296,768]{1,0:T(8,128)} fusion(f32[15296,768]{1,0:T(8,128)} %scatter_custom_fusion, s32[4096]{0:T(1024)S(1)} %bitcast.86, f32[4096,768]{1,0:T(8,128)} %bitcast.66), kind=kCustom, calls=%fused_computation.5 | custom fusion | flops 3145728 | bytes 37765120 | tf_op jit(solution)/shard_map/scatter-add | solution.py:775
  1383.7 452.6 %reduce_table.1 = f32[15296,768]{1,0:T(8,128)} custom-call(f32[15296,768]{1,0:T(8,128)} %scatter_fusion), custom_call_target="tpu_custom_call" | custom-call | flops 399999991808 | bytes 93978624 | tf_op jit(solution)/shard_map/reduce_table/pallas_call | solution.py:620
  1862.4 32.6 %copy.157 = f32[15296,768]{1,0:T(8,128)} copy(f32[15296,768]{1,0:T(8,128)} %reduce_table.1) | data formatting | bytes 93978624
  (158 shorter events, 140.3 us)
Async XLA Ops:
  7.2 63.6 %copy-start.8 = (bf16[6,192]{1,0:T(8,128)(2,1)S(1)}, bf16[6,192]{1,0:T(8,128)(2,1)}, u32[]{:S(2)}) copy-start(bf16[6,192]{1,0:T(8,128)(2,1)} %param.22) | copy-start | bytes 6916
  7.2 63.7 %copy-start.9 = (bf16[1536]{0:T(1024)(128)(2,1)S(1)}, bf16[1536]{0:T(1024)(128)(2,1)}, u32[]{:S(2)}) copy-start(bf16[1536]{0:T(1024)(128)(2,1)} %param.28) | copy-start | bytes 9220
  7.2 63.7 %copy-start.10 = (bf16[1536]{0:T(1024)(128)(2,1)S(1)}, bf16[1536]{0:T(1024)(128)(2,1)}, u32[]{:S(2)}) copy-start(bf16[1536]{0:T(1024)(128)(2,1)} %param.30) | copy-start | bytes 9220
  7.2 179.3 %all-gather.5.cloned.1.call-start = ((), (), s32[]{:S(2)}) async-start(), calls=%async_computation.2 | async-start | bytes 5308416 | tf_op jit(solution)/shard_map/all_gather | solution.py:674
  7.3 65.2 %copy-start.7 = (s32[16,512]{1,0:T(8,128)S(1)}, s32[16,512]{1,0:T(8,128)}, u32[]{:S(2)}) copy-start(s32[16,512]{1,0:T(8,128)} %param.18) | copy-start | bytes 98308
  9.4 16.6 collective-permute-start.1
  26.9 341.4 %all-gather.7.cloned.1.call-start = ((), (), s32[]{:S(2)}) async-start(), calls=%async_computation.3 | async-start | bytes 15925248 | tf_op jit(solution)/shard_map/all_gather | solution.py:674
  29.7 39.8 %collective-permute-start.8 = (f32[96,4608]{1,0:T(8,128)S(1)}, f32[96,4608]{1,0:T(8,128)S(1)}, u32[]{:S(2)}, u32[]{:S(2)}) collective-permute-start(f32[96,4608]{1,0:T(8,128)S(1)} %maximum_convert_fusion), channel_id=1, source_target_pairs={{0,8},{8,0},{1,9},{9,1},{2,10},{10,2},{3,11},{11,3},{4,12},{12,4},... | collective-permute-start | bytes 5308424 | tf_op jit(solution)/shard_map/ppermute | solution.py:670
  70.8 949.9 %reduce-scatter.3.cloned.1.call-start = ((), (), s32[]{:S(2)}) async-start(), calls=%async_computation.4 | async-start | bytes 11501568 | tf_op jit(solution)/shard_map/reduce_scatter | solution.py:634
  71.0 113.6 %collective-permute-start.2 = (f32[1,4224]{1,0:T(1,128)S(1)}, f32[1,4224]{1,0:T(1,128)S(1)}, u32[]{:S(2)}, u32[]{:S(2)}) collective-permute-start(f32[1,4224]{1,0:T(1,128)S(1)} %maximum_convert_fusion.2), channel_id=1, source_target_pairs={{0,8},{8,0},{1,9},{9,1},{2,10},{10,2},{3,11},{11,3},{4,12},{12,4},... | collective-permute-start | bytes 50696 | tf_op jit(solution)/shard_map/ppermute | solution.py:670
  72.5 42.1 %copy-start.3 = (s32[16,512]{1,0:T(8,128)}, s32[16,512]{1,0:T(8,128)S(1)}, u32[]{:S(2)}) copy-start(s32[16,512]{1,0:T(8,128)S(1)} %get-tuple-element.250) | copy-start | bytes 98308
  72.5 48.7 %copy-start.5 = (pred[16,512]{1,0:T(8,128)(4,1)}, pred[16,512]{1,0:T(8,128)(4,1)S(1)}, u32[]{:S(2)}) copy-start(pred[16,512]{1,0:T(8,128)(4,1)S(1)} %get-tuple-element.249) | copy-start | bytes 24580
  140.7 6.8 slice-start
  142.2 5.3 slice-start.1
  145.5 374.6 %collective-permute-start.3 = (f32[2,512,768]{2,1,0:T(8,128)}, f32[2,512,768]{2,1,0:T(8,128)}, u32[]{:S(2)}, u32[]{:S(2)}) collective-permute-start(f32[2,512,768]{2,1,0:T(8,128)} %get-tuple-element.258), channel_id=1, source_target_pairs={{0,8},{8,0},{1,9},{9,1},{2,10},{10,2},{3,11},{11,3},{4,12},{12,4},... | collective-permute-start | bytes 9437192 | tf_op jit(solution)/shard_map/ppermute | solution.py:670
  145.5 403.6 %collective-permute-start = (f32[2,512,768]{2,1,0:T(8,128)}, f32[2,512,768]{2,1,0:T(8,128)}, u32[]{:S(2)}, u32[]{:S(2)}) collective-permute-start(f32[2,512,768]{2,1,0:T(8,128)} %get-tuple-element.259), channel_id=1, source_target_pairs={{0,8},{8,0},{1,9},{9,1},{2,10},{10,2},{3,11},{11,3},{4,12},{12,4},... | collective-permute-start | bytes 9437192 | tf_op jit(solution)/shard_map/ppermute | solution.py:670
  150.3 167.6 %collective-permute-start.7 = (f32[1,512,768]{2,1,0:T(8,128)}, f32[1,512,768]{2,1,0:T(8,128)}, u32[]{:S(2)}, u32[]{:S(2)}) collective-permute-start(f32[1,512,768]{2,1,0:T(8,128)} %get-tuple-element.254), channel_id=1, source_target_pairs={{0,8},{8,0},{1,9},{9,1},{2,10},{10,2},{3,11},{11,3},{4,12},{12,4},... | collective-permute-start | bytes 4718600 | tf_op jit(solution)/shard_map/ppermute | solution.py:670
  150.3 201.3 %collective-permute-start.6 = (f32[1,512,768]{2,1,0:T(8,128)}, f32[1,512,768]{2,1,0:T(8,128)}, u32[]{:S(2)}, u32[]{:S(2)}) collective-permute-start(f32[1,512,768]{2,1,0:T(8,128)} %get-tuple-element.255), channel_id=1, source_target_pairs={{0,8},{8,0},{1,9},{9,1},{2,10},{10,2},{3,11},{11,3},{4,12},{12,4},... | collective-permute-start | bytes 4718600 | tf_op jit(solution)/shard_map/ppermute | solution.py:670
  178.4 5.7 copy-start.15
  184.6 248.9 %collective-permute-start.5 = (f32[1,512,768]{2,1,0:T(8,128)}, f32[1,512,768]{2,1,0:T(8,128)}, u32[]{:S(2)}, u32[]{:S(2)}) collective-permute-start(f32[1,512,768]{2,1,0:T(8,128)} %get-tuple-element.256), channel_id=1, source_target_pairs={{0,8},{8,0},{1,9},{9,1},{2,10},{10,2},{3,11},{11,3},{4,12},{12,4},... | collective-permute-start | bytes 4718600 | tf_op jit(solution)/shard_map/ppermute | solution.py:670
  317.9 132.4 %collective-permute-start.4 = (f32[1,512,768]{2,1,0:T(8,128)}, f32[1,512,768]{2,1,0:T(8,128)}, u32[]{:S(2)}, u32[]{:S(2)}) collective-permute-start(f32[1,512,768]{2,1,0:T(8,128)} %get-tuple-element.257), channel_id=1, source_target_pairs={{0,8},{8,0},{1,9},{9,1},{2,10},{10,2},{3,11},{11,3},{4,12},{12,4},... | collective-permute-start | bytes 4718600 | tf_op jit(solution)/shard_map/ppermute | solution.py:670
  945.8 248.2 %reduce-scatter.5.cloned.1.call-start = ((), (), s32[]{:S(2)}) async-start(), calls=%async_computation.6 | async-start | bytes 31850496 | tf_op jit(solution)/shard_map/reduce_scatter | solution.py:634
  945.9 97.6 %copy-start.4 = (s32[16,512]{1,0:T(8,128)S(1)}, s32[16,512]{1,0:T(8,128)}, u32[]{:S(2)}) copy-start(s32[16,512]{1,0:T(8,128)} %copy-done.3) | copy-start | bytes 98308
  945.9 97.6 %copy-start.6 = (pred[16,512]{1,0:T(8,128)(4,1)S(1)}, pred[16,512]{1,0:T(8,128)(4,1)}, u32[]{:S(2)}) copy-start(pred[16,512]{1,0:T(8,128)(4,1)} %copy-done.5) | copy-start | bytes 24580
  946.4 889.9 %all-gather.9.cloned.1.call-start = ((), (), s32[]{:S(2)}) async-start(), calls=%async_computation.5 | async-start | bytes 5750784 | tf_op jit(solution)/shard_map/all_gather | solution.py:637
  1021.8 16.0 collective-permute-start.12
  1039.9 805.9 %all-gather.11.cloned.1.call-start = ((), (), s32[]{:S(2)}) async-start(), calls=%async_computation.7 | async-start | bytes 15925248 | tf_op jit(solution)/shard_map/all_gather | solution.py:637
  1039.9 273.6 %collective-permute-start.9 = (f32[4,512,768]{2,1,0:T(8,128)}, f32[4,512,768]{2,1,0:T(8,128)}, u32[]{:S(2)}, u32[]{:S(2)}) collective-permute-start(f32[4,512,768]{2,1,0:T(8,128)} %get-tuple-element.207), channel_id=1, source_target_pairs={{0,8},{8,0},{1,9},{9,1},{2,10},{10,2},{3,11},{11,3},{4,12},{12,4},... | collective-permute-start | bytes 18874376 | tf_op jit(solution)/shard_map/ppermute | solution.py:670
  1041.5 204.5 %collective-permute-start.11 = (f32[2,512,768]{2,1,0:T(8,128)}, f32[2,512,768]{2,1,0:T(8,128)S(1)}, u32[]{:S(2)}, u32[]{:S(2)}) collective-permute-start(f32[2,512,768]{2,1,0:T(8,128)} %get-tuple-element.209), channel_id=1, source_target_pairs={{0,8},{8,0},{1,9},{9,1},{2,10},{10,2},{3,11},{11,3},{4,12},{12,4},... | collective-permute-start | bytes 9437192 | tf_op jit(solution)/shard_map/ppermute | solution.py:670
  1042.0 271.5 %collective-permute-start.10 = (f32[2,512,768]{2,1,0:T(8,128)}, f32[2,512,768]{2,1,0:T(8,128)}, u32[]{:S(2)}, u32[]{:S(2)}) collective-permute-start(f32[2,512,768]{2,1,0:T(8,128)} %get-tuple-element.208), channel_id=1, source_target_pairs={{0,8},{8,0},{1,9},{9,1},{2,10},{10,2},{3,11},{11,3},{4,12},{12,4},... | collective-permute-start | bytes 9437192 | tf_op jit(solution)/shard_map/ppermute | solution.py:670
  1196.8 184.0 %collective-permute-start.13 = (f32[96,4608]{1,0:T(8,128)}, f32[96,4608]{1,0:T(8,128)}, u32[]{:S(2)}, u32[]{:S(2)}) collective-permute-start(f32[96,4608]{1,0:T(8,128)} %slice.180), channel_id=1, source_target_pairs={{0,8},{8,0},{1,9},{9,1},{2,10},{10,2},{3,11},{11,3},{4,12},{12,4},... | collective-permute-start | bytes 5308424 | tf_op jit(solution)/shard_map/ppermute | solution.py:636
  1322.7 58.1 %copy-start = (f32[96,9216]{1,0:T(8,128)S(1)}, f32[96,9216]{1,0:T(8,128)}, u32[]{:S(2)}) copy-start(f32[96,9216]{1,0:T(8,128)} %reduce-scatter.5.cloned.1.call-done) | copy-start | bytes 10616836
  (6 other events, 18.9 us)
Sparse Core Ops, SparseCore 0:
  27.0 36.2 all-gather.4
  70.9 75.6 all-gather.6
  945.9 74.6 reduce-scatter.2
  1024.2 169.7 reduce-scatter.4
  1196.3 36.6 all-gather.8
  1383.8 103.4 all-gather.10

commit v5 on v4

--- a/solution.py
+++ b/solution.py
@@ -405,7 +405,7 @@
     )(*operands, *extra, *deps)
 
 
-def outer_kernel(left_ref, right_ref, *refs):
+def outer_kernel(own_ref, left_ref, right_ref, *refs):
     out_ref, token_ref, left_t = refs[-3:]
     clear(token_ref)
 
@@ -421,24 +421,28 @@
     out_ref[...] = dot_nn(full(left_t), full(right_ref))
 
 
-def outer(left, right, block, shape, slot, previous, deps):
+def outer(left, right, block, shape, slot, index, previous, deps):
     rows, width = left.shape
     wide = right.shape[1]
     per_half = wide // (2 * block)
-    half_blocks = shape[1] // (2 * block)
     extra = (previous,) if previous is not None else ()
+    grid_spec = pltpu.PrefetchScalarGridSpec(
+        num_scalar_prefetch=1,
+        grid=(wide // block,),
+        in_specs=[pl.BlockSpec((rows, width), lambda i, own: (0, 0), pipeline_mode=pl.Buffered(1)), pl.BlockSpec((rows, block), lambda i, own: (0, i))]
+        + [ANYWHERE] * (len(extra) + len(deps)),
+        out_specs=[pl.BlockSpec((None, width, block), lambda i, own: ((i // per_half + own[0]) % 2, 0, slot + i % per_half)),
+                   pl.BlockSpec(TOKEN, lambda i, own: (0, 0))],
+        scratch_shapes=[pltpu.VMEM((width, rows), BF16)])
     return pl.pallas_call(
         outer_kernel,
-        grid=(wide // block,),
-        in_specs=[whole((rows, width)), pl.BlockSpec((rows, block), lambda i: (0, i))] + [ANYWHERE] * (len(extra) + len(deps)),
-        out_specs=[pl.BlockSpec((width, block), lambda i: (0, slot + i % per_half + half_blocks * (i // per_half))), token_spec()],
+        grid_spec=grid_spec,
         out_shape=[jax.ShapeDtypeStruct(shape, F32), jax.ShapeDtypeStruct(TOKEN, F32)],
-        input_output_aliases={2 + num: num for num in range(len(extra))},
-        scratch_shapes=[pltpu.VMEM((width, rows), BF16)],
+        input_output_aliases={3 + num: num for num in range(len(extra))},
         compiler_params=params(),
         cost_estimate=cost(2 * rows * width * wide, 4 * width * wide + 2 * rows * (width + wide)),
         name='outer',
-    )(left, right, *extra, *deps)
+    )(index, left, right, *extra, *deps)
 
 
 def groups_of(start, stop, size):
@@ -631,10 +635,8 @@
 
 
 def reduce_gradient(grad):
-    piece = lax.psum_scatter(grad, 'dp', scatter_dimension=0, tiled=True)
-    half = piece.shape[1] // 2
-    other = lax.ppermute(piece[:, half:], 'tp', SWAP)
-    return lax.all_gather(piece[:, :half] + other, 'dp', axis=0, tiled=True)
+    piece = lax.psum_scatter(grad.reshape(-1, grad.shape[2]), ('tp', 'dp'), scatter_dimension=0, tiled=True)
+    return lax.all_gather(piece, 'dp', axis=0, tiled=True)
 
 
 def tie(value, token):
@@ -662,9 +664,11 @@
         peer_in = lax.dynamic_slice_in_dim(in_shard, (1 - tp_index) * total, total)
         own_cot = lax.dynamic_slice_in_dim(cotangent, tp_index * total, total)
 
-        def rows_of(ids, inside):
-            rows = jnp.take(emb_table, jnp.where(inside, ids, 0), axis=0)
-            return jnp.where(inside[:, :, None], rows, 0.0)
+        def rows_of(part, head):
+            ids = jnp.concatenate([peer_ids[part], own_ids[part]])
+            rows = jnp.take(emb_table, tie(jnp.where((ids >= 0) & (ids < vocab_loc), ids, 0), head), axis=0)
+            peer_rows, own_rows = (jnp.where(inside[part][:, :, None], piece, 0.0) for inside, piece in zip((peer_in, own_in), jnp.split(rows, 2)))
+            return peer_rows.astype(F32), own_rows
 
         def exchange(value):
             return lax.ppermute(value, 'tp', SWAP)
@@ -680,17 +684,14 @@
         qkv_loc, wide_loc = b_qkv.size, b_gate.shape[0]
         groups = [(num, 1) for num in range(half)] + groups_of(half, total, 2)
 
-        def both_halves(ids, inside, kind):
-            head = rows_of(ids[:half], inside[:half]).astype(kind)
-            return head, rows_of(tie(ids[half:], head), inside[half:]).astype(kind)
-
-        peer_halves = both_halves(peer_ids, peer_in, F32)
-        own_halves = both_halves(own_ids, own_in, BF16)
+        first_rows = rows_of(slice(half), tp_index)
+        rest_rows = rows_of(slice(half, total), first_rows)
+        peer_halves, own_halves = zip(first_rows, rest_rows)
         front_peer = collect(shared_slice((w_qkv,), (w_out,), dp_index, parts))
+        own_bias = jnp.concatenate([row_of(b_qkv), row_of(b_gate), row_of(b_lin)], axis=1)
+        biases = jnp.concatenate([own_bias, exchange(own_bias)])
         wide_peer = collect(shared_slice((w_gate, w_lin), (w_down,), dp_index, parts))
         arrived = [exchange(peer_halves[base // half][base % half:base % half + count]) for base, count in groups]
-        own_bias = jnp.concatenate([row_of(b_qkv), row_of(b_gate), row_of(b_lin)], axis=1)
-        biases = jnp.concatenate([own_bias, exchange(own_bias)])
         bqkv_full = biases[:, :qkv_loc].reshape(1, -1)
         bgate_full = biases[:, qkv_loc:qkv_loc + wide_loc].reshape(1, -1)
         blin_full = biases[:, qkv_loc + wide_loc:].reshape(1, -1)
@@ -734,7 +735,7 @@
 
         def run_outer(left, right, block, shape, slot, previous):
             nonlocal deps
-            out, token = outer(left.reshape(-1, left.shape[-1]), right.reshape(-1, right.shape[-1]), block, shape, slot, previous, deps)
+            out, token = outer(left.reshape(-1, left.shape[-1]), right.reshape(-1, right.shape[-1]), block, shape, slot, half_index, previous, deps)
             deps = (token,)
             return out
 
@@ -746,7 +747,8 @@
         run_ffn(half, half)
         inner, d_gate, d_lin, d_ffn, _, d_attn = ffn_saved
         emb, _, _, context, _, _, hidden = saved
-        shape = (width, 6 * wide_loc)
+        half_index = tp_index.reshape(1)
+        shape = (2, width, 3 * wide_loc)
         step = wide_loc // CHUNK
         grads = run_outer(hidden, d_gate, CHUNK, shape, 0, None)
         grads = run_outer(hidden, d_lin, CHUNK, shape, step, grads)
@@ -755,17 +757,18 @@
         for base, count in groups_of(half, total, 2):
             run_backward(base, count)
         block = w_out.shape[0]
-        shape = (width + parts * TILE, 2 * (qkv_loc + block))
+        shape = (2, width + parts * TILE, qkv_loc + block)
         d_qkv, d_all = d_kept
         grads = run_outer(d_attn, context, block, shape, qkv_loc // block, None)
-        grads = run_outer(emb, d_qkv, block, shape, 0, grads)
+        grads = run_outer(emb, d_qkv, qkv_loc, shape, 0, grads)
 
         narrow = jnp.sum(sum(narrow_parts).reshape(5, 8, -1), axis=1).reshape(1, -1)
         d_bwide = jnp.sum(sum(wide_parts).reshape(2, 8, -1), axis=1).reshape(2, 2, -1)
         small = jnp.concatenate([jnp.sum(sum(bias_parts), axis=0).reshape(2, -1), d_bwide[0], d_bwide[1], jnp.concatenate([narrow] * 2)], axis=1)
         used = small.shape[1]
         small = jnp.pad(small, ((0, 0), (0, TILE * (qkv_loc + block) - used))).reshape(2, TILE, -1)
-        grads = lax.dynamic_update_slice(grads, jnp.concatenate([small[0], small[1]], axis=1), (width, 0))
+        small = jnp.where(tp_index == 0, small, small[::-1])
+        grads = lax.dynamic_update_slice(grads, small, (0, width, 0))
         front_grads = reduce_gradient(grads)
 
         own_row_ids = jnp.where(own_in, own_ids, vocab_loc)

time: 1910 us -> 1990 us (1.042)
  waiting for transfers between devices: 501 us -> 601 us
  local copies, waits for them, and re-layouts: 170 us -> 147 us
    ppermute x12, waiting for transfers between devices: 261 us -> 518 us  [exchange(): return lax.ppermute(value, 'tp', SWAP)]
    reduce_scatter x2, waiting for transfers between devices: 225 us -> 82.5 us  [reduce_gradient(): lax.psum_scatter(grad.reshape(-1, grad.shape[2]), ('tp', 'dp'), scatter_d...]
    gather x4 -> x2, local copies, waits for them, and re-layouts: 80.6 us -> 61.7 us  [rows_of(): jnp.take(emb_table, tie(jnp.where((ids >= 0) & (ids < vocab_loc), ids, 0)...]
    unnamed x51 -> x48, local copies, waits for them, and re-layouts: 44.9 us -> 46.2 us
  transfers between devices with their start and end apart: 20 -> 18, of which waited for: 9 -> 7; matrix products, arithmetic and copies ran while one was open for 13% -> 11% of each run, Pallas kernels for 35% -> 34%
where the time goes in v5:
time: 1990 us; the launch traced here: 1980 us
  Pallas kernels  1060 us (53%)
  waiting for transfers between devices  601 us (30%)
  local copies, waits for them, and re-layouts  147 us (7%)
  other arithmetic  142 us (7%)
    ppermute x12, waiting for transfers between devices, exchange(): return lax.ppermute(value, 'tp', SWAP)  518 us
    pallas_call x1, Pallas kernels, reduce_table(): pl.pallas_call(table_kernel, in_specs=[ANYWHERE], out_specs=ANYWHERE, out...  453 us
    pallas_call x3, Pallas kernels, ffn(): pl.pallas_call(functools.partial(ffn_kernel, base), grid=(count,), in_spe...  204 us
    pallas_call x3, Pallas kernels, attn_backward(): pl.pallas_call(functools.partial(attn_backward_kernel, head_dim, len(extr...  134 us
    pallas_call x5, Pallas kernels, outer(): pl.pallas_call(outer_kernel, grid_spec=grid_spec, out_shape=[jax.ShapeDty...  125 us
    pallas_call x6, Pallas kernels, attn_forward(): pl.pallas_call(functools.partial(attn_forward_kernel, head_dim, len(extra...  125 us
    scatter-add x2, other arithmetic, add_rows(): return grad.at[ids.reshape(-1)].add(rows.reshape(-1, width), mode='drop')  108 us
    reduce_scatter x2, waiting for transfers between devices, reduce_gradient(): lax.psum_scatter(grad.reshape(-1, grad.shape[2]), ('tp', 'dp'), scatter_d...  82.5 us
  transfers between devices with their start and end apart: 18, of which 7 were waited for; matrix products, arithmetic and copies ran while one was open for 11% of the time, Pallas kernels for 34%

profile of v5, /device:TPU:0, one launch (start us, length us, event | category | flops | bytes accessed | tf_op | source)
XLA Modules:
  0.0 1981.2 jit_solution(8459731188332983222)
XLA Ops:
  12.7 13.3 collective-permute-done.1
  31.5 38.0 %collective-permute-done.8 = f32[96,4608]{1,0:T(8,128)S(1)} collective-permute-done((f32[96,4608]{1,0:T(8,128)S(1)}, f32[96,4608]{1,0:T(8,128)S(1)}, u32[]{:S(2)}, u32[]{:S(2)}) %collective-permute-start.8) | collective-permute-done | bytes 1769504 | tf_op jit(solution)/shard_map/ppermute | solution.py:674
  71.5 31.7 %gather_fusion = bf16[4096,768]{1,0:T(8,128)(2,1)} fusion(bf16[15296,768]{1,0:T(8,128)(2,1)} %param.20, s32[4096]{0:T(1024)S(1)} %broadcast_clamp_fusion.1), kind=kCustom, calls=%fused_computation.clone | custom fusion | bytes 12599296 | tf_op jit(solution)/shard_map/jit(_take)/gather | solution.py:669
  112.5 30.0 %gather_fusion.1 = bf16[4096,768]{1,0:T(8,128)(2,1)} fusion(bf16[15296,768]{1,0:T(8,128)(2,1)} %param.20, s32[4096]{0:T(1024)S(1)} %broadcast_clamp_fusion), kind=kCustom, calls=%fused_computation.1.clone | custom fusion | bytes 12599296 | tf_op jit(solution)/shard_map/jit(_take)/gather | solution.py:669
  171.9 86.3 %collective-permute-done.2 = f32[1,4224]{1,0:T(1,128)S(1)} collective-permute-done((f32[1,4224]{1,0:T(1,128)S(1)}, f32[1,4224]{1,0:T(1,128)S(1)}, u32[]{:S(2)}, u32[]{:S(2)}) %collective-permute-start.2) | collective-permute-done | bytes 16928 | tf_op jit(solution)/shard_map/ppermute | solution.py:674
  268.5 17.3 attn_forward.6
  285.9 73.6 %collective-permute-done.6.refs_1_ = f32[1,512,768]{2,1,0:T(8,128)} collective-permute-done((f32[1,512,768]{2,1,0:T(8,128)}, f32[1,512,768]{2,1,0:T(8,128)}, u32[]{:S(2)}, u32[]{:S(2)}) %collective-permute-start.6) | collective-permute-done | bytes 1572896 | tf_op jit(solution)/shard_map/ppermute | solution.py:674
  359.4 16.5 attn_forward.7
  376.0 12.4 join_weights.3
  388.4 52.8 %ffn.3 = (bf16[4096,3072]{1,0:T(8,128)(2,1)}, bf16[4096,3072]{1,0:T(8,128)(2,1)}, bf16[4096,3072]{1,0:T(8,128)(2,1)}, bf16[8,512,768]{2,1,0:T(8,128)(2,1)}, f32[...) custom-call(bf16[8,512,768]{2,1,0:T(8,128)(2,1)} %get-tuple-element., ...), custom_call_target="tpu_custom_call" | custom-call | flops 43486543872 | bytes 28000000 | tf_op jit(solution)/shard_map/ffn/pallas_call | solution.py:368
  441.2 16.7 attn_forward.8
  457.9 16.5 attn_forward.9
  474.4 53.2 %ffn.4 = (bf16[4096,3072]{1,0:T(8,128)(2,1)}, bf16[4096,3072]{1,0:T(8,128)(2,1)}, bf16[4096,3072]{1,0:T(8,128)(2,1)}, bf16[8,512,768]{2,1,0:T(8,128)(2,1)}, f32[...) custom-call(bf16[8,512,768]{2,1,0:T(8,128)(2,1)} %get-tuple-element., ...), custom_call_target="tpu_custom_call", output_to_operand_aliasing={{0}: (12, {}), {1}: (13, {}), {2}: (14, {}), {3}: (15, {}),... | custom-call | flops 43486543872 | bytes 28000000 | tf_op jit(solution)/shard_map/ffn/pallas_call | solution.py:368
  527.7 29.0 %attn_forward.10 = (bf16[8,512,768]{2,1,0:T(8,128)(2,1)}, bf16[8,512,2304]{2,1,0:T(8,128)(2,1)}, bf16[8,12,768,256]{3,2,1,0:T(8,128)(2,1)}, bf16[8,512,768]{2,1,...) custom-call(bf16[4,512,768]{2,1,0:T(8,128)(2,1)} %get-tuple-element., ...), custom_call_target="tpu_custom_call", output_to_operand_aliasing={{0}: (10, {}), {1}: (11, {}), {2}: (12, {}), {3}: (13, {}),... | custom-call | flops 12884901888 | bytes 24000000 | tf_op jit(solution)/shard_map/attn_forward/pallas_call | solution.py:345
  556.7 29.2 %attn_forward.11 = (bf16[8,512,768]{2,1,0:T(8,128)(2,1)}, bf16[8,512,2304]{2,1,0:T(8,128)(2,1)}, bf16[8,12,768,256]{3,2,1,0:T(8,128)(2,1)}, bf16[8,512,768]{2,1,...) custom-call(bf16[4,512,768]{2,1,0:T(8,128)(2,1)} %get-tuple-element., ...), custom_call_target="tpu_custom_call", output_to_operand_aliasing={{0}: (10, {}), {1}: (11, {}), {2}: (12, {}), {3}: (13, {}),... | custom-call | flops 12884901888 | bytes 24000000 | tf_op jit(solution)/shard_map/attn_forward/pallas_call | solution.py:345
  585.9 63.6 %attn_backward.3 = (f32[4,512,768]{2,1,0:T(8,128)}, bf16[8,512,2304]{2,1,0:T(8,128)(2,1)}, f32[8,512,768]{2,1,0:T(8,128)}, f32[8,2304]{1,0:T(8,128)}, f32[8,128]{1,0:T(8,128)}) custom-call(f32[8,512,768]{2,1,0:T(8,128)} %get-tuple-element.183.refs_0_.refs_4_, bf16[8,512,768]{2,1,0:T(8,128)(2,1)} %get-tuple-element.184.refs_1_.refs_5_, ...), custom_call_target="tpu_custom_call" | custom-call | flops 32212254720 | bytes 48000000 | tf_op jit(solution)/shard_map/attn_backward/pallas_call | solution.py:393
  649.6 97.7 %ffn.5 = (bf16[4096,3072]{1,0:T(8,128)(2,1)}, bf16[4096,3072]{1,0:T(8,128)(2,1)}, bf16[4096,3072]{1,0:T(8,128)(2,1)}, bf16[8,512,768]{2,1,0:T(8,128)(2,1)}, f32[...) custom-call(bf16[8,512,768]{2,1,0:T(8,128)(2,1)} %get-tuple-element., ...), custom_call_target="tpu_custom_call", output_to_operand_aliasing={{0}: (12, {}), {1}: (13, {}), {2}: (14, {}), {3}: (15, {}),... | custom-call | flops 86973087744 | bytes 56000000 | tf_op jit(solution)/shard_map/ffn/pallas_call | solution.py:368
  751.5 28.2 %outer.5 = (f32[2,768,4608]{2,1,0:T(8,128)}, f32[8,128]{1,0:T(8,128)}) custom-call(s32[1]{0:T(128)} %bitcast.7.own_ref, bf16[4096,768]{1,0:T(8,128)(2,1)} %bitcast.63, bf16[4096,3072]{1,0:T(8,128)(2,1)} %get-tuple-element.196.right_ref, f32[8,128]{1,0:T(8,128)} %get-tuple-element.197.refs_0_), custom_call_target="tpu_custom_call" | custom-call | flops 19327352832 | bytes 40894464 | tf_op jit(solution)/shard_map/outer/pallas_call | solution.py:437
  779.7 28.2 %outer.6 = (f32[2,768,4608]{2,1,0:T(8,128)}, f32[8,128]{1,0:T(8,128)}) custom-call(s32[1]{0:T(128)} %bitcast.7.own_ref, bf16[4096,768]{1,0:T(8,128)(2,1)} %bitcast.64, bf16[4096,3072]{1,0:T(8,128)(2,1)} %get-tuple-element.195.right_ref, f32[2,768,4608]{2,1,0:T(8,128)} %get-tuple-element.198.refs_0_, ...), custom_call_target="tpu_custom_call", output_to_operand_aliasing={{0}: (3, {})} | custom-call | flops 19327352832 | bytes 40894464 | tf_op jit(solution)/shard_map/outer/pallas_call | solution.py:437
  807.9 28.6 %outer.7 = (f32[2,768,4608]{2,1,0:T(8,128)}, f32[8,128]{1,0:T(8,128)}) custom-call(s32[1]{0:T(128)} %bitcast.7.own_ref, bf16[4096,768]{1,0:T(8,128)(2,1)} %bitcast.100, bf16[4096,3072]{1,0:T(8,128)(2,1)} %get-tuple-element.194.right_ref, f32[2,768,4608]{2,1,0:T(8,128)} %get-tuple-element.200.refs_0_, ...), custom_call_target="tpu_custom_call", output_to_operand_aliasing={{0}: (3, {})} | custom-call | flops 19327352832 | bytes 40894464 | tf_op jit(solution)/shard_map/outer/pallas_call | solution.py:437
  836.5 35.4 %attn_backward.4 = (f32[2,512,768]{2,1,0:T(8,128)}, bf16[8,512,2304]{2,1,0:T(8,128)(2,1)}, f32[8,512,768]{2,1,0:T(8,128)}, f32[8,2304]{1,0:T(8,128)}, f32[8,128]{1,0:T(8,128)}) custom-call(f32[8,512,768]{2,1,0:T(8,128)} %get-tuple-element.189.refs_0_, bf16[8,512,768]{2,1,0:T(8,128)(2,1)} %get-tuple-element.190.refs_1_, ...), custom_call_target="tpu_custom_call", output_to_operand_aliasing={{1}: (8, {}), {2}: (9, {})} | custom-call | flops 16106127360 | bytes 24000000 | tf_op jit(solution)/shard_map/attn_backward/pallas_call | solution.py:393
  871.9 35.3 %attn_backward.5 = (f32[2,512,768]{2,1,0:T(8,128)}, bf16[8,512,2304]{2,1,0:T(8,128)(2,1)}, f32[8,512,768]{2,1,0:T(8,128)}, f32[8,2304]{1,0:T(8,128)}, f32[8,128]{1,0:T(8,128)}) custom-call(f32[8,512,768]{2,1,0:T(8,128)} %get-tuple-element.189.refs_0_, bf16[8,512,768]{2,1,0:T(8,128)(2,1)} %get-tuple-element.190.refs_1_, ...), custom_call_target="tpu_custom_call", output_to_operand_aliasing={{1}: (8, {}), {2}: (9, {})} | custom-call | flops 16106127360 | bytes 24000000 | tf_op jit(solution)/shard_map/attn_backward/pallas_call | solution.py:393
  909.7 14.0 outer.8
  923.8 26.2 %outer.9 = (f32[2,832,1536]{2,1,0:T(8,128)}, f32[8,128]{1,0:T(8,128)}) custom-call(s32[1]{0:T(128)} %bitcast.7.own_ref, bf16[4096,768]{1,0:T(8,128)(2,1)} %bitcast.61, bf16[4096,2304]{1,0:T(8,128)(2,1)} %bitcast.65, f32[2,832,1536]{2,1,0:T(8,128)} %get-tuple-element.214.refs_0_, f32[8,128]{1,0:T(8,128)} %get-tuple-element.215.refs_1_), custom_call_target="tpu_custom_call", output_to_operand_aliasing={{0}: (3, {})} | custom-call | flops 14495514624 | bytes 32243712 | tf_op jit(solution)/shard_map/outer/pallas_call | solution.py:437
  952.3 82.5 %reduce-scatter.7.cloned.1.call-done = f32[104,1536]{1,0:T(8,128)} async-done(((f32[1664,1536]{1,0:T(8,128)}), f32[104,1536]{1,0:T(8,128)}) %reduce-scatter.7.cloned.1.call-update) | async-done | bytes 638992 | tf_op jit(solution)/shard_map/reduce_scatter | solution.py:638
  1038.5 50.4 %scatter_custom_fusion = f32[15296,768]{1,0:T(8,128)} fusion(s32[4096]{0:T(1024)S(1)} %bitcast.93, f32[4096,768]{1,0:T(8,128)} %bitcast.66, f32[]{:T(128)} %constant.22.clone.1), kind=kCustom, calls=%fused_computation.4 | custom fusion | flops 3145728 | bytes 46989824 | tf_op jit(solution)/shard_map/scatter-add | solution.py:778
  1088.9 240.5 %collective-permute-done.11 = f32[2,512,768]{2,1,0:T(8,128)S(1)} collective-permute-done((f32[2,512,768]{2,1,0:T(8,128)}, f32[2,512,768]{2,1,0:T(8,128)S(1)}, u32[]{:S(2)}, u32[]{:S(2)}) %collective-permute-start.11) | collective-permute-done | bytes 3145760 | tf_op jit(solution)/shard_map/ppermute | solution.py:674
  1329.4 66.2 %collective-permute-done.10 = f32[2,512,768]{2,1,0:T(8,128)} collective-permute-done((f32[2,512,768]{2,1,0:T(8,128)}, f32[2,512,768]{2,1,0:T(8,128)}, u32[]{:S(2)}, u32[]{:S(2)}) %collective-permute-start.10) | collective-permute-done | bytes 3145760 | tf_op jit(solution)/shard_map/ppermute | solution.py:674
  1404.7 57.9 %scatter_fusion = f32[15296,768]{1,0:T(8,128)} fusion(f32[15296,768]{1,0:T(8,128)} %scatter_custom_fusion, s32[4096]{0:T(1024)S(1)} %bitcast.91, f32[4096,768]{1,0:T(8,128)} %bitcast.67), kind=kCustom, calls=%fused_computation.3 | custom fusion | flops 3145728 | bytes 37765120 | tf_op jit(solution)/shard_map/scatter-add | solution.py:778
  1462.7 452.6 %reduce_table.1 = f32[15296,768]{1,0:T(8,128)} custom-call(f32[15296,768]{1,0:T(8,128)} %scatter_fusion), custom_call_target="tpu_custom_call" | custom-call | flops 399999991808 | bytes 93978624 | tf_op jit(solution)/shard_map/reduce_table/pallas_call | solution.py:624
  1924.8 10.6 slice_bitcast_fusion
  1941.5 32.6 %copy.182 = f32[15296,768]{1,0:T(8,128)} copy(f32[15296,768]{1,0:T(8,128)} %reduce_table.1) | data formatting | bytes 93978624
  (142 shorter events, 98.9 us)
Async XLA Ops:
  7.2 63.6 %copy-start.6 = (s32[16,512]{1,0:T(8,128)S(1)}, s32[16,512]{1,0:T(8,128)}, u32[]{:S(2)}) copy-start(s32[16,512]{1,0:T(8,128)} %param.18) | copy-start | bytes 98308
  7.2 253.6 %all-gather.5.cloned.1.call-start = ((), (), s32[]{:S(2)}) async-start(), calls=%async_computation.2 | async-start | bytes 5308416 | tf_op jit(solution)/shard_map/all_gather | solution.py:678
  9.4 16.6 collective-permute-start.1
  26.9 349.1 %all-gather.7.cloned.1.call-start = ((), (), s32[]{:S(2)}) async-start(), calls=%async_computation.3 | async-start | bytes 15925248 | tf_op jit(solution)/shard_map/all_gather | solution.py:678
  29.7 39.8 %collective-permute-start.8 = (f32[96,4608]{1,0:T(8,128)S(1)}, f32[96,4608]{1,0:T(8,128)S(1)}, u32[]{:S(2)}, u32[]{:S(2)}) collective-permute-start(f32[96,4608]{1,0:T(8,128)S(1)} %maximum_convert_fusion), channel_id=1, source_target_pairs={{0,8},{8,0},{1,9},{9,1},{2,10},{10,2},{3,11},{11,3},{4,12},{12,4},... | collective-permute-start | bytes 5308424 | tf_op jit(solution)/shard_map/ppermute | solution.py:674
  70.7 964.1 %reduce-scatter.7.cloned.1.call-start = ((), (), s32[]{:S(2)}) async-start(), calls=%async_computation.6 | async-start | bytes 10862592 | tf_op jit(solution)/shard_map/reduce_scatter | solution.py:638
  70.8 32.4 %copy-start.4 = (pred[16,512]{1,0:T(8,128)(4,1)}, pred[16,512]{1,0:T(8,128)(4,1)S(1)}, u32[]{:S(2)}) copy-start(pred[16,512]{1,0:T(8,128)(4,1)S(1)} %get-tuple-element.271) | copy-start | bytes 24580
  142.5 11.2 slice-start
  147.0 6.7 slice-start.1
  153.0 4.9 copy-start.7
  153.0 4.9 copy-start.8
  153.0 4.9 copy-start.9
  153.0 403.8 %collective-permute-start = (f32[2,512,768]{2,1,0:T(8,128)}, f32[2,512,768]{2,1,0:T(8,128)}, u32[]{:S(2)}, u32[]{:S(2)}) collective-permute-start(f32[2,512,768]{2,1,0:T(8,128)} %get-tuple-element.281), channel_id=1, source_target_pairs={{0,8},{8,0},{1,9},{9,1},{2,10},{10,2},{3,11},{11,3},{4,12},{12,4},... | collective-permute-start | bytes 9437192 | tf_op jit(solution)/shard_map/ppermute | solution.py:674
  156.5 110.7 %collective-permute-start.7 = (f32[1,512,768]{2,1,0:T(8,128)}, f32[1,512,768]{2,1,0:T(8,128)}, u32[]{:S(2)}, u32[]{:S(2)}) collective-permute-start(f32[1,512,768]{2,1,0:T(8,128)} %get-tuple-element.276), channel_id=1, source_target_pairs={{0,8},{8,0},{1,9},{9,1},{2,10},{10,2},{3,11},{11,3},{4,12},{12,4},... | collective-permute-start | bytes 4718600 | tf_op jit(solution)/shard_map/ppermute | solution.py:674
  158.0 100.2 %collective-permute-start.2 = (f32[1,4224]{1,0:T(1,128)S(1)}, f32[1,4224]{1,0:T(1,128)S(1)}, u32[]{:S(2)}, u32[]{:S(2)}) collective-permute-start(f32[1,4224]{1,0:T(1,128)S(1)} %maximum_convert_fusion.2), channel_id=1, source_target_pairs={{0,8},{8,0},{1,9},{9,1},{2,10},{10,2},{3,11},{11,3},{4,12},{12,4},... | collective-permute-start | bytes 50696 | tf_op jit(solution)/shard_map/ppermute | solution.py:674
  158.7 368.9 %collective-permute-start.3 = (f32[2,512,768]{2,1,0:T(8,128)}, f32[2,512,768]{2,1,0:T(8,128)}, u32[]{:S(2)}, u32[]{:S(2)}) collective-permute-start(f32[2,512,768]{2,1,0:T(8,128)} %get-tuple-element.280), channel_id=1, source_target_pairs={{0,8},{8,0},{1,9},{9,1},{2,10},{10,2},{3,11},{11,3},{4,12},{12,4},... | collective-permute-start | bytes 9437192 | tf_op jit(solution)/shard_map/ppermute | solution.py:674
  160.0 199.4 %collective-permute-start.6 = (f32[1,512,768]{2,1,0:T(8,128)}, f32[1,512,768]{2,1,0:T(8,128)}, u32[]{:S(2)}, u32[]{:S(2)}) collective-permute-start(f32[1,512,768]{2,1,0:T(8,128)} %get-tuple-element.277), channel_id=1, source_target_pairs={{0,8},{8,0},{1,9},{9,1},{2,10},{10,2},{3,11},{11,3},{4,12},{12,4},... | collective-permute-start | bytes 4718600 | tf_op jit(solution)/shard_map/ppermute | solution.py:674
  161.8 7.2 copy-start.10
  161.8 7.8 copy-start.11
  161.8 8.3 copy-start.12
  161.8 8.9 copy-start.13
  161.8 9.5 copy-start.14
  258.2 199.7 %collective-permute-start.4 = (f32[1,512,768]{2,1,0:T(8,128)}, f32[1,512,768]{2,1,0:T(8,128)}, u32[]{:S(2)}, u32[]{:S(2)}) collective-permute-start(f32[1,512,768]{2,1,0:T(8,128)} %get-tuple-element.279), channel_id=1, source_target_pairs={{0,8},{8,0},{1,9},{9,1},{2,10},{10,2},{3,11},{11,3},{4,12},{12,4},... | collective-permute-start | bytes 4718600 | tf_op jit(solution)/shard_map/ppermute | solution.py:674
  267.2 173.9 %collective-permute-start.5 = (f32[1,512,768]{2,1,0:T(8,128)}, f32[1,512,768]{2,1,0:T(8,128)}, u32[]{:S(2)}, u32[]{:S(2)}) collective-permute-start(f32[1,512,768]{2,1,0:T(8,128)} %get-tuple-element.278), channel_id=1, source_target_pairs={{0,8},{8,0},{1,9},{9,1},{2,10},{10,2},{3,11},{11,3},{4,12},{12,4},... | collective-permute-start | bytes 4718600 | tf_op jit(solution)/shard_map/ppermute | solution.py:674
  951.6 511.1 %reduce-scatter.9.cloned.1.call-start = ((), (), s32[]{:S(2)}) async-start(), calls=%async_computation.7 | async-start | bytes 30081024 | tf_op jit(solution)/shard_map/reduce_scatter | solution.py:638
  951.7 86.7 %copy-start.3 = (s32[16,512]{1,0:T(8,128)S(1)}, s32[16,512]{1,0:T(8,128)}, u32[]{:S(2)}) copy-start(s32[16,512]{1,0:T(8,128)} %copy-done.2) | copy-start | bytes 98308
  951.7 86.7 %copy-start.5 = (pred[16,512]{1,0:T(8,128)(4,1)S(1)}, pred[16,512]{1,0:T(8,128)(4,1)}, u32[]{:S(2)}) copy-start(pred[16,512]{1,0:T(8,128)(4,1)} %copy-done.4) | copy-start | bytes 24580
  952.2 963.1 %all-gather.9.cloned.1.call-start = ((), (), s32[]{:S(2)}) async-start(), calls=%async_computation.4 | async-start | bytes 5750784 | tf_op jit(solution)/shard_map/all_gather | solution.py:639
  1034.8 890.0 %all-gather.11.cloned.1.call-start = ((), (), s32[]{:S(2)}) async-start(), calls=%async_computation.5 | async-start | bytes 15925248 | tf_op jit(solution)/shard_map/all_gather | solution.py:639
  1034.9 360.7 %collective-permute-start.9 = (f32[4,512,768]{2,1,0:T(8,128)}, f32[4,512,768]{2,1,0:T(8,128)}, u32[]{:S(2)}, u32[]{:S(2)}) collective-permute-start(f32[4,512,768]{2,1,0:T(8,128)} %get-tuple-element.207), channel_id=1, source_target_pairs={{0,8},{8,0},{1,9},{9,1},{2,10},{10,2},{3,11},{11,3},{4,12},{12,4},... | collective-permute-start | bytes 18874376 | tf_op jit(solution)/shard_map/ppermute | solution.py:674
  1036.3 293.0 %collective-permute-start.11 = (f32[2,512,768]{2,1,0:T(8,128)}, f32[2,512,768]{2,1,0:T(8,128)S(1)}, u32[]{:S(2)}, u32[]{:S(2)}) collective-permute-start(f32[2,512,768]{2,1,0:T(8,128)} %get-tuple-element.209), channel_id=1, source_target_pairs={{0,8},{8,0},{1,9},{9,1},{2,10},{10,2},{3,11},{11,3},{4,12},{12,4},... | collective-permute-start | bytes 9437192 | tf_op jit(solution)/shard_map/ppermute | solution.py:674
  1036.9 358.7 %collective-permute-start.10 = (f32[2,512,768]{2,1,0:T(8,128)}, f32[2,512,768]{2,1,0:T(8,128)}, u32[]{:S(2)}, u32[]{:S(2)}) collective-permute-start(f32[2,512,768]{2,1,0:T(8,128)} %get-tuple-element.208), channel_id=1, source_target_pairs={{0,8},{8,0},{1,9},{9,1},{2,10},{10,2},{3,11},{11,3},{4,12},{12,4},... | collective-permute-start | bytes 9437192 | tf_op jit(solution)/shard_map/ppermute | solution.py:674
  (3 other events, 2.6 us)
Sparse Core Ops, SparseCore 0:
  27.0 36.2 all-gather.4
  70.9 75.6 all-gather.6
  951.8 82.9 reduce-scatter.6
  1039.5 241.4 reduce-scatter.8
  1282.7 36.6 all-gather.8
  1462.8 103.4 all-gather.10

commit v6 on v4

--- a/solution.py
+++ b/solution.py
@@ -85,11 +85,11 @@
 
 
 def attn_forward_kernel(head_dim, alias_count, *refs):
-    (own_ref, other_ref, wqkv_ref, bqkv_ref, wo_ref, bo_ref, gain_ref, bias_ref, cos_ref, sin_ref) = refs[:10]
-    (emb_ref, qkv_ref, prob_ref, ctx_ref, hat_ref, rstd_ref, hid_ref, token_ref) = refs[10 + alias_count:]
+    (own_ref, other_ref, mask_ref, wqkv_ref, bqkv_ref, wo_ref, bo_ref, gain_ref, bias_ref, cos_ref, sin_ref) = refs[:11]
+    (emb_ref, qkv_ref, prob_ref, ctx_ref, hat_ref, rstd_ref, hid_ref, token_ref) = refs[11 + alias_count:]
     seq_len, width = own_ref.shape
     clear(token_ref)
-    emb_ref[...] = (full(own_ref).astype(F32) + full(other_ref)).astype(BF16)
+    emb_ref[...] = jnp.where(mask_ref[:, :1] > 0, full(own_ref).astype(F32), full(other_ref)).astype(BF16)
     low, mask_low, mask_high, first_half = lane_masks()
     score_scale = head_dim ** -0.5 * LOG2E
     causal = lax.broadcasted_iota(jnp.int32, (HALF_Q, HALF_Q), 0) <= lax.broadcasted_iota(jnp.int32, (HALF_Q, HALF_Q), 1)
@@ -146,7 +146,7 @@
     hid_ref[...] = (hat * full(gain_ref) + full(bias_ref)).astype(BF16)
 
 
-def ffn_kernel(base, hid_ref, cot_ref, hat_ref, rstd_ref, wg_ref, wl_ref, wd_ref, bg_ref, bl_ref, bd_ref, gain1_ref, gain2_ref,
+def ffn_kernel(base, half_ref, hid_ref, cot_ref, hat_ref, rstd_ref, wg_ref, wl_ref, wd_ref, bg_ref, bl_ref, bd_ref, gain1_ref, gain2_ref,
                *refs):
     (inner_out, gate_out, lin_out, dffn_ref, dres_ref, dattn_ref, narrow_ref, wide_ref, token_ref,
      act_buf, slope_buf, inner_buf, gate_buf, lin_buf, acc_buf, sems) = refs[-16:]
@@ -331,14 +331,14 @@
     return pl.BlockSpec(TOKEN, lambda i: (0, 0))
 
 
-def attn_forward(base, count, total, own, own_base, other, weights, tables, previous, deps, head_dim):
+def attn_forward(base, count, total, own, own_base, other, mask, weights, tables, previous, deps, head_dim):
     seq_len, width = own.shape[1:]
     wqkv = weights[0]
     heads = width // head_dim
     shapes = [((seq_len, width), BF16), ((seq_len, 3 * width), BF16), ((heads, seq_len * 3 // 2, HALF_Q), BF16), ((seq_len, width), BF16),
               ((seq_len, width), F32), ((seq_len, LANES), F32), ((seq_len, width), BF16)]
-    operands = (own, other) + tuple(weights) + tuple(tables)
-    specs = [per_seq((seq_len, width), own_base), per_seq((seq_len, width))] + [whole(item.shape) for item in operands[2:]]
+    operands = (own, other, mask) + tuple(weights) + tuple(tables)
+    specs = [per_seq((seq_len, width), own_base), per_seq((seq_len, width)), per_seq((seq_len, LANES), base)] + [whole(item.shape) for item in operands[3:]]
     extra = tuple(previous) if previous is not None else ()
     specs += [ANYWHERE] * (len(extra) + len(deps))
     flops = count * (2 * seq_len * width * (wqkv.shape[1] + width) + 4 * heads * seq_len * seq_len * 64)
@@ -355,30 +355,39 @@
     )(*operands, *extra, *deps)
 
 
-def ffn(base, count, hidden, cotangent, hat, rstd, weights, previous, deps):
+def ffn(base, count, hidden, cotangent, half_index, hat, rstd, weights, previous, deps):
     total, seq_len, width = hidden.shape
     wide = weights[0].shape[1]
     operands = (hidden, cotangent, hat, rstd) + tuple(weights)
     extra = tuple(previous) if previous is not None else ()
-    specs = [per_seq(item.shape[1:], base) for item in operands[:4]] + [whole(item.shape) for item in operands[4:]]
-    specs += [ANYWHERE] * (len(extra) + len(deps))
+
+    def seq_block(lanes, shift=0):
+        return pl.BlockSpec((None, seq_len, lanes), lambda i, half: (i + base + half[0] * shift, 0, 0))
+
+    def fixed(shape, **kwargs):
+        return pl.BlockSpec(shape, lambda i, half: (0, 0), **kwargs)
+
+    specs = [seq_block(width), seq_block(width, total), seq_block(width), seq_block(LANES)]
+    specs += [fixed(item.shape, pipeline_mode=pl.Buffered(1)) for item in weights] + [ANYWHERE] * (len(extra) + len(deps))
     big = jax.ShapeDtypeStruct((total * seq_len, wide), BF16)
     narrow = jax.ShapeDtypeStruct((total, seq_len, width), BF16)
-    flops = 12 * count * seq_len * width * wide
+    sums = ((5 * TILE, width), (2 * TILE, wide), TOKEN)
+    grid_spec = pltpu.PrefetchScalarGridSpec(
+        num_scalar_prefetch=1,
+        grid=(count,),
+        in_specs=specs,
+        out_specs=[ANYWHERE] * 3 + [seq_block(width)] * 3 + [fixed(shape) for shape in sums],
+        scratch_shapes=[pltpu.VMEM((seq_len, wide), F32)] * 2 + [pltpu.VMEM((seq_len, wide), BF16)] * 3
+        + [pltpu.VMEM((seq_len, width), F32), pltpu.SemaphoreType.DMA((3, wide // FFN_CHUNK))])
     return pl.pallas_call(
         functools.partial(ffn_kernel, base),
-        grid=(count,),
-        in_specs=specs,
-        out_specs=[ANYWHERE] * 3 + [per_seq((seq_len, width), base)] * 3 + [pl.BlockSpec((40, width), lambda i: (0, 0)), pl.BlockSpec((16, wide), lambda i: (0, 0)), token_spec()],
-        out_shape=[big] * 3 + [narrow, jax.ShapeDtypeStruct((total, seq_len, width), F32), narrow,
-                               jax.ShapeDtypeStruct((40, width), F32), jax.ShapeDtypeStruct((16, wide), F32), jax.ShapeDtypeStruct(TOKEN, F32)],
-        scratch_shapes=[pltpu.VMEM((seq_len, wide), F32)] * 2 + [pltpu.VMEM((seq_len, wide), BF16)] * 3
-        + [pltpu.VMEM((seq_len, width), F32), pltpu.SemaphoreType.DMA((3, wide // FFN_CHUNK))],
-        input_output_aliases={len(operands) + num: num for num in range(len(extra))},
+        grid_spec=grid_spec,
+        out_shape=[big] * 3 + [narrow, jax.ShapeDtypeStruct((total, seq_len, width), F32), narrow] + [jax.ShapeDtypeStruct(shape, F32) for shape in sums],
+        input_output_aliases={1 + len(operands) + num: num for num in range(len(extra))},
         compiler_params=params(),
-        cost_estimate=cost(int(1.5 * flops), count * 14_000_000),
+        cost_estimate=cost(18 * count * seq_len * width * wide, count * 14_000_000),
         name='ffn',
-    )(*operands, *extra, *deps)
+    )(half_index, *operands, *extra, *deps)
 
 
 def attn_backward(base, count, total, d_resid, d_attn, qkv, probs, weights, tables, previous, deps, head_dim):
@@ -660,11 +669,13 @@
         own_in = lax.dynamic_slice_in_dim(in_shard, tp_index * total, total)
         peer_ids = lax.dynamic_slice_in_dim(local_ids, (1 - tp_index) * total, total)
         peer_in = lax.dynamic_slice_in_dim(in_shard, (1 - tp_index) * total, total)
-        own_cot = lax.dynamic_slice_in_dim(cotangent, tp_index * total, total)
-
-        def rows_of(ids, inside):
-            rows = jnp.take(emb_table, jnp.where(inside, ids, 0), axis=0)
-            return jnp.where(inside[:, :, None], rows, 0.0)
+
+        own_mask = jnp.broadcast_to(own_in.astype(F32)[:, :, None], own_in.shape + (LANES,))
+
+        def rows_of(part, head):
+            ids = jnp.concatenate([peer_ids[part], own_ids[part]])
+            rows = jnp.take(emb_table, tie(jnp.clip(ids, 0, vocab_loc - 1), head), axis=0, mode='clip')
+            return rows
 
         def exchange(value):
             return lax.ppermute(value, 'tp', SWAP)
@@ -680,17 +691,19 @@
         qkv_loc, wide_loc = b_qkv.size, b_gate.shape[0]
         groups = [(num, 1) for num in range(half)] + groups_of(half, total, 2)
 
-        def both_halves(ids, inside, kind):
-            head = rows_of(ids[:half], inside[:half]).astype(kind)
-            return head, rows_of(tie(ids[half:], head), inside[half:]).astype(kind)
-
-        peer_halves = both_halves(peer_ids, peer_in, F32)
-        own_halves = both_halves(own_ids, own_in, BF16)
+        first_rows = rows_of(slice(half), tp_index)
+        halves = (first_rows, rows_of(slice(half, total), first_rows))
         front_peer = collect(shared_slice((w_qkv,), (w_out,), dp_index, parts))
-        wide_peer = collect(shared_slice((w_gate, w_lin), (w_down,), dp_index, parts))
-        arrived = [exchange(peer_halves[base // half][base % half:base % half + count]) for base, count in groups]
         own_bias = jnp.concatenate([row_of(b_qkv), row_of(b_gate), row_of(b_lin)], axis=1)
         biases = jnp.concatenate([own_bias, exchange(own_bias)])
+        wide_peer = collect(shared_slice((w_gate, w_lin), (w_down,), dp_index, parts))
+
+        def send_rows(base, count):
+            return exchange(halves[base // half][base % half:base % half + count].astype(F32))
+
+        arrived = [send_rows(*group) for group in groups[:half]]
+        halves = (first_rows, tie(halves[1], arrived[0]))
+        arrived += [send_rows(*group) for group in groups[half:]]
         bqkv_full = biases[:, :qkv_loc].reshape(1, -1)
         bgate_full = biases[:, qkv_loc:qkv_loc + wide_loc].reshape(1, -1)
         blin_full = biases[:, qkv_loc + wide_loc:].reshape(1, -1)
@@ -711,14 +724,14 @@
         def run_attention(num):
             nonlocal saved, deps
             base, count = groups[num]
-            out = attn_forward(base, count, total, own_halves[base // half], base % half, arrived[num], front, tables, saved, deps, head_dim)
+            out = attn_forward(base, count, total, halves[base // half], half + base % half, arrived[num], own_mask, front, tables, saved, deps, head_dim)
             *kept, token = out
             saved, deps = kept, (token,)
 
         def run_ffn(base, count):
             nonlocal ffn_saved, deps
             *_, hat, rstd, hidden = saved
-            *kept, narrow, wide, token = ffn(base, count, hidden, own_cot, hat, rstd, middle, ffn_saved, deps)
+            *kept, narrow, wide, token = ffn(base, count, hidden, cotangent, tp_index.reshape(1), hat, rstd, middle, ffn_saved, deps)
             ffn_saved, deps = kept, (token,)
             narrow_parts.append(narrow)
             wide_parts.append(wide)

time: 1910 us -> 1750 us (0.916)
  waiting for transfers between devices: 501 us -> 360 us
  local copies, waits for them, and re-layouts: 170 us -> 144 us
    ppermute x12, waiting for transfers between devices: 261 us -> 120 us  [exchange(): return lax.ppermute(value, 'tp', SWAP)]
    gather x4 -> x2, local copies, waits for them, and re-layouts: 80.6 us -> 61.6 us  [rows_of(): jnp.take(emb_table, tie(jnp.clip(ids, 0, vocab_loc - 1), head), axis=0, m...]
    unnamed x51 -> x47, local copies, waits for them, and re-layouts: 44.9 us -> 46.6 us
  transfers between devices with their start and end apart: 20 -> 20, of which waited for: 9 -> 7; matrix products, arithmetic and copies ran while one was open for 13% -> 12% of each run, Pallas kernels for 35% -> 39%
where the time goes in v6:
time: 1750 us; the launch traced here: 1740 us
  Pallas kernels  1070 us (61%)
  waiting for transfers between devices  360 us (21%)
  local copies, waits for them, and re-layouts  144 us (8%)
  other arithmetic  138 us (8%)
  starting transfers between devices  19.1 us (1%)
    pallas_call x1, Pallas kernels, reduce_table(): pl.pallas_call(table_kernel, in_specs=[ANYWHERE], out_specs=ANYWHERE, out...  453 us
    reduce_scatter x2, waiting for transfers between devices, reduce_gradient(): piece = lax.psum_scatter(grad, 'dp', scatter_dimension=0, tiled=True)  225 us
    pallas_call x3, Pallas kernels, ffn(): pl.pallas_call(functools.partial(ffn_kernel, base), grid_spec=grid_spec,...  204 us
    pallas_call x3, Pallas kernels, attn_backward(): pl.pallas_call(functools.partial(attn_backward_kernel, head_dim, len(extr...  135 us
    pallas_call x6, Pallas kernels, attn_forward(): pl.pallas_call(functools.partial(attn_forward_kernel, head_dim, len(extra...  130 us
    pallas_call x5, Pallas kernels, outer(): pl.pallas_call(outer_kernel, grid=(wide // block,), in_specs=[whole((rows...  126 us
    ppermute x12, waiting for transfers between devices, exchange(): return lax.ppermute(value, 'tp', SWAP)  120 us
    scatter-add x2, other arithmetic, add_rows(): return grad.at[ids.reshape(-1)].add(rows.reshape(-1, width), mode='drop')  105 us
  transfers between devices with their start and end apart: 20, of which 7 were waited for; matrix products, arithmetic and copies ran while one was open for 12% of the time, Pallas kernels for 39%

profile of v6, /device:TPU:0, one launch (start us, length us, event | category | flops | bytes accessed | tf_op | source)
XLA Modules:
  0.0 1741.4 jit_solution(7542854295300233203)
XLA Ops:
  12.7 13.3 collective-permute-done.2
  31.5 38.0 %collective-permute-done.8 = f32[96,4608]{1,0:T(8,128)S(1)} collective-permute-done((f32[96,4608]{1,0:T(8,128)S(1)}, f32[96,4608]{1,0:T(8,128)S(1)}, u32[]{:S(2)}, u32[]{:S(2)}) %collective-permute-start.8) | collective-permute-done | bytes 1769504 | tf_op jit(solution)/shard_map/ppermute | solution.py:681
  71.5 31.5 %gather_fusion = bf16[4096,768]{1,0:T(8,128)(2,1)} fusion(bf16[15296,768]{1,0:T(8,128)(2,1)} %param.18, s32[4096]{0:T(1024)S(1)} %broadcast_clamp_fusion), kind=kCustom, calls=%fused_computation | custom fusion | bytes 12599296 | tf_op jit(solution)/shard_map/jit(_take)/gather | solution.py:677
  119.4 30.1 %gather_fusion.1 = bf16[4096,768]{1,0:T(8,128)(2,1)} fusion(bf16[15296,768]{1,0:T(8,128)(2,1)} %param.18, s32[4096]{0:T(1024)S(1)} %broadcast_clamp_fusion.1), kind=kCustom, calls=%fused_computation.1 | custom fusion | bytes 12599296 | tf_op jit(solution)/shard_map/jit(_take)/gather | solution.py:677
  168.5 17.5 %attn_forward.6 = (bf16[8,512,768]{2,1,0:T(8,128)(2,1)}, bf16[8,512,2304]{2,1,0:T(8,128)(2,1)}, bf16[8,12,768,256]{3,2,1,0:T(8,128)(2,1)}, bf16[8,512,768]{2,1,0...) custom-call(bf16[8,512,768]{2,1,0:T(8,128)(2,1)} %bitcast.75, ...), custom_call_target="tpu_custom_call" | custom-call | flops 6442450944 | bytes 12000000 | tf_op jit(solution)/shard_map/attn_forward/pallas_call | solution.py:345
  186.0 17.7 %attn_forward.7 = (bf16[8,512,768]{2,1,0:T(8,128)(2,1)}, bf16[8,512,2304]{2,1,0:T(8,128)(2,1)}, bf16[8,12,768,256]{3,2,1,0:T(8,128)(2,1)}, bf16[8,512,768]{2,1,0...) custom-call(bf16[8,512,768]{2,1,0:T(8,128)(2,1)} %bitcast.76, ...), custom_call_target="tpu_custom_call", output_to_operand_aliasing={{0}: (11, {}), {1}: (12, {}), {2}: (13, {}), {3}: (14, {}),... | custom-call | flops 6442450944 | bytes 12000000 | tf_op jit(solution)/shard_map/attn_forward/pallas_call | solution.py:345
  203.7 12.4 join_weights.3
  216.1 52.8 %ffn.3 = (bf16[4096,3072]{1,0:T(8,128)(2,1)}, bf16[4096,3072]{1,0:T(8,128)(2,1)}, bf16[4096,3072]{1,0:T(8,128)(2,1)}, bf16[8,512,768]{2,1,0:T(8,128)(2,1)}, f32[...) custom-call(s32[1]{0:T(128)} %bitcast.1.half_ref, ...), custom_call_target="tpu_custom_call" | custom-call | flops 43486543872 | bytes 28000000 | tf_op jit(solution)/shard_map/ffn/pallas_call | solution.py:382
  268.9 17.9 %attn_forward.8 = (bf16[8,512,768]{2,1,0:T(8,128)(2,1)}, bf16[8,512,2304]{2,1,0:T(8,128)(2,1)}, bf16[8,12,768,256]{3,2,1,0:T(8,128)(2,1)}, bf16[8,512,768]{2,1,0...) custom-call(bf16[8,512,768]{2,1,0:T(8,128)(2,1)} %bitcast.77, ...), custom_call_target="tpu_custom_call", output_to_operand_aliasing={{0}: (11, {}), {1}: (12, {}), {2}: (13, {}), {3}: (14, {}),... | custom-call | flops 6442450944 | bytes 12000000 | tf_op jit(solution)/shard_map/attn_forward/pallas_call | solution.py:345
  286.8 17.5 %attn_forward.9 = (bf16[8,512,768]{2,1,0:T(8,128)(2,1)}, bf16[8,512,2304]{2,1,0:T(8,128)(2,1)}, bf16[8,12,768,256]{3,2,1,0:T(8,128)(2,1)}, bf16[8,512,768]{2,1,0...) custom-call(bf16[8,512,768]{2,1,0:T(8,128)(2,1)} %bitcast.78, ...), custom_call_target="tpu_custom_call", output_to_operand_aliasing={{0}: (11, {}), {1}: (12, {}), {2}: (13, {}), {3}: (14, {}),... | custom-call | flops 6442450944 | bytes 12000000 | tf_op jit(solution)/shard_map/attn_forward/pallas_call | solution.py:345
  304.3 53.0 %ffn.4 = (bf16[4096,3072]{1,0:T(8,128)(2,1)}, bf16[4096,3072]{1,0:T(8,128)(2,1)}, bf16[4096,3072]{1,0:T(8,128)(2,1)}, bf16[8,512,768]{2,1,0:T(8,128)(2,1)}, f32[...) custom-call(s32[1]{0:T(128)} %bitcast.1.half_ref, ...), custom_call_target="tpu_custom_call", output_to_operand_aliasing={{0}: (13, {}), {1}: (14, {}), {2}: (15, {}), {3}: (16, {}),... | custom-call | flops 43486543872 | bytes 28000000 | tf_op jit(solution)/shard_map/ffn/pallas_call | solution.py:382
  357.3 29.6 %attn_forward.10 = (bf16[8,512,768]{2,1,0:T(8,128)(2,1)}, bf16[8,512,2304]{2,1,0:T(8,128)(2,1)}, bf16[8,12,768,256]{3,2,1,0:T(8,128)(2,1)}, bf16[8,512,768]{2,1,...) custom-call(bf16[8,512,768]{2,1,0:T(8,128)(2,1)} %bitcast.80, ...), custom_call_target="tpu_custom_call", output_to_operand_aliasing={{0}: (11, {}), {1}: (12, {}), {2}: (13, {}), {3}: (14, {}),... | custom-call | flops 12884901888 | bytes 24000000 | tf_op jit(solution)/shard_map/attn_forward/pallas_call | solution.py:345
  387.0 29.8 %attn_forward.11 = (bf16[8,512,768]{2,1,0:T(8,128)(2,1)}, bf16[8,512,2304]{2,1,0:T(8,128)(2,1)}, bf16[8,12,768,256]{3,2,1,0:T(8,128)(2,1)}, bf16[8,512,768]{2,1,...) custom-call(bf16[8,512,768]{2,1,0:T(8,128)(2,1)} %bitcast.81, ...), custom_call_target="tpu_custom_call", output_to_operand_aliasing={{0}: (11, {}), {1}: (12, {}), {2}: (13, {}), {3}: (14, {}),... | custom-call | flops 12884901888 | bytes 24000000 | tf_op jit(solution)/shard_map/attn_forward/pallas_call | solution.py:345
  416.8 63.6 %attn_backward.3 = (f32[4,512,768]{2,1,0:T(8,128)}, bf16[8,512,2304]{2,1,0:T(8,128)(2,1)}, f32[8,512,768]{2,1,0:T(8,128)}, f32[8,2304]{1,0:T(8,128)}, f32[8,128]{1,0:T(8,128)}) custom-call(f32[8,512,768]{2,1,0:T(8,128)} %get-tuple-element.184.refs_0_.refs_4_, bf16[8,512,768]{2,1,0:T(8,128)(2,1)} %get-tuple-element.185.refs_1_.refs_5_, ...), custom_call_target="tpu_custom_call" | custom-call | flops 32212254720 | bytes 48000000 | tf_op jit(solution)/shard_map/attn_backward/pallas_call | solution.py:402
  480.4 97.9 %ffn.5 = (bf16[4096,3072]{1,0:T(8,128)(2,1)}, bf16[4096,3072]{1,0:T(8,128)(2,1)}, bf16[4096,3072]{1,0:T(8,128)(2,1)}, bf16[8,512,768]{2,1,0:T(8,128)(2,1)}, f32[...) custom-call(s32[1]{0:T(128)} %bitcast.1.half_ref, ...), custom_call_target="tpu_custom_call", output_to_operand_aliasing={{0}: (13, {}), {1}: (14, {}), {2}: (15, {}), {3}: (16, {}),... | custom-call | flops 86973087744 | bytes 56000000 | tf_op jit(solution)/shard_map/ffn/pallas_call | solution.py:382
  582.5 28.3 %outer.5 = (f32[768,9216]{1,0:T(8,128)}, f32[8,128]{1,0:T(8,128)}) custom-call(bf16[4096,768]{1,0:T(8,128)(2,1)} %bitcast.73, bf16[4096,3072]{1,0:T(8,128)(2,1)} %get-tuple-element.197.right_ref, f32[8,128]{1,0:T(8,128)} %get-tuple-element.198.refs_0_), custom_call_target="tpu_custom_call" | custom-call | flops 19327352832 | bytes 40894464 | tf_op jit(solution)/shard_map/outer/pallas_call | solution.py:439
  610.8 28.2 %outer.6 = (f32[768,9216]{1,0:T(8,128)}, f32[8,128]{1,0:T(8,128)}) custom-call(bf16[4096,768]{1,0:T(8,128)(2,1)} %bitcast.74, bf16[4096,3072]{1,0:T(8,128)(2,1)} %get-tuple-element.196.right_ref, f32[768,9216]{1,0:T(8,128)} %get-tuple-element.199.refs_0_, f32[8,128]{1,0:T(8,128)} %get-tuple-element.200.refs_1_), custom_call_target="tpu_custom_call", output_to_operand_aliasing={{0}: (2, {})} | custom-call | flops 19327352832 | bytes 40894464 | tf_op jit(solution)/shard_map/outer/pallas_call | solution.py:439
  639.0 28.3 %outer.7 = (f32[768,9216]{1,0:T(8,128)}, f32[8,128]{1,0:T(8,128)}) custom-call(bf16[4096,768]{1,0:T(8,128)(2,1)} %bitcast.111, bf16[4096,3072]{1,0:T(8,128)(2,1)} %get-tuple-element.195.right_ref, f32[768,9216]{1,0:T(8,128)} %get-tuple-element.201.refs_0_, f32[8,128]{1,0:T(8,128)} %get-tuple-element.202.refs_1_), custom_call_target="tpu_custom_call", output_to_operand_aliasing={{0}: (2, {})} | custom-call | flops 19327352832 | bytes 40894464 | tf_op jit(solution)/shard_map/outer/pallas_call | solution.py:439
  667.3 35.5 %attn_backward.4 = (f32[2,512,768]{2,1,0:T(8,128)}, bf16[8,512,2304]{2,1,0:T(8,128)(2,1)}, f32[8,512,768]{2,1,0:T(8,128)}, f32[8,2304]{1,0:T(8,128)}, f32[8,128]{1,0:T(8,128)}) custom-call(f32[8,512,768]{2,1,0:T(8,128)} %get-tuple-element.190.refs_0_, bf16[8,512,768]{2,1,0:T(8,128)(2,1)} %get-tuple-element.191.refs_1_, ...), custom_call_target="tpu_custom_call", output_to_operand_aliasing={{1}: (8, {}), {2}: (9, {})} | custom-call | flops 16106127360 | bytes 24000000 | tf_op jit(solution)/shard_map/attn_backward/pallas_call | solution.py:402
  702.9 35.5 %attn_backward.5 = (f32[2,512,768]{2,1,0:T(8,128)}, bf16[8,512,2304]{2,1,0:T(8,128)(2,1)}, f32[8,512,768]{2,1,0:T(8,128)}, f32[8,2304]{1,0:T(8,128)}, f32[8,128]{1,0:T(8,128)}) custom-call(f32[8,512,768]{2,1,0:T(8,128)} %get-tuple-element.190.refs_0_, bf16[8,512,768]{2,1,0:T(8,128)(2,1)} %get-tuple-element.191.refs_1_, ...), custom_call_target="tpu_custom_call", output_to_operand_aliasing={{1}: (8, {}), {2}: (9, {})} | custom-call | flops 16106127360 | bytes 24000000 | tf_op jit(solution)/shard_map/attn_backward/pallas_call | solution.py:402
  741.7 13.9 outer.8
  755.6 27.6 %outer.9 = (f32[832,3072]{1,0:T(8,128)}, f32[8,128]{1,0:T(8,128)}) custom-call(bf16[4096,768]{1,0:T(8,128)(2,1)} %bitcast.71, bf16[4096,2304]{1,0:T(8,128)(2,1)} %bitcast.82, f32[832,3072]{1,0:T(8,128)} %get-tuple-element.215.refs_0_, f32[8,128]{1,0:T(8,128)} %get-tuple-element.216.refs_1_), custom_call_target="tpu_custom_call", output_to_operand_aliasing={{0}: (2, {})} | custom-call | flops 14495514624 | bytes 32243712 | tf_op jit(solution)/shard_map/outer/pallas_call | solution.py:439
  785.3 74.4 %reduce-scatter.3.cloned.1.call-done = f32[104,3072]{1,0:T(8,128)} async-done(((f32[832,3072]{1,0:T(8,128)}), f32[104,3072]{1,0:T(8,128)}) %reduce-scatter.3.cloned.1.call-update) | async-done | bytes 1277968 | tf_op jit(solution)/shard_map/reduce_scatter | solution.py:643
  862.3 14.5 collective-permute-done.12
  882.6 150.5 %reduce-scatter.5.cloned.1.call-done = f32[96,9216]{1,0:T(8,128)} async-done(((f32[768,9216]{1,0:T(8,128)}), f32[96,9216]{1,0:T(8,128)}) %reduce-scatter.5.cloned.1.call-update) | async-done | bytes 3538960 | tf_op jit(solution)/shard_map/reduce_scatter | solution.py:643
  1037.4 46.9 %scatter_custom_fusion = f32[15296,768]{1,0:T(8,128)} fusion(s32[4096]{0:T(1024)S(1)} %bitcast.104, f32[4096,768]{1,0:T(8,128)} %bitcast.83, f32[]{:T(128)} %constant.14.clone.1), kind=kCustom, calls=%fused_computation.4 | custom fusion | flops 3145728 | bytes 46989824 | tf_op jit(solution)/shard_map/scatter-add | solution.py:788
  1085.1 67.5 %collective-permute-done.10 = f32[2,512,768]{2,1,0:T(8,128)} collective-permute-done((f32[2,512,768]{2,1,0:T(8,128)}, f32[2,512,768]{2,1,0:T(8,128)}, u32[]{:S(2)}, u32[]{:S(2)}) %collective-permute-start.10) | collective-permute-done | bytes 3145760 | tf_op jit(solution)/shard_map/ppermute | solution.py:681
  1152.6 9.2 pad_maximum_fusion
  1161.8 58.1 %scatter_fusion = f32[15296,768]{1,0:T(8,128)} fusion(f32[15296,768]{1,0:T(8,128)} %scatter_custom_fusion, s32[4096]{0:T(1024)S(1)} %bitcast.102, f32[4096,768]{1,0:T(8,128)} %bitcast.84), kind=kCustom, calls=%fused_computation.3 | custom fusion | flops 3145728 | bytes 37765120 | tf_op jit(solution)/shard_map/scatter-add | solution.py:788
  1222.8 452.5 %reduce_table.1 = f32[15296,768]{1,0:T(8,128)} custom-call(f32[15296,768]{1,0:T(8,128)} %scatter_fusion), custom_call_target="tpu_custom_call" | custom-call | flops 399999991808 | bytes 93978624 | tf_op jit(solution)/shard_map/reduce_table/pallas_call | solution.py:629
  1684.8 10.6 slice_bitcast_fusion
  1701.4 32.6 %copy.155 = f32[15296,768]{1,0:T(8,128)} copy(f32[15296,768]{1,0:T(8,128)} %reduce_table.1) | data formatting | bytes 93978624
  (143 shorter events, 89.6 us)
Async XLA Ops:
  7.2 63.6 %copy-start.7 = (s32[16,512]{1,0:T(8,128)S(1)}, s32[16,512]{1,0:T(8,128)}, u32[]{:S(2)}) copy-start(s32[16,512]{1,0:T(8,128)} %param.16) | copy-start | bytes 98308
  7.2 152.3 %all-gather.5.cloned.1.call-start = ((), (), s32[]{:S(2)}) async-start(), calls=%async_computation.2 | async-start | bytes 5308416 | tf_op jit(solution)/shard_map/all_gather | solution.py:685
  9.4 16.6 collective-permute-start.2
  26.9 176.8 %all-gather.7.cloned.1.call-start = ((), (), s32[]{:S(2)}) async-start(), calls=%async_computation.3 | async-start | bytes 15925248 | tf_op jit(solution)/shard_map/all_gather | solution.py:685
  29.7 39.8 %collective-permute-start.8 = (f32[96,4608]{1,0:T(8,128)S(1)}, f32[96,4608]{1,0:T(8,128)S(1)}, u32[]{:S(2)}, u32[]{:S(2)}) collective-permute-start(f32[96,4608]{1,0:T(8,128)S(1)} %maximum_convert_fusion), channel_id=1, source_target_pairs={{0,8},{8,0},{1,9},{9,1},{2,10},{10,2},{3,11},{11,3},{4,12},{12,4},... | collective-permute-start | bytes 5308424 | tf_op jit(solution)/shard_map/ppermute | solution.py:681
  70.7 789.0 %reduce-scatter.3.cloned.1.call-start = ((), (), s32[]{:S(2)}) async-start(), calls=%async_computation.4 | async-start | bytes 11501568 | tf_op jit(solution)/shard_map/reduce_scatter | solution.py:643
  70.8 45.0 %copy-start.5 = (pred[16,512]{1,0:T(8,128)(4,1)}, pred[16,512]{1,0:T(8,128)(4,1)S(1)}, u32[]{:S(2)}) copy-start(pred[16,512]{1,0:T(8,128)(4,1)S(1)} %get-tuple-element.246) | copy-start | bytes 24580
  103.0 6.4 copy-start.9
  103.0 6.4 copy-start.10
  103.0 13.4 copy-start.11
  103.0 14.0 copy-start.12
  103.0 14.6 copy-start.13
  103.0 15.2 copy-start.14
  103.0 15.7 copy-start.15
  108.0 43.3 %collective-permute-start = (f32[1,512,768]{2,1,0:T(8,128)S(1)}, f32[1,512,768]{2,1,0:T(8,128)S(1)}, u32[]{:S(2)}, u32[]{:S(2)}) collective-permute-start(f32[1,512,768]{2,1,0:T(8,128)S(1)} %get-tuple-element.254), channel_id=1, source_target_pairs={{0,8},{8,0},{1,9},{9,1},{2,10},{10,2},{3,11},{11,3},{4,12},{12,4},... | collective-permute-start | bytes 4718600 | tf_op jit(solution)/shard_map/ppermute | solution.py:681
  109.4 40.0 %collective-permute-start.3 = (f32[1,4224]{1,0:T(1,128)S(1)}, f32[1,4224]{1,0:T(1,128)S(1)}, u32[]{:S(2)}, u32[]{:S(2)}) collective-permute-start(f32[1,4224]{1,0:T(1,128)S(1)} %maximum_convert_fusion.2), channel_id=1, source_target_pairs={{0,8},{8,0},{1,9},{9,1},{2,10},{10,2},{3,11},{11,3},{4,12},{12,4},... | collective-permute-start | bytes 50696 | tf_op jit(solution)/shard_map/ppermute | solution.py:681
  110.3 75.7 %collective-permute-start.7 = (f32[1,512,768]{2,1,0:T(8,128)}, f32[1,512,768]{2,1,0:T(8,128)}, u32[]{:S(2)}, u32[]{:S(2)}) collective-permute-start(f32[1,512,768]{2,1,0:T(8,128)} %get-tuple-element.251), channel_id=1, source_target_pairs={{0,8},{8,0},{1,9},{9,1},{2,10},{10,2},{3,11},{11,3},{4,12},{12,4},... | collective-permute-start | bytes 4718600 | tf_op jit(solution)/shard_map/ppermute | solution.py:681
  111.5 157.4 %collective-permute-start.6 = (f32[1,512,768]{2,1,0:T(8,128)}, f32[1,512,768]{2,1,0:T(8,128)}, u32[]{:S(2)}, u32[]{:S(2)}) collective-permute-start(f32[1,512,768]{2,1,0:T(8,128)} %get-tuple-element.252), channel_id=1, source_target_pairs={{0,8},{8,0},{1,9},{9,1},{2,10},{10,2},{3,11},{11,3},{4,12},{12,4},... | collective-permute-start | bytes 4718600 | tf_op jit(solution)/shard_map/ppermute | solution.py:681
  112.3 174.6 %collective-permute-start.5 = (f32[1,512,768]{2,1,0:T(8,128)}, f32[1,512,768]{2,1,0:T(8,128)}, u32[]{:S(2)}, u32[]{:S(2)}) collective-permute-start(f32[1,512,768]{2,1,0:T(8,128)} %get-tuple-element.253), channel_id=1, source_target_pairs={{0,8},{8,0},{1,9},{9,1},{2,10},{10,2},{3,11},{11,3},{4,12},{12,4},... | collective-permute-start | bytes 4718600 | tf_op jit(solution)/shard_map/ppermute | solution.py:681
  157.4 199.9 %collective-permute-start.4 = (f32[2,512,768]{2,1,0:T(8,128)}, f32[2,512,768]{2,1,0:T(8,128)}, u32[]{:S(2)}, u32[]{:S(2)}) collective-permute-start(f32[2,512,768]{2,1,0:T(8,128)} %get-tuple-element.255), channel_id=1, source_target_pairs={{0,8},{8,0},{1,9},{9,1},{2,10},{10,2},{3,11},{11,3},{4,12},{12,4},... | collective-permute-start | bytes 9437192 | tf_op jit(solution)/shard_map/ppermute | solution.py:681
  158.1 228.9 %collective-permute-start.1 = (f32[2,512,768]{2,1,0:T(8,128)}, f32[2,512,768]{2,1,0:T(8,128)}, u32[]{:S(2)}, u32[]{:S(2)}) collective-permute-start(f32[2,512,768]{2,1,0:T(8,128)} %get-tuple-element.256), channel_id=1, source_target_pairs={{0,8},{8,0},{1,9},{9,1},{2,10},{10,2},{3,11},{11,3},{4,12},{12,4},... | collective-permute-start | bytes 9437192 | tf_op jit(solution)/shard_map/ppermute | solution.py:681
  784.7 248.3 %reduce-scatter.5.cloned.1.call-start = ((), (), s32[]{:S(2)}) async-start(), calls=%async_computation.6 | async-start | bytes 31850496 | tf_op jit(solution)/shard_map/reduce_scatter | solution.py:643
  784.7 97.8 %copy-start.4 = (s32[16,512]{1,0:T(8,128)S(1)}, s32[16,512]{1,0:T(8,128)}, u32[]{:S(2)}) copy-start(s32[16,512]{1,0:T(8,128)} %copy-done.3) | copy-start | bytes 98308
  784.8 97.8 %copy-start.6 = (pred[16,512]{1,0:T(8,128)(4,1)S(1)}, pred[16,512]{1,0:T(8,128)(4,1)}, u32[]{:S(2)}) copy-start(pred[16,512]{1,0:T(8,128)(4,1)} %copy-done.5) | copy-start | bytes 24580
  785.3 890.1 %all-gather.9.cloned.1.call-start = ((), (), s32[]{:S(2)}) async-start(), calls=%async_computation.5 | async-start | bytes 5750784 | tf_op jit(solution)/shard_map/all_gather | solution.py:646
  860.8 16.0 collective-permute-start.12
  879.0 805.8 %all-gather.11.cloned.1.call-start = ((), (), s32[]{:S(2)}) async-start(), calls=%async_computation.7 | async-start | bytes 15925248 | tf_op jit(solution)/shard_map/all_gather | solution.py:646
  879.1 273.6 %collective-permute-start.9 = (f32[4,512,768]{2,1,0:T(8,128)}, f32[4,512,768]{2,1,0:T(8,128)}, u32[]{:S(2)}, u32[]{:S(2)}) collective-permute-start(f32[4,512,768]{2,1,0:T(8,128)} %get-tuple-element.208), channel_id=1, source_target_pairs={{0,8},{8,0},{1,9},{9,1},{2,10},{10,2},{3,11},{11,3},{4,12},{12,4},... | collective-permute-start | bytes 18874376 | tf_op jit(solution)/shard_map/ppermute | solution.py:681
  880.5 204.6 %collective-permute-start.11 = (f32[2,512,768]{2,1,0:T(8,128)}, f32[2,512,768]{2,1,0:T(8,128)S(1)}, u32[]{:S(2)}, u32[]{:S(2)}) collective-permute-start(f32[2,512,768]{2,1,0:T(8,128)} %get-tuple-element.210), channel_id=1, source_target_pairs={{0,8},{8,0},{1,9},{9,1},{2,10},{10,2},{3,11},{11,3},{4,12},{12,4},... | collective-permute-start | bytes 9437192 | tf_op jit(solution)/shard_map/ppermute | solution.py:681
  881.1 271.5 %collective-permute-start.10 = (f32[2,512,768]{2,1,0:T(8,128)}, f32[2,512,768]{2,1,0:T(8,128)}, u32[]{:S(2)}, u32[]{:S(2)}) collective-permute-start(f32[2,512,768]{2,1,0:T(8,128)} %get-tuple-element.209), channel_id=1, source_target_pairs={{0,8},{8,0},{1,9},{9,1},{2,10},{10,2},{3,11},{11,3},{4,12},{12,4},... | collective-permute-start | bytes 9437192 | tf_op jit(solution)/shard_map/ppermute | solution.py:681
  1035.8 184.1 %collective-permute-start.13 = (f32[96,4608]{1,0:T(8,128)}, f32[96,4608]{1,0:T(8,128)}, u32[]{:S(2)}, u32[]{:S(2)}) collective-permute-start(f32[96,4608]{1,0:T(8,128)} %slice.162), channel_id=1, source_target_pairs={{0,8},{8,0},{1,9},{9,1},{2,10},{10,2},{3,11},{11,3},{4,12},{12,4},... | collective-permute-start | bytes 5308424 | tf_op jit(solution)/shard_map/ppermute | solution.py:645
  1161.8 58.1 %copy-start = (f32[96,9216]{1,0:T(8,128)S(1)}, f32[96,9216]{1,0:T(8,128)}, u32[]{:S(2)}) copy-start(f32[96,9216]{1,0:T(8,128)} %reduce-scatter.5.cloned.1.call-done) | copy-start | bytes 10616836
  (5 other events, 10.0 us)
Sparse Core Ops, SparseCore 0:
  27.0 36.2 all-gather.4
  70.9 75.6 all-gather.6
  784.8 74.8 reduce-scatter.2
  863.2 169.7 reduce-scatter.4
  1035.3 36.6 all-gather.8
  1222.9 103.3 all-gather.10
